TPU v7x, 512 devices: a whole 4x4x16 slice. The times are simulated.
512 devices in a mesh: seq: 32 (over y, x, core), hid: 16 (over z).
Axes of the slice: x: 4, y: 4, z: 16, core: 2. Of those that a mesh axis runs over, the one named last changes fastest.
Arguments:
- skip_stream: bfloat16 [4096, 4096], P('seq', 'hid'), may hold values from -6 to 6
- acceptance_signal: bfloat16 [4096, 4096], P('seq', 'hid'), may hold values from -6 to 6
- attention_lookups: bfloat16 [4096, 4096], P('seq', 'hid'), may hold values from -6 to 6
- attention_payloads: bfloat16 [4096, 4096], P('seq', 'hid'), may hold values from -6 to 6
- output_gating: bfloat16 [4096, 4096], P('seq', 'hid'), may hold values from -6 to 6
- forgetting_logit: float32 [4096, 4096], P('seq', 'hid'), may hold values from -16 to 0
- present_boost: float32 [64, 64], P('hid'), may hold values from -4 to 4
- groupwise_scaling: float32 [4096], P('hid'), may hold values from 0.1 to 1.9
- groupwise_offset: float32 [4096], P('hid'), may hold values from -3 to 3
- normalizer_scaling: float32 [4096], P('hid'), may hold values from 0.1 to 1.9
- normalizer_offset: float32 [4096], P('hid'), may hold values from -3 to 3
- lagged_blend_factor: float32 [4096], P('hid'), may hold values from 0.1 to 0.9
- feedforward_query_matrix: bfloat16 [4096, 7168], P('seq', 'hid'), may hold values from -0.09375 to 0.09375
- feedforward_output_matrix: bfloat16 [4096, 7168], P('seq', 'hid'), may hold values from -0.125 to 0.125
Outputs:
- block_out: bfloat16 [4096, 4096], P('seq', 'hid')
All inputs are finite; a program needn't handle non-finite values.
Results may differ from a plain program's by a relative error of at most 0.019.
Values may be sent and summed in bfloat16 or wider, within the bound.
No kernel may reach another device: no remote copies, remote signals or barrier semaphores. Data moves between devices by JAX's collectives and lax.ppermute only.
A program may use at most 64 MiB of HBM per device.

v0:
```python
import jax
import jax.numpy as jnp
from jax import lax
from jax.sharding import Mesh
from jax.sharding import PartitionSpec as P

SEQ = ("seq_0", "seq_1", "seq_2")


EPS_GROUP = 0.00064
EPS_LAYER = 1e-05


def filled_with(x, identity):
    return jax.tree.map(
        lambda a, e: jnp.broadcast_to(jnp.asarray(e, a.dtype), a.shape), x, identity
    )


def gathered_once(x, axis):
    leaves = jax.tree.leaves(x)
    order = sorted(range(len(leaves)), key=lambda k: -leaves[k].size)
    width = (1, *leaves[order[0]].shape)[-1]
    lines = [
        jnp.pad(leaves[k].reshape(-1), (0, -leaves[k].size % width)).reshape(-1, width)
        for k in order
    ]
    both, at, found = (lax.all_gather(jnp.concatenate(lines), axis), 0, {})
    for k, line in zip(order, lines):
        piece = both[:, at : at + len(line)].reshape(len(both), -1)
        found[k] = piece[:, : leaves[k].size].reshape(-1, *leaves[k].shape)
        at += len(line)
    numbers = iter(range(len(leaves)))
    return jax.tree.map(lambda _: found[next(numbers)], x)


def carried_in(x, axes, combine, identity):
    before = start = filled_with(x, identity)
    total = x
    for axis in reversed(axes):
        devices, position = (lax.axis_size(axis), lax.axis_index(axis))
        pieces = gathered_once(
            jax.tree.map(lambda part, kind: part.astype(kind), total, (jnp.bfloat16, jnp.bfloat16)),
            axis,
        )
        inside, total = (start, start)
        for k in range(devices):
            passed = k < position
            total = combine(
                total, jax.tree.map(lambda part, own: part[k].astype(own.dtype), pieces, x)
            )
            inside = jax.tree.map(lambda new, old: jnp.where(passed, new, old), total, inside)
        before = combine(inside, before)
    return before


def sent_to_all(x, axis):
    copies = jnp.broadcast_to(x, (lax.axis_size(axis), *x.shape))
    return lax.all_to_all(copies, axis, split_axis=0, concat_axis=0, tiled=True)


def taken_together(x, axis):
    return sent_to_all(x, axis).sum(axis=0)


def shifted(block, axis, distance):
    devices = range(lax.axis_size(axis))
    route = [(i - distance, i) for i in devices if i - distance in devices]
    return lax.ppermute(block, axis, route)


def laid_out(tiles, dim):
    lengths = list(tiles.shape[1:])
    lengths[dim] *= tiles.shape[0]
    return jnp.moveaxis(tiles, 0, dim).reshape(lengths)


def collect(x, axis, dim):
    tiles = sent_to_all(x, axis)
    return laid_out(tiles, dim)


def sent_together(arrays, axis, dim, along):
    both = jnp.concatenate(arrays, axis=along)
    filled, at, outs = (lax.all_gather(both, axis, axis=dim, tiled=True), 0, [])
    for a in arrays:
        outs.append(lax.slice_in_dim(filled, at, at + a.shape[along], axis=along))
        at += a.shape[along]
    return tuple(outs)


def split_up(x, dim, devices):
    lengths = x.shape
    tiles = x.reshape(*lengths[:dim], devices, lengths[dim] // devices, *lengths[dim + 1 :])
    return jnp.moveaxis(tiles, dim, 0)


def sum_at_owner(x, axis, dim):
    devices = lax.axis_size(axis)
    tiles = lax.all_to_all(split_up(x, dim, devices), axis, 0, 0, tiled=True)
    return jnp.sum(tiles.astype(jnp.float32), axis=0)


def lookup_payload_outer(
    memory_matrix, acceptance_product, key, payload_entries, forgetting_exponent, present_boost
):
    span = acceptance_product.shape[0]
    inclusive_prefix = jnp.cumsum(forgetting_exponent, axis=0)
    exclusive_prefix = inclusive_prefix - forgetting_exponent
    differ = exclusive_prefix[:, None] - inclusive_prefix[None, :]
    later = jnp.arange(span)[:, None] > jnp.arange(span)[None, :]
    factor = jnp.where(later[:, :, None, None], jnp.exp(jnp.minimum(differ, 0.0)), 0.0)
    scores = jnp.einsum("thk,tshk,shk->tsh", acceptance_product, factor, key)
    inside_segment = jnp.sum(acceptance_product * present_boost[None] * key, axis=-1)
    block_result = (
        jnp.einsum("tsh,shv->thv", scores, payload_entries)
        + inside_segment[..., None] * payload_entries
    )
    block_result = block_result + jnp.einsum(
        "jsn,snm->jsm", acceptance_product * jnp.exp(exclusive_prefix), memory_matrix
    )
    trailing_rows = jnp.exp(inclusive_prefix[-1][None] - inclusive_prefix)
    memory_matrix = jnp.exp(inclusive_prefix[-1])[..., None] * memory_matrix + jnp.einsum(
        "gte,gtc->tec", key * trailing_rows, payload_entries
    )
    return (memory_matrix, block_result)


def join_carry(earlier, later):
    return (jnp.exp(later[1])[..., None] * earlier[0] + later[0], earlier[1] + later[1])


def local(
    skip_stream,
    acceptance_signal,
    attention_lookups,
    attention_payloads,
    output_gating,
    forgetting_logit,
    present_boost,
    groupwise_scaling,
    groupwise_offset,
    normalizer_scaling,
    normalizer_offset,
    lagged_blend_factor,
    feedforward_query_matrix,
    feedforward_output_matrix,
):
    rows, width = skip_stream.shape
    subspace_slices, subspace_ordinal = present_boost.shape
    span = min(64, rows)
    count = rows // span

    def split(a):
        return a.astype(jnp.float32).reshape(count, span, subspace_slices, subspace_ordinal)

    forgetting_exponent = -jnp.exp(forgetting_logit)
    blocks = (
        split(acceptance_signal),
        split(attention_lookups),
        split(attention_payloads),
        forgetting_exponent.reshape(count, span, subspace_slices, subspace_ordinal),
    )

    def step(memory_matrix, segment_ordinal):
        return lookup_payload_outer(
            memory_matrix,
            segment_ordinal[0],
            segment_ordinal[1],
            segment_ordinal[2],
            segment_ordinal[3],
            present_boost,
        )

    zero_state = jnp.zeros((subspace_slices, subspace_ordinal, subspace_ordinal), jnp.float32)
    local_state, pieces = lax.scan(step, zero_state, blocks)
    wkv = pieces.reshape(rows, subspace_slices, subspace_ordinal)
    logw_rows = forgetting_exponent.reshape(rows, subspace_slices, subspace_ordinal)
    total = jnp.sum(logw_rows, axis=0)
    preceding_rows = jnp.cumsum(logw_rows, axis=0) - logw_rows
    incoming_state, unused_total = carried_in(
        (local_state, total), SEQ, join_carry, (zero_state, jnp.zeros_like(total))
    )
    receptance_rows = acceptance_signal.astype(jnp.float32).reshape(
        rows, subspace_slices, subspace_ordinal
    )
    wkv = wkv + jnp.einsum(
        "jsn,snm->jsm", receptance_rows * jnp.exp(preceding_rows), incoming_state
    )
    centre = wkv - jnp.mean(wkv, axis=-1, keepdims=True)
    spread = jnp.mean(centre * centre, axis=-1, keepdims=True)
    normed = (centre * lax.rsqrt(spread + EPS_GROUP)).reshape(rows, width)
    normed = normed * groupwise_scaling + groupwise_offset
    middle = skip_stream.astype(jnp.float32) + normed * jax.nn.silu(
        output_gating.astype(jnp.float32)
    )
    first, second = (
        taken_together(jnp.sum(middle, axis=1, keepdims=True), "hid"),
        taken_together(jnp.sum(middle * middle, axis=1, keepdims=True), "hid"),
    )
    full_width = width * lax.axis_size("hid")
    mean_row = first / full_width
    var_row = second / full_width - mean_row * mean_row
    xn = (
        (middle - mean_row) * lax.rsqrt(var_row + EPS_LAYER) * normalizer_scaling
        + normalizer_offset
    ).astype(jnp.bfloat16)
    carried_row = shifted(xn[rows - 1 :], SEQ, 1)
    prev = jnp.concatenate([carried_row, xn[: rows - 1]], axis=0)
    xn_wide = xn.astype(jnp.float32)
    xk = (xn_wide + (prev.astype(jnp.float32) - xn_wide) * lagged_blend_factor).astype(jnp.bfloat16)
    whole = collect(xk, "hid", 1)
    key_all, value_all = sent_together(
        (feedforward_query_matrix, feedforward_output_matrix), SEQ, 0, 1
    )
    pre = jnp.dot(whole, key_all, preferred_element_type=jnp.float32)
    hidden = jnp.square(jnp.maximum(pre, 0.0)).astype(jnp.bfloat16)
    down = lax.dot_general(
        hidden, value_all, (((1,), (1,)), ((), ())), preferred_element_type=jnp.float32
    )
    mixed = sum_at_owner(down.astype(jnp.bfloat16), "hid", 1)
    return (middle + mixed).astype(jnp.bfloat16)


def solution(mesh):
    finer = Mesh(
        mesh.devices.reshape(4, 4, 2, mesh.shape["hid"]), ("seq_0", "seq_1", "seq_2", "hid")
    )
    in_specs = (
        P(SEQ, "hid"),
        P(SEQ, "hid"),
        P(SEQ, "hid"),
        P(SEQ, "hid"),
        P(SEQ, "hid"),
        P(SEQ, "hid"),
        P("hid", None),
        P("hid"),
        P("hid"),
        P("hid"),
        P("hid"),
        P("hid"),
        P(SEQ, "hid"),
        P(SEQ, "hid"),
    )
    out_specs = P(SEQ, "hid")
    return jax.shard_map(local, mesh=finer, in_specs=in_specs, out_specs=out_specs, check_vma=False)
```

profile of v0, /device:TPU:6, one launch (start us, length us, event | category | flops | bytes accessed | tf_op | source)
XLA Modules:
  0.0 247.7 jit_solution(14247085353347959316)
XLA Ops:
  6.5 1.7 pad_maximum_fusion
  8.3 1.0 copy.95
  9.4 1.0 copy.94
  10.8 1.0 reshape.364
  11.8 1.0 reshape.366
  12.8 27.1 %while.13 = (s32[]{:T(128)}, f32[4,64,64]{2,1,0:T(8,128)S(1)}, f32[2,64,4,64]{1,0,3,2:T(2,128)S(1)}, f32[2,64,4,64]{1,0,3,2:T(2,128)S(1)}, f32[2,64,4,64]{3,2,1,...) while((s32[]{:T(128)}, f32[4,64,64]{2,1,0:T(8,128)S(1)}, ...), condition=%wide.region_3.4_spmd.clone, body=%wide.region_0.3_spmd.clone.sunk | while | flops 14929667 | bytes 6769792 | solution.py:176
  12.8 0.3 constant_dynamic-slice_fusion.5
  13.2 0.8 fusion.95
  14.3 6.2 %multiply_bitcast_fusion.3 = bf16[64,4,64,64]{2,1,0,3:T(4,128)(2,1)S(1)} fusion(f32[64,4,64]{2,1,0:T(4,128)S(1)} %get-tuple-element.221, f32[64,4,64]{2,1,0:T(4,128)S(1)} %fusion.94, f32[64,4,64]{2,1,0:T(4,128)S(1)} %get-tuple-element.224, pred[64,64]{1,0:T(8,128)(4,1)S(1)} %iota_compare_fusion.2), kind=kLoop, calls=%fused_computation.2.clone.1 | loop fusion | flops 5242880 | bytes 2297856 | tf_op jit(solution)/shard_map/while/body/eval_jaxpr/thk,tshk,shk->tsh/dot_general | solution.py:113
  20.5 2.3 fusion.97
  23.3 2.8 %dynamic_update_slice.6 = f32[2,64,4,64]{1,0,3,2:T(2,128)S(1)} dynamic-update-slice(f32[2,64,4,64]{1,0,3,2:T(2,128)S(1)} %get-tuple-element.238, f32[1,64,4,64]{1,0,3,2:T(1,128)S(1)} %copy.196, s32[]{:T(128)} %get-tuple-element.236, s32[]{:T(128)} %constant.30.clone.1..sunk, s32[]{:T(128)} %constant.30.clone.1..sunk, s32[]{:T(128)} %constant.30.clone.1..sunk) | dynamic-update-slice | bytes 131076 | tf_op jit(solution)/shard_map/while/body/jit(dynamic_update_index_in_dim)/dynamic_update_slice | solution.py:176
  26.1 0.2 convolution_add_fusion.2
  26.3 0.3 constant_dynamic-slice_fusion.5
  26.7 0.8 fusion.95
  27.9 6.2 %multiply_bitcast_fusion.3 = bf16[64,4,64,64]{2,1,0,3:T(4,128)(2,1)S(1)} fusion(f32[64,4,64]{2,1,0:T(4,128)S(1)} %get-tuple-element.221, f32[64,4,64]{2,1,0:T(4,128)S(1)} %fusion.94, f32[64,4,64]{2,1,0:T(4,128)S(1)} %get-tuple-element.224, pred[64,64]{1,0:T(8,128)(4,1)S(1)} %iota_compare_fusion.2), kind=kLoop, calls=%fused_computation.2.clone.1 | loop fusion | flops 5242880 | bytes 2297856 | tf_op jit(solution)/shard_map/while/body/eval_jaxpr/thk,tshk,shk->tsh/dot_general | solution.py:113
  34.1 2.3 fusion.97
  36.9 2.8 %dynamic_update_slice.6 = f32[2,64,4,64]{1,0,3,2:T(2,128)S(1)} dynamic-update-slice(f32[2,64,4,64]{1,0,3,2:T(2,128)S(1)} %get-tuple-element.238, f32[1,64,4,64]{1,0,3,2:T(1,128)S(1)} %copy.196, s32[]{:T(128)} %get-tuple-element.236, s32[]{:T(128)} %constant.30.clone.1..sunk, s32[]{:T(128)} %constant.30.clone.1..sunk, s32[]{:T(128)} %constant.30.clone.1..sunk) | dynamic-update-slice | bytes 131076 | tf_op jit(solution)/shard_map/while/body/jit(dynamic_update_index_in_dim)/dynamic_update_slice | solution.py:176
  39.7 0.2 convolution_add_fusion.2
  40.3 1.9 all-gather.3
  42.6 14.7 %all-gather.4 = bf16[4,260,64]{1,2,0:T(8,128)(2,1)S(1)} all-gather(bf16[1,260,64]{1,2,0:T(8,128)(2,1)S(1)} %maximum_bitcast_fusion.1), channel_id=3, replica_groups=mesh['seq_0'=4,'seq_1'=4,'seq_2'=2,'hid'=16] {'seq_1'}, dimensions={0}, use_global_device_ids=true | all-gather | bytes 166400 | tf_op jit(solution)/shard_map/all_gather | solution.py:28
  58.1 12.8 %all-gather.5 = bf16[4,260,64]{1,2,0:T(8,128)(2,1)S(1)} all-gather(bf16[1,260,64]{1,2,0:T(8,128)(2,1)S(1)} %maximum_bitcast_fusion.2), channel_id=4, replica_groups=mesh['seq_0'=4,'seq_1'=4,'seq_2'=2,'hid'=16] {'seq_0'}, dimensions={0}, use_global_device_ids=true | all-gather | bytes 166400 | tf_op jit(solution)/shard_map/all_gather | solution.py:28
  73.8 0.3 add_add_fusion
  74.7 25.5 %all_to_all.20 = f32[16,128,1]{1,2,0:T(1,128)S(1)} all-to-all(f32[16,128,1]{1,2,0:T(1,128)S(1)} %broadcast_in_dim.37), channel_id=1, replica_groups=mesh['seq_0'=4,'seq_1'=4,'seq_2'=2,'hid'=16] {'hid'}, dimensions={0} | all-to-all | bytes 16384 | tf_op jit(solution)/shard_map/all_to_all | solution.py:59
  100.2 0.6 broadcast_in_dim.38
  100.8 3.5 %all-to-all-start.1 = ((f32[16,128,1]{1,2,0:T(1,128)}), f32[16,128,1]{1,2,0:T(1,128)S(1)}, u32[]{:S(2)}, u32[]{:S(2)}) async-start(f32[16,128,1]{1,2,0:T(1,128)} %broadcast_in_dim.38), calls=%async_computation.1 | async-start | bytes 16384 | tf_op jit(solution)/shard_map/all_to_all | solution.py:59
  104.3 12.3 %all-to-all-done.1 = f32[16,128,1]{1,2,0:T(1,128)S(1)} async-done(((f32[16,128,1]{1,2,0:T(1,128)}), f32[16,128,1]{1,2,0:T(1,128)S(1)}, u32[]{:S(2)}, u32[]{:S(2)}) %all-to-all-start.1) | async-done | bytes 8224 | tf_op jit(solution)/shard_map/all_to_all | solution.py:59
  116.8 1.9 collective-permute-start
  118.7 3.0 %collective-permute-done = bf16[1,256]{1,0:T(2,128)(2,1)S(1)} collective-permute-done((bf16[1,256]{1,0:T(2,128)(2,1)S(1)}, bf16[1,256]{1,0:T(2,128)(2,1)S(1)}, u32[]{:S(2)}, u32[]{:S(2)}) %collective-permute-start) | collective-permute-done | bytes 544 | tf_op jit(solution)/shard_map/ppermute | solution.py:69
  122.2 54.1 %all_to_all.21 = bf16[16,128,256]{1,2,0:T(8,128)(2,1)S(1)} all-to-all(bf16[16,128,256]{1,2,0:T(8,128)(2,1)S(1)} %broadcast_in_dim.39), channel_id=1, replica_groups=mesh['seq_0'=4,'seq_1'=4,'seq_2'=2,'hid'=16] {'hid'}, dimensions={0} | all-to-all | bytes 2097152 | tf_op jit(solution)/shard_map/all_to_all | solution.py:59
  176.3 6.0 %convolution_convert_fusion = bf16[128,4096]{1,0:T(8,128)(2,1)S(1)} fusion(bf16[4096,896]{0,1:T(8,128)(2,1)} %all-gather.8.cloned.1.call-done, bf16[128,4096]{0,1:T(8,128)(2,1)S(1)} %bitcast.195), kind=kOutput, calls=%fused_computation.33 | convolution fusion | flops 940220416 | bytes 9437184 | tf_op jit(solution)/shard_map/dot_general | solution.py:218
  182.4 57.7 %all_to_all.22 = bf16[16,128,256]{2,1,0:T(8,128)(2,1)S(1)} all-to-all(bf16[16,128,256]{2,1,0:T(8,128)(2,1)S(1)} %bitcast.193), channel_id=1, replica_groups=mesh['seq_0'=4,'seq_1'=4,'seq_2'=2,'hid'=16] {'hid'}, dimensions={0} | all-to-all | bytes 2097152 | tf_op jit(solution)/shard_map/all_to_all | solution.py:100
  240.2 0.6 add_convert_fusion
  (120 shorter events, 8.0 us)
Async XLA Ops:
  6.5 169.7 %all-gather.8.cloned.1.call-start = ((), (), s32[]{:S(2)}) async-start(), calls=%async_computation.4 | async-start | bytes 7569408 | tf_op jit(solution)/shard_map/all_gather | solution.py:85
  39.9 34.6 %copy-start = (bf16[128,256]{1,0:T(8,128)(2,1)S(1)}, bf16[128,256]{1,0:T(8,128)(2,1)}, u32[]{:S(2)}) copy-start(bf16[128,256]{1,0:T(8,128)(2,1)} %param.20) | copy-start | bytes 196612
  39.9 34.6 %copy-start.1 = (bf16[128,256]{1,0:T(8,128)(2,1)S(1)}, bf16[128,256]{1,0:T(8,128)(2,1)}, u32[]{:S(2)}) copy-start(bf16[128,256]{1,0:T(8,128)(2,1)} %param.16) | copy-start | bytes 196612
  39.9 34.6 %copy-start.4 = (f32[256]{0:T(256)S(1)}, f32[256]{0:T(256)}, u32[]{:S(2)}) copy-start(f32[256]{0:T(256)} %param.24) | copy-start | bytes 3076
  39.9 34.6 %copy-start.5 = (f32[256]{0:T(256)S(1)}, f32[256]{0:T(256)}, u32[]{:S(2)}) copy-start(f32[256]{0:T(256)} %param.23) | copy-start | bytes 3076
  39.9 76.7 %copy-start.2 = (f32[256]{0:T(256)S(1)}, f32[256]{0:T(256)}, u32[]{:S(2)}) copy-start(f32[256]{0:T(256)} %param.26) | copy-start | bytes 3076
  40.0 76.7 %copy-start.3 = (f32[256]{0:T(256)S(1)}, f32[256]{0:T(256)}, u32[]{:S(2)}) copy-start(f32[256]{0:T(256)} %param.25) | copy-start | bytes 3076
  40.0 81.7 %copy-start.6 = (f32[256]{0:T(256)S(1)}, f32[256]{0:T(256)}, u32[]{:S(2)}) copy-start(f32[256]{0:T(256)} %param.27) | copy-start | bytes 3076
  100.8 15.8 %all-to-all-start.1 = ((f32[16,128,1]{1,2,0:T(1,128)}), f32[16,128,1]{1,2,0:T(1,128)S(1)}, u32[]{:S(2)}, u32[]{:S(2)}) async-start(f32[16,128,1]{1,2,0:T(1,128)} %broadcast_in_dim.38), calls=%async_computation.1 | async-start | bytes 16384 | tf_op jit(solution)/shard_map/all_to_all | solution.py:59
  116.8 4.9 %collective-permute-start = (bf16[1,256]{1,0:T(2,128)(2,1)S(1)}, bf16[1,256]{1,0:T(2,128)(2,1)S(1)}, u32[]{:S(2)}, u32[]{:S(2)}) collective-permute-start(bf16[1,256]{1,0:T(2,128)(2,1)S(1)} %slice.159), channel_id=1, source_target_pairs={{0,16},{16,32},{32,48},{48,64},{64,80},{80,96},{96,112},{112,128},... | collective-permute-start | bytes 1544 | tf_op jit(solution)/shard_map/ppermute | solution.py:69
Sparse Core Ops, SparseCore 0:
  10.4 76.0 all-gather.7
where the time goes:
time: 248 us
  blocking collectives  167 us (67%)
  other arithmetic  18.4 us (7%)
  local copies, waits for them, and re-layouts  16 us (6%)
  waiting for transfers between devices  15.3 us (6%)
  between operations  13.9 us (6%)
  matrix products  11.8 us (5%)
  starting transfers between devices  5.39 us (2%)
    all_to_all x2, blocking collectives, sent_to_all(): return lax.all_to_all(copies, axis, split_axis=0, concat_axis=0, tiled=True)  79.7 us
    all_to_all x1, blocking collectives, sum_at_owner(): tiles = lax.all_to_all(split_up(x, dim, devices), axis, 0, 0, tiled=True)  57.7 us
    all_gather x3, blocking collectives, gathered_once(): both, at, found = (lax.all_gather(jnp.concatenate(lines), axis), 0, {})  29.4 us
    dot_general x2, other arithmetic, lookup_payload_outer(): scores = jnp.einsum('thk,tshk,shk->tsh', acceptance_product, factor, key)  12.4 us
    all_to_all x1, waiting for transfers between devices, sent_to_all(): return lax.all_to_all(copies, axis, split_axis=0, concat_axis=0, tiled=True)  12.3 us
    dot_general x1, matrix products, local(): lax.dot_general(hidden, value_all, (((1,), (1,)), ((), ())), preferred_el...  5.98 us
    dynamic_update_slice x4, local copies, waits for them, and re-layouts, local(): local_state, pieces = lax.scan(step, zero_state, blocks)  5.7 us
  transfers between devices with their start and end apart: 3, of which 2 were waited for; matrix products, arithmetic and copies ran while one was open for 15% of the time, Pallas kernels for 0%

commit v1 on v0

v1 whole, which is shorter than its diff:
```python
import functools

import jax
import jax.numpy as jnp
from jax import lax
from jax.experimental import pallas as pl
from jax.experimental.pallas import tpu as pltpu
from jax.sharding import Mesh
from jax.sharding import PartitionSpec as P

SEQ = ("y", "x", "c")
HID = ("zl", "zh")
EPS_GROUP = 0.00064
EPS_LAYER = 1e-05
F32 = jnp.float32
BF16 = jnp.bfloat16
NN = (((1,), (0,)), ((), ()))
NT = (((1,), (1,)), ((), ()))
TN = (((0,), (0,)), ((), ()))


def dot(a, b, dims):
    return lax.dot_general(a, b, dims, preferred_element_type=F32)


def iota(shape, dim):
    return lax.broadcasted_iota(jnp.int32, shape, dim)


def hi_lo(x):
    hi = x.astype(BF16)
    return hi, (x - hi.astype(F32)).astype(BF16)


def wkv_kernel(r_ref, k_ref, v_ref, logit_ref, boost_ref, own_ref, rec_ref, pay_ref):
    rows, width = r_ref.shape
    logw = -jnp.exp(logit_ref[...])
    lower = (iota((rows, rows), 0) >= iota((rows, rows), 1)).astype(BF16)
    part0, rest = logw.astype(BF16), logw
    rest = rest - part0.astype(F32)
    part1, part2 = hi_lo(rest)
    incl = dot(lower, part0, NN) + dot(lower, part1, NN) + dot(lower, part2, NN)
    excl = incl - logw
    total = incl[rows - 1 : rows]
    half = rows // 2
    edge = incl[half - 1 : half]
    top = iota((rows, width), 0) < half
    ref = jnp.where(top, incl[half // 2 - 1 : half // 2], incl[half + half // 2 - 1 : half + half // 2])
    r = r_ref[...].astype(F32)
    k = k_ref[...].astype(F32)
    v = v_ref[...]
    r_in = (r * jnp.exp(excl - ref)).astype(BF16)
    k_in = (k * jnp.exp(ref - incl)).astype(BF16)
    r_off = (r * jnp.exp(jnp.minimum(excl - edge, 0.0))).astype(BF16)
    k_off = (k * jnp.exp(jnp.minimum(edge - incl, 0.0))).astype(BF16)
    rec_ref[...] = (r * jnp.exp(excl)).astype(BF16)
    k_end = (k * jnp.exp(total - incl)).astype(BF16)
    now = r * boost_ref[...] * k
    row, col = iota((rows, rows), 0), iota((rows, rows), 1)
    same = (row > col) & ((row < half) == (col < half))
    cross = (row >= half) & (col < half)
    left = iota((rows, 128), 1) < 64
    zero = jnp.zeros((), BF16)
    for p in range(width // 128):
        at = slice(128 * p, 128 * p + 128)
        scores, values, sums = [], [], []
        for mask in (left, ~left):
            inner = dot(r_in[:, at], jnp.where(mask, k_in[:, at], zero), NT)
            outer = dot(r_off[:, at], jnp.where(mask, k_off[:, at], zero), NT)
            scores.append(jnp.where(same, inner, jnp.where(cross, outer, 0.0)).astype(BF16))
            values.append(jnp.where(mask, v[:, at], zero))
            sums.append(jnp.sum(jnp.where(mask, now[:, at], 0.0), axis=1, keepdims=True))
        out = dot(jnp.concatenate(scores, axis=1), jnp.concatenate(values, axis=0), NN)
        own_ref[:, at] = out + jnp.where(left, sums[0], sums[1]) * v[:, at].astype(F32)
        state = dot(v[:, at], k_end[:, at], TN)
        pay_ref[0:64, at] = jnp.where(left[0:64], state[0:64], state[64:128]).astype(BF16)
    hi, lo = hi_lo(total)
    line = iota((8, width), 0)
    pay_ref[64:72, :] = jnp.where(
        line == 0, hi.astype(F32), jnp.where(line == 1, lo.astype(F32), 0.0)
    ).astype(BF16)


def middle_kernel(
    at_ref, all_ref, own_ref, rec_ref, skip_ref, gate_ref, gn_ref, ln_ref, mid_ref, pay_ref
):
    rows, width = own_ref.shape

    def join(i, state):
        piece = all_ref[i].astype(F32)
        return state * jnp.exp(piece[64:65] + piece[65:66]) + piece[0:64]

    state = lax.fori_loop(0, at_ref[0], join, jnp.zeros((64, width), F32))
    left64 = iota((64, 128), 1) < 64
    left = iota((rows, 128), 1) < 64

    def mean(x):
        a = jnp.sum(jnp.where(left, x, 0.0), axis=1, keepdims=True)
        b = jnp.sum(jnp.where(left, 0.0, x), axis=1, keepdims=True)
        return jnp.where(left, a, b) * (1.0 / 64)

    for p in range(width // 128):
        at = slice(128 * p, 128 * p + 128)
        here = state[:, at]
        both = jnp.concatenate(
            [jnp.where(left64, here, 0.0), jnp.where(left64, 0.0, here)], axis=0
        ).astype(BF16)
        wkv = own_ref[:, at] + dot(rec_ref[:, at], both, NT)
        centre = wkv - mean(wkv)
        normed = centre * lax.rsqrt(mean(centre * centre) + EPS_GROUP)
        normed = normed * gn_ref[0:1, at] + gn_ref[1:2, at]
        gate = gate_ref[:, at].astype(F32)
        middle = skip_ref[:, at].astype(F32) + normed * (gate / (1.0 + jnp.exp(-gate)))
        mid_ref[:, at] = middle
        half = rows // 2
        for h in range(2):
            pay_ref[h, 0:half, at] = middle[h * half : h * half + half].astype(BF16)
    half = rows // 2
    line = iota((8, width), 0)
    tail = jnp.zeros((8, width), F32)
    for n in range(3):
        hi, lo = hi_lo(ln_ref[n : n + 1])
        tail = jnp.where(line == 2 * n, hi.astype(F32), tail)
        tail = jnp.where(line == 2 * n + 1, lo.astype(F32), tail)
    for h in range(2):
        pay_ref[h, half : half + 8, :] = tail.astype(BF16)


def norm_kernel(at_ref, all_ref, prev_ref, out_ref):
    groups, _, lines, width = all_ref.shape
    rows = lines - 8
    zh = at_ref[0]
    full = 2 * groups * width

    def stats(load, n):
        first, second = jnp.zeros((n, width), F32), jnp.zeros((n, width), F32)
        for g in range(groups):
            for i in range(2):
                x = load(g, i)
                first, second = first + x, second + x * x
        mu = jnp.sum(first, axis=1, keepdims=True) / full
        var = jnp.sum(second, axis=1, keepdims=True) / full - mu * mu
        return mu, lax.rsqrt(var + EPS_LAYER)

    mu, scale = stats(lambda g, i: all_ref[g, i, 0:rows].astype(F32), rows)
    pmu, pscale = stats(lambda g, i: prev_ref[g, i].astype(F32), 8)
    live = at_ref[1] > 0
    head = iota((rows, width), 0) == 0
    for g in range(groups):
        for i in range(2):
            mine = jnp.bitwise_xor(zh, i)
            block = all_ref[g, mine]
            x = block[0:rows].astype(F32)
            p = prev_ref[g, 1 - mine].astype(F32)
            vec = block[rows : rows + 8].astype(F32)
            gain, bias, blend = (vec[2 * n : 2 * n + 1] + vec[2 * n + 1 : 2 * n + 2] for n in range(3))
            xn = ((x - mu) * scale * gain + bias).astype(BF16).astype(F32)
            pn = ((p - pmu) * pscale * gain + bias).astype(BF16).astype(F32)
            pn = jnp.where(live, pn[0:1], 0.0)
            prev = jnp.where(head, pn, pltpu.roll(xn, 1, 0))
            at = (2 * g + i) * width
            out_ref[:, at : at + width] = (xn + (prev - xn) * blend).astype(BF16)


def ffn_kernel(own_ref, peer_ref, w_hbm, keep_ref, give_ref, w_ref, sems):
    rows, full = own_ref.shape
    blocks, depth, wide = w_hbm.shape
    units = wide // 2
    cut = units + 64
    chunks = sems.shape[0]
    step = blocks // chunks

    def copy(q):
        at = pl.ds(q * step, step)
        return pltpu.make_async_copy(w_hbm.at[at], w_ref.at[at], sems.at[q])

    for q in range(chunks):
        copy(q).start()
    acc = jnp.zeros((2 * rows, cut), F32)
    for q in range(chunks):
        copy(q).wait()
        for j in range(q * step // 2, (q + 1) * step // 2):
            at = slice(2 * depth * j, 2 * depth * (j + 1))
            x = jnp.concatenate([own_ref[:, at], peer_ref[:, at]], axis=0)
            w = w_ref[2 * j : 2 * j + 2, :, 0:cut].reshape(2 * depth, cut)
            acc = acc + dot(x, w, NN)
    hidden = jnp.square(jnp.maximum(acc, 0.0))
    hidden = jnp.where(iota(hidden.shape, 1) < units, hidden, 0.0)
    hidden = pltpu.roll(hidden, 64, 1).astype(BF16)
    for j in range(blocks // 2):
        w = w_ref[2 * j : 2 * j + 2, :, units - 64 : wide].reshape(2 * depth, cut)
        out = dot(hidden, w, NT)
        at = slice((j % 2) * 2 * depth, (j % 2 + 1) * 2 * depth)
        keep_ref[j // 2, :, at] = out[0:rows]
        give_ref[j // 2, :, at] = out[rows:].astype(BF16)


VMEM = functools.partial(pl.BlockSpec, memory_space=pltpu.VMEM)
SMEM = functools.partial(pl.BlockSpec, memory_space=pltpu.SMEM)
SWAP = [(0, 1), (1, 0)]


def make(interpret):
    def call(kernel, outs, *args, in_specs=None, **more):
        return pl.pallas_call(
            kernel,
            out_shape=[jax.ShapeDtypeStruct(s, t) for s, t in outs],
            in_specs=in_specs or [VMEM() for _ in args],
            out_specs=[VMEM() for _ in outs],
            interpret=interpret,
            **more,
        )(*args)

    def local(
        skip, recept, keys, values, gating, logit, boost, gn_gain, gn_bias, ln_gain, ln_bias, blend, wk, wv
    ):
        rows, width = skip.shape
        half = rows // 2
        groups = lax.axis_size("zl")
        blocks = lax.axis_size(SEQ)
        at_seq = lax.axis_index(SEQ)
        zh = lax.axis_index("zh")

        weights = jnp.concatenate([wk, wv], axis=1)
        weights = lax.ppermute(weights, ("c", "zh"), [(0, 0), (1, 2), (2, 1), (3, 3)])
        weights = lax.all_gather(weights, ("y", "x", "zh"))

        own, recall, state = call(
            wkv_kernel,
            [((rows, width), F32), ((rows, width), BF16), ((72, width), BF16)],
            recept, keys, values, logit, boost.reshape(1, width),
        )
        states = lax.all_to_all(
            jnp.broadcast_to(state, (blocks, *state.shape)), SEQ, 0, 0, tiled=True
        )
        middle, pay = call(
            middle_kernel,
            [((rows, width), F32), ((2, half + 8, width), BF16)],
            at_seq.reshape(1), states, own, recall, skip, gating,
            jnp.stack([gn_gain, gn_bias]), jnp.stack([ln_gain, ln_bias, blend]),
            in_specs=[SMEM()] + [VMEM()] * 7,
        )
        mine = lax.dynamic_index_in_dim(pay, zh, 0, keepdims=False)
        other = lax.dynamic_index_in_dim(pay, 1 - zh, 0, keepdims=False)
        other = lax.ppermute(other, "zh", SWAP)
        wide = lax.all_gather(jnp.stack([mine, other]), "zl")
        count = 2 * blocks
        last = lax.ppermute(
            wide[:, :, half - 1 : half, :], (*SEQ, "zh"), [(n, n + 1) for n in range(count - 1)]
        )
        last = jnp.broadcast_to(last, (groups, 2, 8, width))
        (xk,) = call(
            norm_kernel,
            [((half, 2 * groups * width), BF16)],
            jnp.stack([zh, at_seq * 2 + zh]), wide, last,
            in_specs=[SMEM(), VMEM(), VMEM()],
        )
        peer = lax.ppermute(xk, "c", SWAP)
        tall = weights.shape
        keep, give = call(
            ffn_kernel,
            [((groups, half, 2 * width), F32), ((groups, half, 2 * width), BF16)],
            xk, peer, weights,
            in_specs=[VMEM(), VMEM(), pl.BlockSpec(memory_space=pl.ANY)],
            scratch_shapes=[pltpu.VMEM(tall, BF16), pltpu.SemaphoreType.DMA((min(8, tall[0] // 2),))],
        )
        part = (keep + lax.ppermute(give, "c", SWAP).astype(F32)).astype(BF16)
        part = lax.all_to_all(part, "zl", 0, 0, tiled=True)
        down = jnp.sum(part.astype(F32), axis=0).reshape(half, 2, width)
        mine = lax.dynamic_index_in_dim(down, zh, 1, keepdims=False).astype(BF16)
        other = lax.dynamic_index_in_dim(down, 1 - zh, 1, keepdims=False).astype(BF16)
        other = lax.ppermute(other, "zh", SWAP)
        whole = jnp.where(
            zh == 0, jnp.concatenate([mine, other]), jnp.concatenate([other, mine])
        )
        return (middle + whole.astype(F32)).astype(BF16)

    return local


def build(finer, interpret=False):
    tile, vec = P(SEQ, HID), P(HID)
    return jax.shard_map(
        make(interpret),
        mesh=finer,
        in_specs=(tile,) * 6 + (P(HID, None),) + (vec,) * 5 + (tile, tile),
        out_specs=tile,
        check_vma=False,
    )


def solution(mesh):
    hid = mesh.shape["hid"]
    return build(Mesh(mesh.devices.reshape(4, 4, 2, hid // 2, 2), (*SEQ, *HID)))
```

time: 248 us -> 313 us (1.26)
  the two profiles are of different devices: /device:TPU:6 before, /device:TPU:32 now
where the time goes in v1:
time: 313 us; the launch traced here: 312 us
  waiting for transfers between devices  148 us (47%)
  blocking collectives  88.9 us (28%)
  starting transfers between devices  22.6 us (7%)
  local copies, waits for them, and re-layouts  18.3 us (6%)
  Pallas kernels  14.7 us (5%)
  between operations  13.5 us (4%)
  other arithmetic  6.24 us (2%)
    all_gather x1, waiting for transfers between devices, local(): weights = lax.all_gather(weights, ('y', 'x', 'zh'))  112 us
    all_to_all x1, blocking collectives, local(): part = lax.all_to_all(part, 'zl', 0, 0, tiled=True)  46.2 us
    all_gather x1, blocking collectives, local(): wide = lax.all_gather(jnp.stack([mine, other]), 'zl')  42.7 us
    all_to_all x1, waiting for transfers between devices, local(): lax.all_to_all(jnp.broadcast_to(state, (blocks, *state.shape)), SEQ, 0, 0...  17.3 us
    pallas_call x4, Pallas kernels, call(): pl.pallas_call(kernel, out_shape=[jax.ShapeDtypeStruct(s, t) for s, t in...  14.7 us
    all_gather x1, local copies, waits for them, and re-layouts, local(): weights = lax.all_gather(weights, ('y', 'x', 'zh'))  10.8 us
    ppermute x2, starting transfers between devices, local(): other = lax.ppermute(other, 'zh', SWAP)  7.65 us
    all_to_all x1, starting transfers between devices, local(): lax.all_to_all(jnp.broadcast_to(state, (blocks, *state.shape)), SEQ, 0, 0...  7.32 us
  transfers between devices with their start and end apart: 8, of which 7 were waited for; matrix products, arithmetic and copies ran while one was open for 6% of the time, Pallas kernels for 2%

profile of v1, /device:TPU:32, one launch (start us, length us, event | category | flops | bytes accessed | tf_op | source)
XLA Modules:
  0.0 312.1 jit_solution(8398746402398249411)
XLA Ops:
  6.5 1.0 pad_maximum_fusion
  7.5 1.9 collective-permute-start.3
  9.4 5.4 %collective-permute-done.3 = bf16[128,896]{0,1:T(8,128)(2,1)S(1)} collective-permute-done((bf16[128,896]{0,1:T(8,128)(2,1)S(1)}, bf16[128,896]{0,1:T(8,128)(2,1)S(1)}, u32[]{:S(2)}, u32[]{:S(2)}) %collective-permute-start.3) | collective-permute-done | bytes 229408 | tf_op jit(solution)/shard_map/ppermute | solution.py:225
  14.9 0.7 copy-done.3
  15.6 1.3 reshape.12.boost_ref
  16.9 2.5 shard_map.136
  19.4 2.0 broadcast_in_dim.10
  21.3 7.3 %all-to-all-start = ((bf16[32,72,256]{2,1,0:T(8,128)(2,1)}), bf16[32,72,256]{2,1,0:T(8,128)(2,1)S(1)}, u32[]{:S(2)}, u32[]{:S(2)}) async-start(bf16[32,72,256]{2,1,0:T(8,128)(2,1)} %broadcast_in_dim.10), calls=%async_computation | async-start | bytes 2359296 | tf_op jit(solution)/shard_map/all_to_all | solution.py:233
  28.7 1.3 pad_maximum_fusion.3.gn_ref
  30.0 1.3 pad_maximum_fusion.2.ln_ref
  31.3 17.3 %all-to-all-done.all_ref = bf16[32,72,256]{2,1,0:T(8,128)(2,1)S(1)} async-done(((bf16[32,72,256]{2,1,0:T(8,128)(2,1)}), bf16[32,72,256]{2,1,0:T(8,128)(2,1)S(1)}, u32[]{:S(2)}, u32[]{:S(2)}) %all-to-all-start) | async-done | bytes 1179680 | tf_op jit(solution)/shard_map/all_to_all | solution.py:233
  48.6 1.1 copy-done
  49.7 2.5 shard_map.137
  52.2 0.8 constant_dynamic-slice_fusion.2
  53.0 5.7 %collective-permute-start = (bf16[72,256]{1,0:T(8,128)(2,1)S(1)}, bf16[72,256]{1,0:T(8,128)(2,1)S(1)}, u32[]{:S(2)}, u32[]{:S(2)}) collective-permute-start(bf16[72,256]{1,0:T(8,128)(2,1)S(1)} %get-tuple-element.20), channel_id=1, source_target_pairs={{0,1},{1,0},{2,3},{3,2},{4,5},{5,4},{6,7},{7,6},{8,9},{9,8},{10,11... | collective-permute-start | bytes 110600 | tf_op jit(solution)/shard_map/ppermute | solution.py:245
  58.7 2.8 collective-permute-done
  61.6 42.7 %all-gather = bf16[16,72,256]{2,1,0:T(8,128)(2,1)S(1)} all-gather(bf16[2,72,256]{2,1,0:T(8,128)(2,1)S(1)} %pad_maximum_fusion.1), channel_id=2, replica_groups=mesh['y'=4,'x'=4,'c'=2,'zl'=8,'zh'=2] {'zl'}, dimensions={0}, use_global_device_ids=true | all-gather | bytes 663552 | tf_op jit(solution)/shard_map/all_gather | solution.py:246
  104.3 1.9 collective-permute-start.1
  106.8 4.5 %collective-permute-done.1 = bf16[8,2,1,256]{3,2,1,0:T(2,128)(2,1)S(1)} collective-permute-done((bf16[8,2,1,256]{3,2,1,0:T(2,128)(2,1)S(1)}, bf16[8,2,1,256]{3,2,1,0:T(2,128)(2,1)S(1)}, u32[]{:S(2)}, u32[]{:S(2)}) %collective-permute-start.1) | collective-permute-done | bytes 8224 | tf_op jit(solution)/shard_map/ppermute | solution.py:248
  111.9 2.5 shard_map.138.own_ref
  114.5 1.9 collective-permute-start.2
  116.4 111.7 %all-gather.4.cloned.1.call-done = bf16[4096,896]{0,1:T(8,128)(2,1)} async-done(((bf16[128,896]{0,1:T(8,128)(2,1)}), bf16[4096,896]{0,1:T(8,128)(2,1)}) %all-gather.4.cloned.1.call-update) | async-done | bytes 7340048 | tf_op jit(solution)/shard_map/all_gather | solution.py:226
  228.1 10.8 %copy.23 = bf16[4096,896]{1,0:T(8,128)(2,1)} copy(bf16[4096,896]{0,1:T(8,128)(2,1)} %all-gather.4.cloned.1.call-done) | data formatting | bytes 14680064 | tf_op jit(solution)/shard_map/all_gather | solution.py:226
  238.9 0.8 copy-done.2
  239.7 7.2 %shard_map.139 = (f32[8,64,512]{2,1,0:T(8,128)}, bf16[8,64,512]{2,1,0:T(8,128)(2,1)}) custom-call(bf16[64,4096]{1,0:T(8,128)(2,1)} %shard_map.138.own_ref, bf16[64,4096]{1,0:T(8,128)(2,1)} %copy-done.2, bf16[32,128,896]{2,1,0:T(8,128)(2,1)} %bitcast.22), custom_call_target="tpu_custom_call" | custom-call | tf_op jit(solution)/shard_map/pallas_call | solution.py:205
  246.9 1.9 collective-permute-start.4
  248.8 2.1 collective-permute-done.4
  250.9 1.4 add_convert_fusion
  252.3 46.2 %all_to_all.10 = bf16[8,64,512]{2,1,0:T(8,128)(2,1)S(1)} all-to-all(bf16[8,64,512]{2,1,0:T(8,128)(2,1)S(1)} %add_convert_fusion), channel_id=1, replica_groups=mesh['y'=4,'x'=4,'c'=2,'zl'=8,'zh'=2] {'zl'}, dimensions={0} | all-to-all | bytes 1048576 | tf_op jit(solution)/shard_map/all_to_all | solution.py:268
  298.7 1.9 collective-permute-start.5
  300.7 3.9 %collective-permute-done.5 = bf16[64,256]{1,0:T(8,128)(2,1)S(1)} collective-permute-done((bf16[64,256]{1,0:T(8,128)(2,1)S(1)}, bf16[64,256]{1,0:T(8,128)(2,1)S(1)}, u32[]{:S(2)}, u32[]{:S(2)}) %collective-permute-start.5) | collective-permute-done | bytes 32800 | tf_op jit(solution)/shard_map/ppermute | solution.py:272
  304.6 0.6 add_convert_fusion.1
  (21 shorter events, 1.5 us)
Async XLA Ops:
  6.5 221.6 %all-gather.4.cloned.1.call-start = ((), (), s32[]{:S(2)}) async-start(), calls=%async_computation.2 | async-start | bytes 7569408 | tf_op jit(solution)/shard_map/all_gather | solution.py:226
  7.5 7.3 %collective-permute-start.3 = (bf16[128,896]{0,1:T(8,128)(2,1)S(1)}, bf16[128,896]{0,1:T(8,128)(2,1)S(1)}, u32[]{:S(2)}, u32[]{:S(2)}) collective-permute-start(bf16[128,896]{0,1:T(8,128)(2,1)S(1)} %pad_maximum_fusion), channel_id=1, source_target_pairs={{0,0},{1,16},{16,1},{17,17},{2,2},{3,18},{18,3},{19,19},{4,4},{5,2... | collective-permute-start | bytes 688136 | tf_op jit(solution)/shard_map/ppermute | solution.py:225
  14.9 0.7 copy-start.3
  21.3 27.3 %all-to-all-start = ((bf16[32,72,256]{2,1,0:T(8,128)(2,1)}), bf16[32,72,256]{2,1,0:T(8,128)(2,1)S(1)}, u32[]{:S(2)}, u32[]{:S(2)}) async-start(bf16[32,72,256]{2,1,0:T(8,128)(2,1)} %broadcast_in_dim.10), calls=%async_computation | async-start | bytes 2359296 | tf_op jit(solution)/shard_map/all_to_all | solution.py:233
  48.6 1.1 copy-start
  53.0 8.5 %collective-permute-start = (bf16[72,256]{1,0:T(8,128)(2,1)S(1)}, bf16[72,256]{1,0:T(8,128)(2,1)S(1)}, u32[]{:S(2)}, u32[]{:S(2)}) collective-permute-start(bf16[72,256]{1,0:T(8,128)(2,1)S(1)} %get-tuple-element.20), channel_id=1, source_target_pairs={{0,1},{1,0},{2,3},{3,2},{4,5},{5,4},{6,7},{7,6},{8,9},{9,8},{10,11... | collective-permute-start | bytes 110600 | tf_op jit(solution)/shard_map/ppermute | solution.py:245
  104.3 7.7 %copy-start.1 = (bf16[16,72,256]{2,1,0:T(8,128)(2,1)}, bf16[16,72,256]{2,1,0:T(8,128)(2,1)S(1)}, u32[]{:S(2)}) copy-start(bf16[16,72,256]{2,1,0:T(8,128)(2,1)S(1)} %all-gather) | copy-start | bytes 1769476
  104.3 7.0 %collective-permute-start.1 = (bf16[8,2,1,256]{3,2,1,0:T(2,128)(2,1)S(1)}, bf16[8,2,1,256]{3,2,1,0:T(2,128)(2,1)S(1)}, u32[]{:S(2)}, u32[]{:S(2)}) collective-permute-start(bf16[8,2,1,256]{3,2,1,0:T(2,128)(2,1)S(1)} %slice.4), channel_id=1, source_target_pairs={{0,1},{1,16},{16,17},{17,32},{32,33},{33,48},{48,49},{49,64},{64,6... | collective-permute-start | bytes 24584 | tf_op jit(solution)/shard_map/ppermute | solution.py:248
  114.5 124.4 %collective-permute-start.2 = (bf16[64,4096]{1,0:T(8,128)(2,1)}, bf16[64,4096]{1,0:T(8,128)(2,1)S(1)}, u32[]{:S(2)}, u32[]{:S(2)}) collective-permute-start(bf16[64,4096]{1,0:T(8,128)(2,1)} %shard_map.138.own_ref), channel_id=1, source_target_pairs={{0,16},{16,0},{1,17},{17,1},{2,18},{18,2},{3,19},{19,3},{4,20},{20... | collective-permute-start | bytes 1572872 | tf_op jit(solution)/shard_map/ppermute | solution.py:258
  238.9 65.7 %copy-start.4 = (f32[128,256]{1,0:T(8,128)S(1)}, f32[128,256]{1,0:T(8,128)}, u32[]{:S(2)}) copy-start(f32[128,256]{1,0:T(8,128)} %get-tuple-element.15) | copy-start | bytes 393220
  238.9 0.8 copy-start.2
  246.9 4.0 %collective-permute-start.4 = (bf16[8,64,512]{2,1,0:T(8,128)(2,1)}, bf16[8,64,512]{2,1,0:T(8,128)(2,1)S(1)}, u32[]{:S(2)}, u32[]{:S(2)}) collective-permute-start(bf16[8,64,512]{2,1,0:T(8,128)(2,1)} %get-tuple-element.18), channel_id=1, source_target_pairs={{0,16},{16,0},{1,17},{17,1},{2,18},{18,2},{3,19},{19,3},{4,20},{20... | collective-permute-start | bytes 1572872 | tf_op jit(solution)/shard_map/ppermute | solution.py:267
  298.7 5.8 %collective-permute-start.5 = (bf16[64,256]{1,0:T(8,128)(2,1)S(1)}, bf16[64,256]{1,0:T(8,128)(2,1)S(1)}, u32[]{:S(2)}, u32[]{:S(2)}) collective-permute-start(bf16[64,256]{1,0:T(8,128)(2,1)S(1)} %bitcast.27), channel_id=1, source_target_pairs={{0,1},{1,0},{2,3},{3,2},{4,5},{5,4},{6,7},{7,6},{8,9},{9,8},{10,11... | collective-permute-start | bytes 98312 | tf_op jit(solution)/shard_map/ppermute | solution.py:272
Sparse Core Ops, SparseCore 0:
  15.7 212.3 all-gather.3

commit v2 on v1

v2 whole, which is shorter than its diff:
```python
import functools

import jax
import jax.numpy as jnp
from jax import lax
from jax.experimental import pallas as pl
from jax.experimental.pallas import tpu as pltpu
from jax.sharding import Mesh
from jax.sharding import PartitionSpec as P

SEQ = ("y", "x", "c")
EPS_GROUP = 0.00064
EPS_LAYER = 1e-05
F32 = jnp.float32
BF16 = jnp.bfloat16
NN = (((1,), (0,)), ((), ()))
NT = (((1,), (1,)), ((), ()))
TN = (((0,), (0,)), ((), ()))


def dot(a, b, dims):
    return lax.dot_general(a, b, dims, preferred_element_type=F32)


def iota(shape, dim):
    return lax.broadcasted_iota(jnp.int32, shape, dim)


def hi_lo(x):
    hi = x.astype(BF16)
    return hi, (x - hi.astype(F32)).astype(BF16)


def wkv_kernel(r_ref, k_ref, v_ref, logit_ref, boost_ref, own_ref, rec_ref, pay_ref):
    rows, width = r_ref.shape
    logw = -jnp.exp(logit_ref[...])
    lower = (iota((rows, rows), 0) >= iota((rows, rows), 1)).astype(BF16)
    part0, rest = logw.astype(BF16), logw
    rest = rest - part0.astype(F32)
    part1, part2 = hi_lo(rest)
    incl = dot(lower, part0, NN) + dot(lower, part1, NN) + dot(lower, part2, NN)
    excl = incl - logw
    total = incl[rows - 1 : rows]
    half = rows // 2
    edge = incl[half - 1 : half]
    top = iota((rows, width), 0) < half
    ref = jnp.where(top, incl[half // 2 - 1 : half // 2], incl[half + half // 2 - 1 : half + half // 2])
    r = r_ref[...].astype(F32)
    k = k_ref[...].astype(F32)
    v = v_ref[...]
    r_in = (r * jnp.exp(excl - ref)).astype(BF16)
    k_in = (k * jnp.exp(ref - incl)).astype(BF16)
    r_off = (r * jnp.exp(jnp.minimum(excl - edge, 0.0))).astype(BF16)
    k_off = (k * jnp.exp(jnp.minimum(edge - incl, 0.0))).astype(BF16)
    rec_ref[...] = (r * jnp.exp(excl)).astype(BF16)
    k_end = (k * jnp.exp(total - incl)).astype(BF16)
    now = r * boost_ref[...] * k
    row, col = iota((rows, rows), 0), iota((rows, rows), 1)
    same = (row > col) & ((row < half) == (col < half))
    cross = (row >= half) & (col < half)
    left = iota((rows, 128), 1) < 64
    zero = jnp.zeros((), BF16)
    for p in range(width // 128):
        at = slice(128 * p, 128 * p + 128)
        scores, values, sums = [], [], []
        for mask in (left, ~left):
            inner = dot(r_in[:, at], jnp.where(mask, k_in[:, at], zero), NT)
            outer = dot(r_off[:, at], jnp.where(mask, k_off[:, at], zero), NT)
            scores.append(jnp.where(same, inner, jnp.where(cross, outer, 0.0)).astype(BF16))
            values.append(jnp.where(mask, v[:, at], zero))
            sums.append(jnp.sum(jnp.where(mask, now[:, at], 0.0), axis=1, keepdims=True))
        out = dot(jnp.concatenate(scores, axis=1), jnp.concatenate(values, axis=0), NN)
        own_ref[:, at] = out + jnp.where(left, sums[0], sums[1]) * v[:, at].astype(F32)
        state = dot(v[:, at], k_end[:, at], TN)
        pay_ref[0:64, at] = jnp.where(left[0:64], state[0:64], state[64:128]).astype(BF16)
    hi, lo = hi_lo(total)
    line = iota((8, width), 0)
    pay_ref[64:72, :] = jnp.where(
        line == 0, hi.astype(F32), jnp.where(line == 1, lo.astype(F32), 0.0)
    ).astype(BF16)


def middle_kernel(
    at_ref, all_ref, own_ref, rec_ref, skip_ref, gate_ref, gn_ref, ln_ref,
    mid_ref, main_ref, edge_ref, vec_ref,
):
    rows, width = own_ref.shape
    main = main_ref.shape[0]

    def join(i, state):
        piece = all_ref[i].astype(F32)
        return state * jnp.exp(piece[64:65] + piece[65:66]) + piece[0:64]

    state = lax.fori_loop(0, at_ref[0], join, jnp.zeros((64, width), F32))
    left64 = iota((64, 128), 1) < 64
    left = iota((rows, 128), 1) < 64

    def mean(x):
        a = jnp.sum(jnp.where(left, x, 0.0), axis=1, keepdims=True)
        b = jnp.sum(jnp.where(left, 0.0, x), axis=1, keepdims=True)
        return jnp.where(left, a, b) * (1.0 / 64)

    for p in range(width // 128):
        at = slice(128 * p, 128 * p + 128)
        here = state[:, at]
        both = jnp.concatenate(
            [jnp.where(left64, here, 0.0), jnp.where(left64, 0.0, here)], axis=0
        ).astype(BF16)
        wkv = own_ref[:, at] + dot(rec_ref[:, at], both, NT)
        centre = wkv - mean(wkv)
        normed = centre * lax.rsqrt(mean(centre * centre) + EPS_GROUP)
        normed = normed * gn_ref[0:1, at] + gn_ref[1:2, at]
        gate = gate_ref[:, at].astype(F32)
        middle = skip_ref[:, at].astype(F32) + normed * (gate / (1.0 + jnp.exp(-gate)))
        mid_ref[:, at] = middle
        main_ref[:, at] = middle[0:main].astype(BF16)
        edge_ref[:, at] = middle[main:].astype(BF16)
    line = iota((8, width), 0)
    tail = jnp.zeros((8, width), F32)
    for n in range(3):
        hi, lo = hi_lo(ln_ref[n : n + 1])
        tail = jnp.where(line == 2 * n + 1, hi.astype(F32), tail)
        tail = jnp.where(line == 2 * n + 2, lo.astype(F32), tail)
    vec_ref[...] = tail.astype(BF16)


def ffn_kernel(at_ref, main_ref, side_ref, w_hbm, out_ref, w_ref, sems):
    groups, rows, width = out_ref.shape
    main = main_ref.shape[1]
    full = groups * width
    wide = w_hbm.shape[1]
    units = wide // 2
    cut = units + 64
    chunks = sems.shape[0]
    step = full // chunks

    def copy(q):
        at = pl.ds(q * step, step)
        return pltpu.make_async_copy(w_hbm.at[at], w_ref.at[at], sems.at[q])

    for q in range(chunks):
        copy(q).start()

    def load(g):
        return jnp.concatenate([main_ref[g].astype(F32), side_ref[g, 0].astype(F32)], axis=0)

    def stats(get, n):
        first, second = jnp.zeros((n, width), F32), jnp.zeros((n, width), F32)
        for g in range(groups):
            x = get(g)
            first, second = first + x, second + x * x
        mu = jnp.sum(first, axis=1, keepdims=True) / full
        var = jnp.sum(second, axis=1, keepdims=True) / full - mu * mu
        return mu, lax.rsqrt(var + EPS_LAYER)

    mu, scale = stats(load, rows)
    pmu, pscale = stats(lambda g: side_ref[g, 1].astype(F32)[0:1], 1)
    live = at_ref[0] > 0
    head = iota((rows, width), 0) == 0
    acc = jnp.zeros((rows, cut), F32)
    for g in range(groups):
        side = side_ref[g, 1].astype(F32)
        gain, bias, blend = (side[n : n + 1] + side[n + 1 : n + 2] for n in (1, 3, 5))
        xn = ((load(g) - mu) * scale * gain + bias).astype(BF16).astype(F32)
        pn = ((side[0:1] - pmu) * pscale * gain + bias).astype(BF16).astype(F32)
        pn = jnp.where(live, pn, 0.0)
        prev = jnp.where(head, pn, pltpu.roll(xn, 1, 0))
        xk = (xn + (prev - xn) * blend).astype(BF16)
        if g * width % step == 0:
            copy(g * width // step).wait()
        acc = acc + dot(xk, w_ref[g * width : (g + 1) * width, 0:cut], NN)
    hidden = jnp.square(jnp.maximum(acc, 0.0))
    hidden = jnp.where(iota(hidden.shape, 1) < units, hidden, 0.0)
    hidden = pltpu.roll(hidden, 64, 1).astype(BF16)
    for g in range(groups):
        out = dot(hidden, w_ref[g * width : (g + 1) * width, units - 64 : wide], NT)
        out_ref[g] = out.astype(BF16)


VMEM = functools.partial(pl.BlockSpec, memory_space=pltpu.VMEM)
SMEM = functools.partial(pl.BlockSpec, memory_space=pltpu.SMEM)


def make(interpret):
    def call(kernel, outs, *args, in_specs=None, **more):
        return pl.pallas_call(
            kernel,
            out_shape=[jax.ShapeDtypeStruct(s, t) for s, t in outs],
            in_specs=in_specs or [VMEM() for _ in args],
            out_specs=[VMEM() for _ in outs],
            interpret=interpret,
            **more,
        )(*args)

    def local(
        skip, recept, keys, values, gating, logit, boost, gn_gain, gn_bias, ln_gain, ln_bias, blend, wk, wv
    ):
        rows, width = skip.shape
        groups = lax.axis_size("hid")
        blocks = lax.axis_size(SEQ)
        at_seq = lax.axis_index(SEQ).reshape(1)

        weights = lax.all_gather(jnp.concatenate([wk, wv], axis=1), SEQ, tiled=True)
        own, recall, state = call(
            wkv_kernel,
            [((rows, width), F32), ((rows, width), BF16), ((72, width), BF16)],
            recept, keys, values, logit, boost.reshape(1, width),
        )
        states = lax.all_to_all(
            jnp.broadcast_to(state, (blocks, *state.shape)), SEQ, 0, 0, tiled=True
        )
        middle, main, edge, vecs = call(
            middle_kernel,
            [((rows, width), F32), ((rows - 8, width), BF16), ((8, width), BF16), ((8, width), BF16)],
            at_seq, states, own, recall, skip, gating,
            jnp.stack([gn_gain, gn_bias]), jnp.stack([ln_gain, ln_bias, blend]),
            in_specs=[SMEM()] + [VMEM()] * 7,
        )
        before = lax.ppermute(edge, SEQ, [(n, n + 1) for n in range(blocks - 1)])
        side = jnp.stack([edge, jnp.concatenate([before[7:8], vecs[1:8]])])
        side = lax.all_to_all(
            jnp.broadcast_to(side, (groups, *side.shape)), "hid", 0, 0, tiled=True
        )
        main = lax.all_gather(main, "hid")
        (part,) = call(
            ffn_kernel,
            [((groups, rows, width), BF16)],
            at_seq, main, side, weights,
            in_specs=[SMEM(), VMEM(), VMEM(), pl.BlockSpec(memory_space=pl.ANY)],
            scratch_shapes=[pltpu.VMEM(weights.shape, BF16), pltpu.SemaphoreType.DMA((min(8, groups),))],
        )
        part = lax.all_to_all(part, "hid", 0, 0, tiled=True)
        return (middle + jnp.sum(part.astype(F32), axis=0)).astype(BF16)

    return local


def build(finer, interpret=False):
    tile, vec = P(SEQ, "hid"), P("hid")
    return jax.shard_map(
        make(interpret),
        mesh=finer,
        in_specs=(tile,) * 6 + (P("hid", None),) + (vec,) * 5 + (tile, tile),
        out_specs=tile,
        check_vma=False,
    )


def solution(mesh):
    return build(Mesh(mesh.devices.reshape(4, 4, 2, mesh.shape["hid"]), (*SEQ, "hid")))
```

time: 313 us -> 180 us (0.58)
  the two profiles are of different devices: /device:TPU:32 before, /device:TPU:6 now
where the time goes in v2:
time: 180 us; the launch traced here: 178 us
  blocking collectives  97 us (54%)
  starting transfers between devices  27.8 us (15%)
  waiting for transfers between devices  16 us (9%)
  between operations  13.5 us (8%)
  Pallas kernels  12.2 us (7%)
  local copies, waits for them, and re-layouts  8.41 us (5%)
  other arithmetic  3.45 us (2%)
    all_to_all x1, blocking collectives, local(): part = lax.all_to_all(part, 'hid', 0, 0, tiled=True)  56.5 us
    all_gather x1, blocking collectives, local(): main = lax.all_gather(main, 'hid')  40.5 us
    all_to_all x1, waiting for transfers between devices, local(): lax.all_to_all(jnp.broadcast_to(state, (blocks, *state.shape)), SEQ, 0, 0...  15.7 us
    all_to_all x1, starting transfers between devices, local(): lax.all_to_all(jnp.broadcast_to(side, (groups, *side.shape)), 'hid', 0, 0...  13.7 us
    pallas_call x3, Pallas kernels, call(): pl.pallas_call(kernel, out_shape=[jax.ShapeDtypeStruct(s, t) for s, t in...  12.2 us
    all_to_all x1, starting transfers between devices, local(): lax.all_to_all(jnp.broadcast_to(state, (blocks, *state.shape)), SEQ, 0, 0...  9.45 us
    ppermute x1, starting transfers between devices, local(): before = lax.ppermute(edge, SEQ, [(n, n + 1) for n in range(blocks - 1)])  4.62 us
    unnamed x18, local copies, waits for them, and re-layouts  3.76 us
  transfers between devices with their start and end apart: 4, of which 2 were waited for; matrix products, arithmetic and copies ran while one was open for 4% of the time, Pallas kernels for 3%

profile of v2, /device:TPU:6, one launch (start us, length us, event | category | flops | bytes accessed | tf_op | source)
XLA Modules:
  0.0 178.4 jit_solution(8174461556105345739)
XLA Ops:
  6.5 0.0 all-gather.3.cloned.1.call-start
  6.5 1.0 copy.16
  7.5 1.0 copy.15
  8.6 0.8 pad_maximum_fusion
  9.4 0.0 copy-start.5
  9.4 0.0 all-gather.3.cloned.1.call-update
  9.4 1.4 reshape.7.boost_ref
  10.8 2.5 %shard_map.136 = (f32[128,256]{1,0:T(8,128)}, bf16[128,256]{1,0:T(8,128)(2,1)}, bf16[72,256]{1,0:T(8,128)(2,1)}) custom-call(bf16[128,256]{1,0:T(8,128)(2,1)} %r_ref.1, bf16[128,256]{1,0:T(8,128)(2,1)} %k_ref.1, bf16[128,256]{1,0:T(8,128)(2,1)} %v_ref.1, f32[128,256]{1,0:T(8,128)} %logit_ref.1, f32[1,256]{1,0:T(1,128)} %reshape.7.boost_ref), custom_call_target="tpu_custom_call" | custom-call | tf_op jit(solution)/shard_map/pallas_call | solution.py:186
  13.2 1.9 %broadcast_in_dim.6 = bf16[32,72,256]{2,1,0:T(8,128)(2,1)} broadcast(bf16[72,256]{1,0:T(8,128)(2,1)} %get-tuple-element.12), dimensions={1,2} | broadcast | bytes 1216512 | tf_op jit(solution)/shard_map/broadcast_in_dim | solution.py:210
  15.2 9.4 %all-to-all-start = ((bf16[32,72,256]{2,1,0:T(8,128)(2,1)}), bf16[32,72,256]{2,1,0:T(8,128)(2,1)S(1)}, u32[]{:S(2)}, u32[]{:S(2)}) async-start(bf16[32,72,256]{2,1,0:T(8,128)(2,1)} %broadcast_in_dim.6), calls=%async_computation | async-start | bytes 2359296 | tf_op jit(solution)/shard_map/all_to_all | solution.py:209
  24.7 0.0 copy-done.6
  24.7 0.0 copy-done.7
  24.7 0.6 pad_maximum_fusion.3.gn_ref
  25.3 0.6 pad_maximum_fusion.2.ln_ref
  25.9 15.7 %all-to-all-done.all_ref = bf16[32,72,256]{2,1,0:T(8,128)(2,1)S(1)} async-done(((bf16[32,72,256]{2,1,0:T(8,128)(2,1)}), bf16[32,72,256]{2,1,0:T(8,128)(2,1)S(1)}, u32[]{:S(2)}, u32[]{:S(2)}) %all-to-all-start) | async-done | bytes 1179680 | tf_op jit(solution)/shard_map/all_to_all | solution.py:209
  41.5 1.1 copy-done
  42.6 2.6 %shard_map.137 = (f32[128,256]{1,0:T(8,128)}, bf16[120,256]{1,0:T(8,128)(2,1)}, bf16[8,256]{1,0:T(8,128)(2,1)}, bf16[8,256]{1,0:T(8,128)(2,1)}) custom-call(s32[1]{0:T(128)} %bitcast.at_ref, bf16[32,72,256]{2,1,0:T(8,128)(2,1)} %copy-done, f32[128,256]{1,0:T(8,128)} %get-tuple-element.13.own_ref, bf16[128,256]{1,0:T(8,128)(2,1)} %get-tuple-element.14.rec_ref, ...), custom_call_target="tpu_custom_call" | custom-call | tf_op jit(solution)/shard_map/pallas_call | solution.py:186
  45.2 4.6 %collective-permute-start = (bf16[8,256]{1,0:T(8,128)(2,1)}, bf16[8,256]{1,0:T(8,128)(2,1)S(1)}, u32[]{:S(2)}, u32[]{:S(2)}) collective-permute-start(bf16[8,256]{1,0:T(8,128)(2,1)} %get-tuple-element.17), channel_id=1, source_target_pairs={{0,16},{16,32},{32,48},{48,64},{64,80},{80,96},{96,112},{112,128},... | collective-permute-start | bytes 12296 | tf_op jit(solution)/shard_map/ppermute | solution.py:219
  49.9 0.7 slice.7
  50.5 0.3 collective-permute-done
  50.9 0.7 pad_maximum_fusion.1
  51.6 0.7 broadcast_in_dim.7
  52.2 13.7 %all-to-all-start.1 = ((bf16[16,2,8,256]{3,2,1,0:T(8,128)(2,1)}), bf16[16,2,8,256]{3,2,1,0:T(8,128)(2,1)S(1)}, u32[]{:S(2)}, u32[]{:S(2)}) async-start(bf16[16,2,8,256]{3,2,1,0:T(8,128)(2,1)} %broadcast_in_dim.7), calls=%async_computation.1 | async-start | bytes 262144 | tf_op jit(solution)/shard_map/all_to_all | solution.py:221
  66.0 40.5 %all-gather = bf16[1920,256]{1,0:T(8,128)(2,1)} all-gather(bf16[120,256]{1,0:T(8,128)(2,1)} %get-tuple-element.16), channel_id=2, replica_groups=mesh['y'=4,'x'=4,'c'=2,'hid'=16] {'hid'}, dimensions={0}, use_global_device_ids=true | all-gather | bytes 1044480 | tf_op jit(solution)/shard_map/all_gather | solution.py:224
  106.5 0.0 all-to-all-done.1.side_ref
  106.5 0.0 all-gather.3.cloned.1.call-done.w_hbm
  106.5 0.6 copy-done.1
  107.1 7.1 %shard_map.138 = bf16[16,128,256]{2,1,0:T(8,128)(2,1)} custom-call(s32[1]{0:T(128)} %bitcast.at_ref, bf16[16,120,256]{2,1,0:T(8,128)(2,1)} %bitcast.10, bf16[16,2,8,256]{3,2,1,0:T(8,128)(2,1)} %copy-done.1, bf16[4096,896]{1,0:T(8,128)(2,1)} %all-gather.3.cloned.1.call-done.w_hbm), custom_call_target="tpu_custom_call" | custom-call | tf_op jit(solution)/shard_map/pallas_call | solution.py:186
  114.2 0.0 copy-start.2
  114.3 56.5 %all_to_all.15 = bf16[16,128,256]{2,1,0:T(8,128)(2,1)S(1)} all-to-all(bf16[16,128,256]{2,1,0:T(8,128)(2,1)} %shard_map.138), channel_id=1, replica_groups=mesh['y'=4,'x'=4,'c'=2,'hid'=16] {'hid'}, dimensions={0} | all-to-all | bytes 2097152 | tf_op jit(solution)/shard_map/all_to_all | solution.py:232
  170.8 0.1 convert_reduce_fusion
  170.9 0.6 add_convert_fusion
  (12 shorter events, 0.0 us)
Async XLA Ops:
  6.5 100.0 %all-gather.3.cloned.1.call-start = ((), (), s32[]{:S(2)}) async-start(), calls=%async_computation.3 | async-start | bytes 7569408 | tf_op jit(solution)/shard_map/all_gather | solution.py:203
  9.3 15.3 %copy-start.6 = (f32[256]{0:T(256)S(1)}, f32[256]{0:T(256)}, u32[]{:S(2)}) copy-start(f32[256]{0:T(256)} %param.22) | copy-start | bytes 3076
  9.4 15.3 %copy-start.7 = (f32[256]{0:T(256)S(1)}, f32[256]{0:T(256)}, u32[]{:S(2)}) copy-start(f32[256]{0:T(256)} %param.21) | copy-start | bytes 3076
  9.4 15.9 %copy-start.3 = (f32[256]{0:T(256)S(1)}, f32[256]{0:T(256)}, u32[]{:S(2)}) copy-start(f32[256]{0:T(256)} %param.25) | copy-start | bytes 3076
  9.4 15.9 %copy-start.4 = (f32[256]{0:T(256)S(1)}, f32[256]{0:T(256)}, u32[]{:S(2)}) copy-start(f32[256]{0:T(256)} %param.24) | copy-start | bytes 3076
  9.4 15.9 %copy-start.5 = (f32[256]{0:T(256)S(1)}, f32[256]{0:T(256)}, u32[]{:S(2)}) copy-start(f32[256]{0:T(256)} %param.23) | copy-start | bytes 3076
  15.2 26.3 %all-to-all-start = ((bf16[32,72,256]{2,1,0:T(8,128)(2,1)}), bf16[32,72,256]{2,1,0:T(8,128)(2,1)S(1)}, u32[]{:S(2)}, u32[]{:S(2)}) async-start(bf16[32,72,256]{2,1,0:T(8,128)(2,1)} %broadcast_in_dim.6), calls=%async_computation | async-start | bytes 2359296 | tf_op jit(solution)/shard_map/all_to_all | solution.py:209
  41.5 1.1 copy-start
  45.2 5.6 %collective-permute-start = (bf16[8,256]{1,0:T(8,128)(2,1)}, bf16[8,256]{1,0:T(8,128)(2,1)S(1)}, u32[]{:S(2)}, u32[]{:S(2)}) collective-permute-start(bf16[8,256]{1,0:T(8,128)(2,1)} %get-tuple-element.17), channel_id=1, source_target_pairs={{0,16},{16,32},{32,48},{48,64},{64,80},{80,96},{96,112},{112,128},... | collective-permute-start | bytes 12296 | tf_op jit(solution)/shard_map/ppermute | solution.py:219
  52.2 54.3 %all-to-all-start.1 = ((bf16[16,2,8,256]{3,2,1,0:T(8,128)(2,1)}), bf16[16,2,8,256]{3,2,1,0:T(8,128)(2,1)S(1)}, u32[]{:S(2)}, u32[]{:S(2)}) async-start(bf16[16,2,8,256]{3,2,1,0:T(8,128)(2,1)} %broadcast_in_dim.7), calls=%async_computation.1 | async-start | bytes 262144 | tf_op jit(solution)/shard_map/all_to_all | solution.py:221
  106.5 0.7 copy-start.1
  114.2 56.7 %copy-start.2 = (f32[128,256]{1,0:T(8,128)S(1)}, f32[128,256]{1,0:T(8,128)}, u32[]{:S(2)}) copy-start(f32[128,256]{1,0:T(8,128)} %get-tuple-element.15) | copy-start | bytes 393220
Sparse Core Ops, SparseCore 0:
  10.5 74.6 all-gather.2

commit v3 on v2

--- a/solution.py
+++ b/solution.py
@@ -54,7 +54,8 @@
     k_off = (k * jnp.exp(jnp.minimum(edge - incl, 0.0))).astype(BF16)
     rec_ref[...] = (r * jnp.exp(excl)).astype(BF16)
     k_end = (k * jnp.exp(total - incl)).astype(BF16)
-    now = r * boost_ref[...] * k
+    boost = jnp.concatenate([boost_ref[h : h + 1] for h in range(boost_ref.shape[0])], axis=1)
+    now = r * boost * k
     row, col = iota((rows, rows), 0), iota((rows, rows), 1)
     same = (row > col) & ((row < half) == (col < half))
     cross = (row >= half) & (col < half)
@@ -80,18 +81,37 @@
     ).astype(BF16)
 
 
+def pair_kernel(pair_ref, wk_ref, wv_ref, out_ref, w_ref):
+    units = wk_ref.shape[0]
+    w_ref[0:units] = wk_ref[...]
+    w_ref[units:] = wv_ref[...]
+    a, b = pair_ref[0].astype(F32), pair_ref[1].astype(F32)
+    last = b[64:65] + b[65:66]
+    state = (a[0:64] * jnp.exp(last) + b[0:64]).astype(BF16)
+    hi, lo = hi_lo(a[64:65] + a[65:66] + last)
+    line = iota((8, a.shape[1]), 0)
+    tail = jnp.where(line == 0, hi.astype(F32), jnp.where(line == 1, lo.astype(F32), 0.0)).astype(BF16)
+    for n in range(out_ref.shape[0]):
+        out_ref[n, 0:64] = state
+        out_ref[n, 64:72] = tail
+
+
 def middle_kernel(
-    at_ref, all_ref, own_ref, rec_ref, skip_ref, gate_ref, gn_ref, ln_ref,
-    mid_ref, main_ref, edge_ref, vec_ref,
+    at_ref, all_ref, pair_ref, own_ref, rec_ref, skip_ref, gate_ref, gn_ref, ln_ref,
+    mid_ref, main_ref, edge_ref, tile_ref,
 ):
     rows, width = own_ref.shape
     main = main_ref.shape[0]
 
-    def join(i, state):
-        piece = all_ref[i].astype(F32)
-        return state * jnp.exp(piece[64:65] + piece[65:66]) + piece[0:64]
-
-    state = lax.fori_loop(0, at_ref[0], join, jnp.zeros((64, width), F32))
+    def join(ref):
+        def step(i, state):
+            piece = ref[i].astype(F32)
+            return state * jnp.exp(piece[64:65] + piece[65:66]) + piece[0:64]
+
+        return step
+
+    state = lax.fori_loop(0, at_ref[0], join(all_ref), jnp.zeros((64, width), F32))
+    state = lax.fori_loop(0, at_ref[1], join(pair_ref), state)
     left64 = iota((64, 128), 1) < 64
     left = iota((rows, 128), 1) < 64
 
@@ -116,27 +136,31 @@
         main_ref[:, at] = middle[0:main].astype(BF16)
         edge_ref[:, at] = middle[main:].astype(BF16)
     line = iota((8, width), 0)
-    tail = jnp.zeros((8, width), F32)
+    tail = jnp.where(line == 0, mid_ref[rows - 1 : rows, :], 0.0)
     for n in range(3):
         hi, lo = hi_lo(ln_ref[n : n + 1])
         tail = jnp.where(line == 2 * n + 1, hi.astype(F32), tail)
         tail = jnp.where(line == 2 * n + 2, lo.astype(F32), tail)
-    vec_ref[...] = tail.astype(BF16)
+    tile_ref[...] = tail.astype(BF16)
 
 
 def ffn_kernel(at_ref, main_ref, side_ref, w_hbm, out_ref, w_ref, sems):
     groups, rows, width = out_ref.shape
     main = main_ref.shape[1]
     full = groups * width
-    wide = w_hbm.shape[1]
-    units = wide // 2
-    cut = units + 64
+    depth = w_hbm.shape[1]
+    tall = w_hbm.shape[0] // (full // depth)
+    units = tall // 2
     chunks = sems.shape[0]
     step = full // chunks
 
     def copy(q):
-        at = pl.ds(q * step, step)
+        at = pl.ds(q * step // depth * tall, step // depth * tall)
         return pltpu.make_async_copy(w_hbm.at[at], w_ref.at[at], sems.at[q])
+
+    def weights(g, first):
+        blocks = range(g * width // depth, (g + 1) * width // depth)
+        return jnp.concatenate([w_ref[b * tall + first : b * tall + first + units] for b in blocks], axis=1)
 
     for q in range(chunks):
         copy(q).start()
@@ -157,7 +181,7 @@
     pmu, pscale = stats(lambda g: side_ref[g, 1].astype(F32)[0:1], 1)
     live = at_ref[0] > 0
     head = iota((rows, width), 0) == 0
-    acc = jnp.zeros((rows, cut), F32)
+    acc = jnp.zeros((rows, units), F32)
     for g in range(groups):
         side = side_ref[g, 1].astype(F32)
         gain, bias, blend = (side[n : n + 1] + side[n + 1 : n + 2] for n in (1, 3, 5))
@@ -168,13 +192,10 @@
         xk = (xn + (prev - xn) * blend).astype(BF16)
         if g * width % step == 0:
             copy(g * width // step).wait()
-        acc = acc + dot(xk, w_ref[g * width : (g + 1) * width, 0:cut], NN)
-    hidden = jnp.square(jnp.maximum(acc, 0.0))
-    hidden = jnp.where(iota(hidden.shape, 1) < units, hidden, 0.0)
-    hidden = pltpu.roll(hidden, 64, 1).astype(BF16)
+        acc = acc + dot(xk, weights(g, 0), NT)
+    hidden = jnp.square(jnp.maximum(acc, 0.0)).astype(BF16)
     for g in range(groups):
-        out = dot(hidden, w_ref[g * width : (g + 1) * width, units - 64 : wide], NT)
-        out_ref[g] = out.astype(BF16)
+        out_ref[g] = dot(hidden, weights(g, units), NN).astype(BF16)
 
 
 VMEM = functools.partial(pl.BlockSpec, memory_space=pltpu.VMEM)
@@ -200,24 +221,31 @@
         blocks = lax.axis_size(SEQ)
         at_seq = lax.axis_index(SEQ).reshape(1)
 
-        weights = lax.all_gather(jnp.concatenate([wk, wv], axis=1), SEQ, tiled=True)
+        core = lax.axis_index("c")
+        chips = blocks // lax.axis_size("c")
         own, recall, state = call(
             wkv_kernel,
             [((rows, width), F32), ((rows, width), BF16), ((72, width), BF16)],
-            recept, keys, values, logit, boost.reshape(1, width),
-        )
-        states = lax.all_to_all(
-            jnp.broadcast_to(state, (blocks, *state.shape)), SEQ, 0, 0, tiled=True
-        )
-        middle, main, edge, vecs = call(
+            recept, keys, values, logit, boost,
+        )
+        pair = lax.all_gather(state, "c")
+        states, weights = call(
+            pair_kernel,
+            [((chips, 72, width), BF16), ((2 * wk.shape[1], wk.shape[0]), BF16)],
+            pair, wk.T, wv.T,
+        )
+        weights = lax.all_gather(weights, SEQ, tiled=True)
+        states = lax.all_to_all(states, ("y", "x"), 0, 0, tiled=True)
+        middle, main, edge, tile = call(
             middle_kernel,
             [((rows, width), F32), ((rows - 8, width), BF16), ((8, width), BF16), ((8, width), BF16)],
-            at_seq, states, own, recall, skip, gating,
+            jnp.stack([lax.axis_index(("y", "x")), core]),
+            states, pair, own, recall, skip, gating,
             jnp.stack([gn_gain, gn_bias]), jnp.stack([ln_gain, ln_bias, blend]),
-            in_specs=[SMEM()] + [VMEM()] * 7,
-        )
-        before = lax.ppermute(edge, SEQ, [(n, n + 1) for n in range(blocks - 1)])
-        side = jnp.stack([edge, jnp.concatenate([before[7:8], vecs[1:8]])])
+            in_specs=[SMEM()] + [VMEM()] * 8,
+        )
+        tile = lax.ppermute(tile, SEQ, [(n, (n + 1) % blocks) for n in range(blocks)])
+        side = jnp.stack([edge, tile])
         side = lax.all_to_all(
             jnp.broadcast_to(side, (groups, *side.shape)), "hid", 0, 0, tiled=True
         )

time: 180 us -> 169 us (0.939)
  local copies, waits for them, and re-layouts: 8.41 us -> 2.13 us
  waiting for transfers between devices: 16 us -> 10.5 us
  starting transfers between devices: 27.8 us -> 24.4 us
  blocking collectives: 97 us -> 99.5 us
    all_to_all x1, waiting for transfers between devices: 15.7 us -> 7.26 us  [local(): states = lax.all_to_all(states, ('y', 'x'), 0, 0, tiled=True)]
    all_gather x0 -> x1, blocking collectives: none -> 3.23 us  [local(): pair = lax.all_gather(state, 'c')]
    ppermute x1, waiting for transfers between devices: 0.33 us -> 3.21 us  [local(): lax.ppermute(tile, SEQ, [(n, (n + 1) % blocks) for n in range(blocks)])]
    ppermute x1, starting transfers between devices: 4.62 us -> 2.04 us  [local(): lax.ppermute(tile, SEQ, [(n, (n + 1) % blocks) for n in range(blocks)])]
    unnamed x18 -> x6, local copies, waits for them, and re-layouts: 3.76 us -> 1.45 us
    broadcast_in_dim x1 -> x0, local copies, waits for them, and re-layouts: 1.95 us -> none  [local(): jnp.broadcast_to(state, (blocks, *state.shape))]
    pallas_call x3 -> x4, Pallas kernels: 12.2 us -> 13.3 us  [call(): pl.pallas_call(kernel, out_shape=[jax.ShapeDtypeStruct(s, t) for s, t in...]
  transfers between devices with their start and end apart: 4 -> 4, of which waited for: 2 -> 2; matrix products, arithmetic and copies ran while one was open for 4% -> 3% of each run, Pallas kernels for 3% -> 1%
where the time goes in v3:
time: 169 us; the launch traced here: 168 us
  blocking collectives  99.5 us (59%)
  starting transfers between devices  24.4 us (14%)
  between operations  13.5 us (8%)
  Pallas kernels  13.3 us (8%)
  waiting for transfers between devices  10.5 us (6%)
  other arithmetic  4.67 us (3%)
  local copies, waits for them, and re-layouts  2.13 us (1%)
    all_to_all x1, blocking collectives, local(): part = lax.all_to_all(part, 'hid', 0, 0, tiled=True)  56.2 us
    all_gather x1, blocking collectives, local(): main = lax.all_gather(main, 'hid')  40 us
    pallas_call x4, Pallas kernels, call(): pl.pallas_call(kernel, out_shape=[jax.ShapeDtypeStruct(s, t) for s, t in...  13.3 us
    all_to_all x1, starting transfers between devices, local(): lax.all_to_all(jnp.broadcast_to(side, (groups, *side.shape)), 'hid', 0, 0...  13.1 us
    all_to_all x1, starting transfers between devices, local(): states = lax.all_to_all(states, ('y', 'x'), 0, 0, tiled=True)  9.22 us
    all_to_all x1, waiting for transfers between devices, local(): states = lax.all_to_all(states, ('y', 'x'), 0, 0, tiled=True)  7.26 us
  transfers between devices with their start and end apart: 4, of which 2 were waited for; matrix products, arithmetic and copies ran while one was open for 3% of the time, Pallas kernels for 1%

profile of v3, /device:TPU:6, one launch (start us, length us, event | category | flops | bytes accessed | tf_op | source)
XLA Modules:
  0.0 167.9 jit_solution(15134099049439497374)
XLA Ops:
  6.5 0.0 all-gather.4.cloned.1.call-start
  6.5 2.5 %shard_map.136 = (f32[128,256]{1,0:T(8,128)}, bf16[128,256]{1,0:T(8,128)(2,1)}, bf16[72,256]{1,0:T(8,128)(2,1)}) custom-call(bf16[128,256]{1,0:T(8,128)(2,1)} %r_ref.1, bf16[128,256]{1,0:T(8,128)(2,1)} %k_ref.1, bf16[128,256]{1,0:T(8,128)(2,1)} %v_ref.1, f32[128,256]{1,0:T(8,128)} %logit_ref.1, f32[4,64]{1,0:T(4,128)} %boost_ref.1), custom_call_target="tpu_custom_call" | custom-call | tf_op jit(solution)/shard_map/pallas_call | solution.py:207
  9.1 3.2 %all-gather = bf16[144,256]{1,0:T(8,128)(2,1)} all-gather(bf16[72,256]{1,0:T(8,128)(2,1)} %get-tuple-element.14), channel_id=2, replica_groups=mesh['y'=4,'x'=4,'c'=2,'hid'=16] {'c'}, dimensions={0}, use_global_device_ids=true | all-gather | bytes 110592 | tf_op jit(solution)/shard_map/all_gather | solution.py:231
  12.3 1.9 %shard_map.137 = (bf16[16,72,256]{2,1,0:T(8,128)(2,1)}, bf16[896,128]{1,0:T(8,128)(2,1)}) custom-call(bf16[2,72,256]{2,1,0:T(8,128)(2,1)} %bitcast.15, bf16[448,128]{1,0:T(8,128)(2,1)} %bitcast.17, bf16[448,128]{1,0:T(8,128)(2,1)} %bitcast.18), custom_call_target="tpu_custom_call" | custom-call | tf_op jit(solution)/shard_map/pallas_call | solution.py:207
  14.2 0.0 all-gather.4.cloned.1.call-update
  14.2 9.2 %all-to-all-start = ((bf16[16,72,256]{2,1,0:T(8,128)(2,1)}), bf16[16,72,256]{2,1,0:T(8,128)(2,1)S(1)}, u32[]{:S(2)}, u32[]{:S(2)}) async-start(bf16[16,72,256]{2,1,0:T(8,128)(2,1)} %get-tuple-element.15), calls=%async_computation | async-start | bytes 1179648 | tf_op jit(solution)/shard_map/all_to_all | solution.py:238
  23.4 0.6 pad_add_fusion.at_ref
  24.0 1.3 pad_maximum_fusion.2.gn_ref
  25.3 1.3 pad_maximum_fusion.1.ln_ref
  26.6 7.3 %all-to-all-done.all_ref = bf16[16,72,256]{2,1,0:T(8,128)(2,1)S(1)} async-done(((bf16[16,72,256]{2,1,0:T(8,128)(2,1)}), bf16[16,72,256]{2,1,0:T(8,128)(2,1)S(1)}, u32[]{:S(2)}, u32[]{:S(2)}) %all-to-all-start) | async-done | bytes 589856 | tf_op jit(solution)/shard_map/all_to_all | solution.py:238
  33.9 0.0 copy-start
  33.9 0.8 copy-done
  34.7 2.4 %shard_map.138 = (f32[128,256]{1,0:T(8,128)}, bf16[120,256]{1,0:T(8,128)(2,1)}, bf16[8,256]{1,0:T(8,128)(2,1)}, bf16[8,256]{1,0:T(8,128)(2,1)}) custom-call(s32[2]{0:T(128)} %pad_add_fusion.at_ref, bf16[16,72,256]{2,1,0:T(8,128)(2,1)} %copy-done, bf16[2,72,256]{2,1,0:T(8,128)(2,1)} %bitcast.16, f32[128,256]{1,0:T(8,128)} %get-tuple-element.16.own_ref, ...), custom_call_target="tpu_custom_call" | custom-call | tf_op jit(solution)/shard_map/pallas_call | solution.py:207
  37.1 0.0 copy-start.2
  37.1 2.0 %collective-permute-start = (bf16[8,256]{1,0:T(8,128)(2,1)}, bf16[8,256]{1,0:T(8,128)(2,1)S(1)}, u32[]{:S(2)}, u32[]{:S(2)}) collective-permute-start(bf16[8,256]{1,0:T(8,128)(2,1)} %get-tuple-element.21), channel_id=1, source_target_pairs={{0,16},{16,32},{32,48},{48,64},{64,80},{80,96},{96,112},{112,128},... | collective-permute-start | bytes 12296 | tf_op jit(solution)/shard_map/ppermute | solution.py:247
  39.1 3.2 %collective-permute-done = bf16[8,256]{1,0:T(8,128)(2,1)S(1)} collective-permute-done((bf16[8,256]{1,0:T(8,128)(2,1)}, bf16[8,256]{1,0:T(8,128)(2,1)S(1)}, u32[]{:S(2)}, u32[]{:S(2)}) %collective-permute-start) | collective-permute-done | bytes 4128 | tf_op jit(solution)/shard_map/ppermute | solution.py:247
  42.4 0.7 pad_maximum_fusion
  43.0 0.7 broadcast_in_dim.3
  43.7 13.1 %all-to-all-start.1 = ((bf16[16,2,8,256]{3,2,1,0:T(8,128)(2,1)}), bf16[16,2,8,256]{3,2,1,0:T(8,128)(2,1)S(1)}, u32[]{:S(2)}, u32[]{:S(2)}) async-start(bf16[16,2,8,256]{3,2,1,0:T(8,128)(2,1)} %broadcast_in_dim.3), calls=%async_computation.1 | async-start | bytes 262144 | tf_op jit(solution)/shard_map/all_to_all | solution.py:249
  56.9 40.0 %all-gather.1 = bf16[1920,256]{1,0:T(8,128)(2,1)} all-gather(bf16[120,256]{1,0:T(8,128)(2,1)} %get-tuple-element.19), channel_id=3, replica_groups=mesh['y'=4,'x'=4,'c'=2,'hid'=16] {'hid'}, dimensions={0}, use_global_device_ids=true | all-gather | bytes 1044480 | tf_op jit(solution)/shard_map/all_gather | solution.py:252
  96.9 0.0 all-to-all-done.1.side_ref
  96.9 0.0 copy-start.1
  96.9 0.0 all-gather.4.cloned.1.call-done.w_hbm
  96.9 0.6 copy-done.1
  97.5 6.5 %shard_map.139 = bf16[16,128,256]{2,1,0:T(8,128)(2,1)} custom-call(s32[1]{0:T(128)} %bitcast.10.at_ref, bf16[16,120,256]{2,1,0:T(8,128)(2,1)} %bitcast.14, bf16[16,2,8,256]{3,2,1,0:T(8,128)(2,1)} %copy-done.1, bf16[28672,128]{1,0:T(8,128)(2,1)} %all-gather.4.cloned.1.call-done.w_hbm), custom_call_target="tpu_custom_call" | custom-call | tf_op jit(solution)/shard_map/pallas_call | solution.py:207
  104.0 56.2 %all_to_all.15 = bf16[16,128,256]{2,1,0:T(8,128)(2,1)S(1)} all-to-all(bf16[16,128,256]{2,1,0:T(8,128)(2,1)} %shard_map.139), channel_id=1, replica_groups=mesh['y'=4,'x'=4,'c'=2,'hid'=16] {'hid'}, dimensions={0} | all-to-all | bytes 2097152 | tf_op jit(solution)/shard_map/all_to_all | solution.py:260
  160.2 0.1 convert_reduce_fusion
  160.4 0.0 copy-done.2
  160.4 0.6 add_convert_fusion
Async XLA Ops:
  6.5 90.3 %all-gather.4.cloned.1.call-start = ((), (), s32[]{:S(2)}) async-start(), calls=%async_computation.3 | async-start | bytes 7569408 | tf_op jit(solution)/shard_map/all_gather | solution.py:237
  14.2 19.7 %all-to-all-start = ((bf16[16,72,256]{2,1,0:T(8,128)(2,1)}), bf16[16,72,256]{2,1,0:T(8,128)(2,1)S(1)}, u32[]{:S(2)}, u32[]{:S(2)}) async-start(bf16[16,72,256]{2,1,0:T(8,128)(2,1)} %get-tuple-element.15), calls=%async_computation | async-start | bytes 1179648 | tf_op jit(solution)/shard_map/all_to_all | solution.py:238
  33.9 0.8 copy-start
  37.1 123.3 %copy-start.2 = (f32[128,256]{1,0:T(8,128)S(1)}, f32[128,256]{1,0:T(8,128)}, u32[]{:S(2)}) copy-start(f32[128,256]{1,0:T(8,128)} %get-tuple-element.18) | copy-start | bytes 393220
  37.1 5.3 %collective-permute-start = (bf16[8,256]{1,0:T(8,128)(2,1)}, bf16[8,256]{1,0:T(8,128)(2,1)S(1)}, u32[]{:S(2)}, u32[]{:S(2)}) collective-permute-start(bf16[8,256]{1,0:T(8,128)(2,1)} %get-tuple-element.21), channel_id=1, source_target_pairs={{0,16},{16,32},{32,48},{48,64},{64,80},{80,96},{96,112},{112,128},... | collective-permute-start | bytes 12296 | tf_op jit(solution)/shard_map/ppermute | solution.py:247
  43.7 53.1 %all-to-all-start.1 = ((bf16[16,2,8,256]{3,2,1,0:T(8,128)(2,1)}), bf16[16,2,8,256]{3,2,1,0:T(8,128)(2,1)S(1)}, u32[]{:S(2)}, u32[]{:S(2)}) async-start(bf16[16,2,8,256]{3,2,1,0:T(8,128)(2,1)} %broadcast_in_dim.3), calls=%async_computation.1 | async-start | bytes 262144 | tf_op jit(solution)/shard_map/all_to_all | solution.py:249
  96.9 0.6 copy-start.1
Sparse Core Ops, SparseCore 0:
  14.3 69.9 all-gather.3

commit v4 on v3

--- a/solution.py
+++ b/solution.py
@@ -31,7 +31,14 @@
     return hi, (x - hi.astype(F32)).astype(BF16)
 
 
-def wkv_kernel(r_ref, k_ref, v_ref, logit_ref, boost_ref, own_ref, rec_ref, pay_ref):
+def last_row(ref):
+    rows = ref.shape[0]
+    return ref[rows - 16 : rows, :].astype(F32)[15:16]
+
+
+def wkv_kernel(
+    r_ref, k_ref, v_ref, logit_ref, boost_ref, skip_ref, gate_ref, own_ref, rec_ref, pay_ref, row_ref
+):
     rows, width = r_ref.shape
     logw = -jnp.exp(logit_ref[...])
     lower = (iota((rows, rows), 0) >= iota((rows, rows), 1)).astype(BF16)
@@ -79,9 +86,20 @@
     pay_ref[64:72, :] = jnp.where(
         line == 0, hi.astype(F32), jnp.where(line == 1, lo.astype(F32), 0.0)
     ).astype(BF16)
-
-
-def pair_kernel(pair_ref, wk_ref, wv_ref, out_ref, w_ref):
+    tail = jnp.where(line == 0, last_row(own_ref), 0.0)
+    tail = jnp.where(line == 1, last_row(rec_ref), tail)
+    tail = jnp.where(line == 2, last_row(skip_ref), tail)
+    row_ref[...] = jnp.where(line == 3, last_row(gate_ref), tail)
+
+
+def apart(state, at):
+    left = iota((64, 128), 1) < 64
+    here = state[:, at]
+    both = [jnp.where(left, here, 0.0), jnp.where(left, 0.0, here)]
+    return jnp.concatenate(both, axis=0).astype(BF16)
+
+
+def pair_kernel(at_ref, pair_ref, row_ref, wk_ref, wv_ref, out_ref, send_ref, w_ref):
     units = wk_ref.shape[0]
     w_ref[0:units] = wk_ref[...]
     w_ref[units:] = wv_ref[...]
@@ -94,11 +112,20 @@
     for n in range(out_ref.shape[0]):
         out_ref[n, 0:64] = state
         out_ref[n, 64:72] = tail
+    second = at_ref[1] > 0
+    row = row_ref[...]
+    for p in range(a.shape[1] // 128):
+        at = slice(128 * p, 128 * p + 128)
+        recall = row[1:2, at]
+        more = dot(jnp.broadcast_to(recall, (8, 128)).astype(BF16), apart(a[0:64], at), NT)
+        fade = recall * (jnp.exp(a[64:65, at] + a[65:66, at]) - 1.0)
+        more = jnp.where(line[:, at] == 0, more, jnp.where(line[:, at] == 1, fade, 0.0))
+        send_ref[:, at] = row[:, at] + jnp.where(second, more, 0.0)
 
 
 def middle_kernel(
-    at_ref, all_ref, pair_ref, own_ref, rec_ref, skip_ref, gate_ref, gn_ref, ln_ref,
-    mid_ref, main_ref, edge_ref, tile_ref,
+    at_ref, all_ref, pair_ref, prior_ref, own_ref, rec_ref, skip_ref, gate_ref, gn_ref, ln_ref,
+    mid_ref, main_ref, side_ref,
 ):
     rows, width = own_ref.shape
     main = main_ref.shape[0]
@@ -110,38 +137,44 @@
 
         return step
 
-    state = lax.fori_loop(0, at_ref[0], join(all_ref), jnp.zeros((64, width), F32))
-    state = lax.fori_loop(0, at_ref[1], join(pair_ref), state)
-    left64 = iota((64, 128), 1) < 64
-    left = iota((rows, 128), 1) < 64
-
-    def mean(x):
-        a = jnp.sum(jnp.where(left, x, 0.0), axis=1, keepdims=True)
-        b = jnp.sum(jnp.where(left, 0.0, x), axis=1, keepdims=True)
-        return jnp.where(left, a, b) * (1.0 / 64)
-
-    for p in range(width // 128):
-        at = slice(128 * p, 128 * p + 128)
-        here = state[:, at]
-        both = jnp.concatenate(
-            [jnp.where(left64, here, 0.0), jnp.where(left64, 0.0, here)], axis=0
-        ).astype(BF16)
-        wkv = own_ref[:, at] + dot(rec_ref[:, at], both, NT)
+    chip, core = at_ref[0], at_ref[1]
+    split = jnp.maximum(chip + core - 1, 0)
+    old = lax.fori_loop(0, split, join(all_ref), jnp.zeros((64, width), F32))
+    state = lax.fori_loop(split, chip, join(all_ref), old)
+    state = lax.fori_loop(0, core, join(pair_ref), state)
+
+    def finish(own, recall, skip, gate, before, at):
+        left = iota(own.shape, 1) < 64
+
+        def mean(x):
+            a = jnp.sum(jnp.where(left, x, 0.0), axis=1, keepdims=True)
+            b = jnp.sum(jnp.where(left, 0.0, x), axis=1, keepdims=True)
+            return jnp.where(left, a, b) * (1.0 / 64)
+
+        wkv = own + dot(recall, apart(before, at), NT)
         centre = wkv - mean(wkv)
         normed = centre * lax.rsqrt(mean(centre * centre) + EPS_GROUP)
         normed = normed * gn_ref[0:1, at] + gn_ref[1:2, at]
-        gate = gate_ref[:, at].astype(F32)
-        middle = skip_ref[:, at].astype(F32) + normed * (gate / (1.0 + jnp.exp(-gate)))
+        return skip + normed * (gate / (1.0 + jnp.exp(-gate)))
+
+    line = iota((8, 128), 0)
+    for p in range(width // 128):
+        at = slice(128 * p, 128 * p + 128)
+        middle = finish(
+            own_ref[:, at], rec_ref[:, at], skip_ref[:, at].astype(F32), gate_ref[:, at].astype(F32), state, at
+        )
         mid_ref[:, at] = middle
         main_ref[:, at] = middle[0:main].astype(BF16)
-        edge_ref[:, at] = middle[main:].astype(BF16)
-    line = iota((8, width), 0)
-    tail = jnp.where(line == 0, mid_ref[rows - 1 : rows, :], 0.0)
-    for n in range(3):
-        hi, lo = hi_lo(ln_ref[n : n + 1])
-        tail = jnp.where(line == 2 * n + 1, hi.astype(F32), tail)
-        tail = jnp.where(line == 2 * n + 2, lo.astype(F32), tail)
-    tile_ref[...] = tail.astype(BF16)
+        own, recall, skip, gate = (jnp.broadcast_to(prior_ref[n : n + 1, at], (8, 128)) for n in range(4))
+        tail = jnp.where(line == 0, finish(own, recall.astype(BF16), skip, gate, old, at), 0.0)
+        for n in range(3):
+            hi, lo = hi_lo(ln_ref[n : n + 1, at])
+            tail = jnp.where(line == 2 * n + 1, hi.astype(F32), tail)
+            tail = jnp.where(line == 2 * n + 2, lo.astype(F32), tail)
+        edge, tail = middle[main:].astype(BF16), tail.astype(BF16)
+        for g in range(side_ref.shape[0]):
+            side_ref[g, 0, :, at] = edge
+            side_ref[g, 1, :, at] = tail
 
 
 def ffn_kernel(at_ref, main_ref, side_ref, w_hbm, out_ref, w_ref, sems):
@@ -223,32 +256,30 @@
 
         core = lax.axis_index("c")
         chips = blocks // lax.axis_size("c")
-        own, recall, state = call(
+        at = jnp.stack([lax.axis_index(("y", "x")), core])
+        own, recall, state, row = call(
             wkv_kernel,
-            [((rows, width), F32), ((rows, width), BF16), ((72, width), BF16)],
-            recept, keys, values, logit, boost,
+            [((rows, width), F32), ((rows, width), BF16), ((72, width), BF16), ((8, width), F32)],
+            recept, keys, values, logit, boost, skip, gating,
         )
         pair = lax.all_gather(state, "c")
-        states, weights = call(
+        states, row, weights = call(
             pair_kernel,
-            [((chips, 72, width), BF16), ((2 * wk.shape[1], wk.shape[0]), BF16)],
-            pair, wk.T, wv.T,
+            [((chips, 72, width), BF16), ((8, width), F32), ((2 * wk.shape[1], wk.shape[0]), BF16)],
+            at, pair, row, wk.T, wv.T,
+            in_specs=[SMEM()] + [VMEM()] * 4,
         )
         weights = lax.all_gather(weights, SEQ, tiled=True)
         states = lax.all_to_all(states, ("y", "x"), 0, 0, tiled=True)
-        middle, main, edge, tile = call(
+        prior = lax.ppermute(row, SEQ, [(n, n + 1) for n in range(blocks - 1)])
+        middle, main, side = call(
             middle_kernel,
-            [((rows, width), F32), ((rows - 8, width), BF16), ((8, width), BF16), ((8, width), BF16)],
-            jnp.stack([lax.axis_index(("y", "x")), core]),
-            states, pair, own, recall, skip, gating,
+            [((rows, width), F32), ((rows - 8, width), BF16), ((groups, 2, 8, width), BF16)],
+            at, states, pair, prior, own, recall, skip, gating,
             jnp.stack([gn_gain, gn_bias]), jnp.stack([ln_gain, ln_bias, blend]),
-            in_specs=[SMEM()] + [VMEM()] * 8,
-        )
-        tile = lax.ppermute(tile, SEQ, [(n, (n + 1) % blocks) for n in range(blocks)])
-        side = jnp.stack([edge, tile])
-        side = lax.all_to_all(
-            jnp.broadcast_to(side, (groups, *side.shape)), "hid", 0, 0, tiled=True
-        )
+            in_specs=[SMEM()] + [VMEM()] * 9,
+        )
+        side = lax.all_to_all(side, "hid", 0, 0, tiled=True)
         main = lax.all_gather(main, "hid")
         (part,) = call(
             ffn_kernel,

time: 169 us -> 165 us (0.976)
  waiting for transfers between devices: 10.5 us -> 5.92 us
    all_to_all x1, waiting for transfers between devices: 7.26 us -> 2.57 us  [local(): states = lax.all_to_all(states, ('y', 'x'), 0, 0, tiled=True)]
  transfers between devices with their start and end apart: 4 -> 4, of which waited for: 2 -> 2; matrix products, arithmetic and copies ran while one was open for 3% -> 2% of each run, Pallas kernels for 1% -> 2%
where the time goes in v4:
time: 165 us; the launch traced here: 163 us
  blocking collectives  100 us (61%)
  starting transfers between devices  24.4 us (15%)
  Pallas kernels  13.5 us (8%)
  between operations  13.5 us (8%)
  waiting for transfers between devices  5.92 us (4%)
  other arithmetic  3.98 us (2%)
    all_to_all x1, blocking collectives, local(): part = lax.all_to_all(part, 'hid', 0, 0, tiled=True)  57.1 us
    all_gather x1, blocking collectives, local(): main = lax.all_gather(main, 'hid')  40.1 us
    pallas_call x4, Pallas kernels, call(): pl.pallas_call(kernel, out_shape=[jax.ShapeDtypeStruct(s, t) for s, t in...  13.5 us
    all_to_all x1, starting transfers between devices, local(): side = lax.all_to_all(side, 'hid', 0, 0, tiled=True)  13.2 us
    all_to_all x1, starting transfers between devices, local(): states = lax.all_to_all(states, ('y', 'x'), 0, 0, tiled=True)  9.22 us
    ppermute x1, waiting for transfers between devices, local(): prior = lax.ppermute(row, SEQ, [(n, n + 1) for n in range(blocks - 1)])  3.32 us
  transfers between devices with their start and end apart: 4, of which 2 were waited for; matrix products, arithmetic and copies ran while one was open for 2% of the time, Pallas kernels for 2%

profile of v4, /device:TPU:6, one launch (start us, length us, event | category | flops | bytes accessed | tf_op | source)
XLA Modules:
  0.0 163.2 jit_solution(8546043802517926201)
XLA Ops:
  6.5 0.0 all-gather.4.cloned.1.call-start
  6.5 2.6 %shard_map.136 = (f32[128,256]{1,0:T(8,128)}, bf16[128,256]{1,0:T(8,128)(2,1)}, bf16[72,256]{1,0:T(8,128)(2,1)}, f32[8,256]{1,0:T(8,128)}) custom-call(bf16[128,256]{1,0:T(8,128)(2,1)} %r_ref.1, bf16[128,256]{1,0:T(8,128)(2,1)} %k_ref.1, bf16[128,256]{1,0:T(8,128)(2,1)} %v_ref.1, f32[128,256]{1,0:T(8,128)} %logit_ref.1, f32[4,64]{1,0:T(4,128)} %boost_ref.1, ...), custom_call_target="tpu_custom_call" | custom-call | tf_op jit(solution)/shard_map/pallas_call | solution.py:240
  9.1 3.2 %all-gather = bf16[144,256]{1,0:T(8,128)(2,1)} all-gather(bf16[72,256]{1,0:T(8,128)(2,1)} %get-tuple-element.15), channel_id=2, replica_groups=mesh['y'=4,'x'=4,'c'=2,'hid'=16] {'c'}, dimensions={0}, use_global_device_ids=true | all-gather | bytes 110592 | tf_op jit(solution)/shard_map/all_gather | solution.py:265
  12.4 0.6 pad_add_fusion.at_ref
  13.0 2.0 %shard_map.137 = (bf16[16,72,256]{2,1,0:T(8,128)(2,1)}, f32[8,256]{1,0:T(8,128)}, bf16[896,128]{1,0:T(8,128)(2,1)}) custom-call(s32[2]{0:T(128)} %pad_add_fusion.at_ref, bf16[2,72,256]{2,1,0:T(8,128)(2,1)} %bitcast.13, f32[8,256]{1,0:T(8,128)} %get-tuple-element.16.row_ref, bf16[448,128]{1,0:T(8,128)(2,1)} %bitcast.15, bf16[448,128]{1,0:T(8,128)(2,1)} %bitcast.16), custom_call_target="tpu_custom_call" | custom-call | tf_op jit(solution)/shard_map/pallas_call | solution.py:240
  15.0 0.0 all-gather.4.cloned.1.call-update
  15.0 9.2 %all-to-all-start = ((bf16[16,72,256]{2,1,0:T(8,128)(2,1)}), bf16[16,72,256]{2,1,0:T(8,128)(2,1)S(1)}, u32[]{:S(2)}, u32[]{:S(2)}) async-start(bf16[16,72,256]{2,1,0:T(8,128)(2,1)} %get-tuple-element.17), calls=%async_computation | async-start | bytes 1179648 | tf_op jit(solution)/shard_map/all_to_all | solution.py:273
  24.2 2.0 %collective-permute-start = (f32[8,256]{1,0:T(8,128)}, f32[8,256]{1,0:T(8,128)S(1)}, u32[]{:S(2)}, u32[]{:S(2)}) collective-permute-start(f32[8,256]{1,0:T(8,128)} %get-tuple-element.18), channel_id=1, source_target_pairs={{0,16},{16,32},{32,48},{48,64},{64,80},{80,96},{96,112},{112,128},... | collective-permute-start | bytes 24584 | tf_op jit(solution)/shard_map/ppermute | solution.py:274
  26.2 1.3 pad_maximum_fusion.ln_ref
  27.5 1.3 pad_maximum_fusion.1.gn_ref
  28.8 3.3 %collective-permute-done.prior_ref = f32[8,256]{1,0:T(8,128)S(1)} collective-permute-done((f32[8,256]{1,0:T(8,128)}, f32[8,256]{1,0:T(8,128)S(1)}, u32[]{:S(2)}, u32[]{:S(2)}) %collective-permute-start) | collective-permute-done | bytes 8224 | tf_op jit(solution)/shard_map/ppermute | solution.py:274
  32.1 0.0 copy-start.3
  32.1 2.6 %all-to-all-done.all_ref = bf16[16,72,256]{2,1,0:T(8,128)(2,1)S(1)} async-done(((bf16[16,72,256]{2,1,0:T(8,128)(2,1)}), bf16[16,72,256]{2,1,0:T(8,128)(2,1)S(1)}, u32[]{:S(2)}, u32[]{:S(2)}) %all-to-all-start) | async-done | bytes 589856 | tf_op jit(solution)/shard_map/all_to_all | solution.py:273
  34.7 0.0 copy-start
  34.7 0.0 copy-done.3
  34.7 0.8 copy-done
  35.5 2.5 %shard_map.138 = (f32[128,256]{1,0:T(8,128)}, bf16[120,256]{1,0:T(8,128)(2,1)}, bf16[16,2,8,256]{3,2,1,0:T(8,128)(2,1)}) custom-call(s32[2]{0:T(128)} %pad_add_fusion.at_ref, bf16[16,72,256]{2,1,0:T(8,128)(2,1)} %copy-done, bf16[2,72,256]{2,1,0:T(8,128)(2,1)} %bitcast.14, f32[8,256]{1,0:T(8,128)} %copy-done.3, f32[128,256]{1,0:T(8,128)} %get-tuple-element.19.own_ref, ...), custom_call_target="tpu_custom_call" | custom-call | tf_op jit(solution)/shard_map/pallas_call | solution.py:240
  38.0 0.0 copy-start.2
  38.0 13.2 %all-to-all-start.1 = ((bf16[16,2,8,256]{3,2,1,0:T(8,128)(2,1)}), bf16[16,2,8,256]{3,2,1,0:T(8,128)(2,1)S(1)}, u32[]{:S(2)}, u32[]{:S(2)}) async-start(bf16[16,2,8,256]{3,2,1,0:T(8,128)(2,1)} %get-tuple-element.23), calls=%async_computation.1 | async-start | bytes 262144 | tf_op jit(solution)/shard_map/all_to_all | solution.py:282
  51.2 40.1 %all-gather.1 = bf16[1920,256]{1,0:T(8,128)(2,1)} all-gather(bf16[120,256]{1,0:T(8,128)(2,1)} %get-tuple-element.22), channel_id=3, replica_groups=mesh['y'=4,'x'=4,'c'=2,'hid'=16] {'hid'}, dimensions={0}, use_global_device_ids=true | all-gather | bytes 1044480 | tf_op jit(solution)/shard_map/all_gather | solution.py:283
  91.3 0.0 all-to-all-done.1.side_ref
  91.4 0.0 copy-start.1
  91.4 0.0 all-gather.4.cloned.1.call-done.w_hbm
  91.4 0.6 copy-done.1
  92.0 6.5 %shard_map.139 = bf16[16,128,256]{2,1,0:T(8,128)(2,1)} custom-call(s32[1]{0:T(128)} %bitcast.10.at_ref, bf16[16,120,256]{2,1,0:T(8,128)(2,1)} %bitcast.12, bf16[16,2,8,256]{3,2,1,0:T(8,128)(2,1)} %copy-done.1, bf16[28672,128]{1,0:T(8,128)(2,1)} %all-gather.4.cloned.1.call-done.w_hbm), custom_call_target="tpu_custom_call" | custom-call | tf_op jit(solution)/shard_map/pallas_call | solution.py:240
  98.5 57.1 %all_to_all.15 = bf16[16,128,256]{2,1,0:T(8,128)(2,1)S(1)} all-to-all(bf16[16,128,256]{2,1,0:T(8,128)(2,1)} %shard_map.139), channel_id=1, replica_groups=mesh['y'=4,'x'=4,'c'=2,'hid'=16] {'hid'}, dimensions={0} | all-to-all | bytes 2097152 | tf_op jit(solution)/shard_map/all_to_all | solution.py:291
  155.6 0.1 convert_reduce_fusion
  155.7 0.0 copy-done.2
  155.8 0.6 add_convert_fusion
Async XLA Ops:
  6.5 84.8 %all-gather.4.cloned.1.call-start = ((), (), s32[]{:S(2)}) async-start(), calls=%async_computation.3 | async-start | bytes 7569408 | tf_op jit(solution)/shard_map/all_gather | solution.py:272
  15.0 19.7 %all-to-all-start = ((bf16[16,72,256]{2,1,0:T(8,128)(2,1)}), bf16[16,72,256]{2,1,0:T(8,128)(2,1)S(1)}, u32[]{:S(2)}, u32[]{:S(2)}) async-start(bf16[16,72,256]{2,1,0:T(8,128)(2,1)} %get-tuple-element.17), calls=%async_computation | async-start | bytes 1179648 | tf_op jit(solution)/shard_map/all_to_all | solution.py:273
  24.2 7.9 %collective-permute-start = (f32[8,256]{1,0:T(8,128)}, f32[8,256]{1,0:T(8,128)S(1)}, u32[]{:S(2)}, u32[]{:S(2)}) collective-permute-start(f32[8,256]{1,0:T(8,128)} %get-tuple-element.18), channel_id=1, source_target_pairs={{0,16},{16,32},{32,48},{48,64},{64,80},{80,96},{96,112},{112,128},... | collective-permute-start | bytes 24584 | tf_op jit(solution)/shard_map/ppermute | solution.py:274
  32.1 2.6 %copy-start.3 = (f32[8,256]{1,0:T(8,128)}, f32[8,256]{1,0:T(8,128)S(1)}, u32[]{:S(2)}) copy-start(f32[8,256]{1,0:T(8,128)S(1)} %collective-permute-done.prior_ref) | copy-start | bytes 24580
  34.7 0.8 copy-start
  38.0 117.8 %copy-start.2 = (f32[128,256]{1,0:T(8,128)S(1)}, f32[128,256]{1,0:T(8,128)}, u32[]{:S(2)}) copy-start(f32[128,256]{1,0:T(8,128)} %get-tuple-element.21) | copy-start | bytes 393220
  38.0 53.4 %all-to-all-start.1 = ((bf16[16,2,8,256]{3,2,1,0:T(8,128)(2,1)}), bf16[16,2,8,256]{3,2,1,0:T(8,128)(2,1)S(1)}, u32[]{:S(2)}, u32[]{:S(2)}) async-start(bf16[16,2,8,256]{3,2,1,0:T(8,128)(2,1)} %get-tuple-element.23), calls=%async_computation.1 | async-start | bytes 262144 | tf_op jit(solution)/shard_map/all_to_all | solution.py:282
  91.4 0.7 copy-start.1
Sparse Core Ops, SparseCore 0:
  15.1 69.9 all-gather.3

commit v5 on v4

--- a/solution.py
+++ b/solution.py
@@ -9,6 +9,7 @@
 from jax.sharding import PartitionSpec as P
 
 SEQ = ("y", "x", "c")
+HID = ("zl", "zh")
 EPS_GROUP = 0.00064
 EPS_LAYER = 1e-05
 F32 = jnp.float32
@@ -177,9 +178,9 @@
             side_ref[g, 1, :, at] = tail
 
 
-def ffn_kernel(at_ref, main_ref, side_ref, w_hbm, out_ref, w_ref, sems):
-    groups, rows, width = out_ref.shape
-    main = main_ref.shape[1]
+def ffn_kernel(at_ref, main_ref, side_ref, w_hbm, give_ref, hidden_ref, w_ref, sems):
+    _, rows, width = give_ref.shape
+    groups, main = main_ref.shape[0:2]
     full = groups * width
     depth = w_hbm.shape[1]
     tall = w_hbm.shape[0] // (full // depth)
@@ -192,8 +193,10 @@
         return pltpu.make_async_copy(w_hbm.at[at], w_ref.at[at], sems.at[q])
 
     def weights(g, first):
-        blocks = range(g * width // depth, (g + 1) * width // depth)
-        return jnp.concatenate([w_ref[b * tall + first : b * tall + first + units] for b in blocks], axis=1)
+        starts = [(g * (width // depth) + b) * tall + first for b in range(width // depth)]
+        if not isinstance(g, int):
+            starts = [pl.multiple_of(start, 64) for start in starts]
+        return jnp.concatenate([w_ref[pl.ds(start, units)] for start in starts], axis=1)
 
     for q in range(chunks):
         copy(q).start()
@@ -227,8 +230,31 @@
             copy(g * width // step).wait()
         acc = acc + dot(xk, weights(g, 0), NT)
     hidden = jnp.square(jnp.maximum(acc, 0.0)).astype(BF16)
+    hidden_ref[...] = hidden
+    for g in range(groups // 2):
+        give_ref[g] = dot(hidden, weights(2 * g + 1 - at_ref[1], units), NN).astype(BF16)
+
+
+def keep_kernel(at_ref, hidden_ref, w_hbm, keep_ref, w_ref, sems):
+    groups, rows, width = keep_ref.shape
+    units = hidden_ref.shape[1]
+    depth = w_hbm.shape[1]
+    each = width // depth
+
+    def copy(g, b):
+        start = (((2 * g + at_ref[1]) * each + b) * 2 + 1) * units
+        return pltpu.make_async_copy(
+            w_hbm.at[pl.ds(pl.multiple_of(start, 64), units)], w_ref.at[g * each + b], sems.at[g * each + b]
+        )
+
     for g in range(groups):
-        out_ref[g] = dot(hidden, weights(g, units), NN).astype(BF16)
+        for b in range(each):
+            copy(g, b).start()
+    for g in range(groups):
+        for b in range(each):
+            copy(g, b).wait()
+        w = jnp.concatenate([w_ref[g * each + b] for b in range(each)], axis=1)
+        keep_ref[g] = dot(hidden_ref[...], w, NN).astype(BF16)
 
 
 VMEM = functools.partial(pl.BlockSpec, memory_space=pltpu.VMEM)
@@ -250,9 +276,9 @@
         skip, recept, keys, values, gating, logit, boost, gn_gain, gn_bias, ln_gain, ln_bias, blend, wk, wv
     ):
         rows, width = skip.shape
-        groups = lax.axis_size("hid")
+        groups = lax.axis_size(HID)
         blocks = lax.axis_size(SEQ)
-        at_seq = lax.axis_index(SEQ).reshape(1)
+        at_seq = lax.axis_index(SEQ)
 
         core = lax.axis_index("c")
         chips = blocks // lax.axis_size("c")
@@ -279,31 +305,43 @@
             jnp.stack([gn_gain, gn_bias]), jnp.stack([ln_gain, ln_bias, blend]),
             in_specs=[SMEM()] + [VMEM()] * 9,
         )
-        side = lax.all_to_all(side, "hid", 0, 0, tiled=True)
-        main = lax.all_gather(main, "hid")
-        (part,) = call(
+        side = lax.all_to_all(side, HID, 0, 0, tiled=True)
+        main = lax.all_gather(main, HID)
+        at = jnp.stack([at_seq, lax.axis_index("zh")])
+        any_space = pl.BlockSpec(memory_space=pl.ANY)
+        units, depth = wk.shape[1], wk.shape[0]
+        give, hidden = call(
             ffn_kernel,
-            [((groups, rows, width), BF16)],
-            at_seq, main, side, weights,
-            in_specs=[SMEM(), VMEM(), VMEM(), pl.BlockSpec(memory_space=pl.ANY)],
+            [((groups // 2, rows, width), BF16), ((rows, units), BF16)],
+            at, main, side, weights,
+            in_specs=[SMEM(), VMEM(), VMEM(), any_space],
             scratch_shapes=[pltpu.VMEM(weights.shape, BF16), pltpu.SemaphoreType.DMA((min(8, groups),))],
         )
-        part = lax.all_to_all(part, "hid", 0, 0, tiled=True)
+        give = lax.ppermute(give, "zh", [(0, 1), (1, 0)])
+        (keep,) = call(
+            keep_kernel,
+            [((groups // 2, rows, width), BF16)],
+            at, hidden, weights,
+            in_specs=[SMEM(), VMEM(), any_space],
+            scratch_shapes=[pltpu.VMEM((blocks // 2, units, depth), BF16), pltpu.SemaphoreType.DMA((blocks // 2,))],
+        )
+        part = (keep.astype(F32) + give.astype(F32)).astype(BF16)
+        part = lax.all_to_all(part, "zl", 0, 0, tiled=True)
         return (middle + jnp.sum(part.astype(F32), axis=0)).astype(BF16)
 
     return local
 
 
 def build(finer, interpret=False):
-    tile, vec = P(SEQ, "hid"), P("hid")
+    tile, vec = P(SEQ, HID), P(HID)
     return jax.shard_map(
         make(interpret),
         mesh=finer,
-        in_specs=(tile,) * 6 + (P("hid", None),) + (vec,) * 5 + (tile, tile),
+        in_specs=(tile,) * 6 + (P(HID, None),) + (vec,) * 5 + (tile, tile),
         out_specs=tile,
         check_vma=False,
     )
 
 
 def solution(mesh):
-    return build(Mesh(mesh.devices.reshape(4, 4, 2, mesh.shape["hid"]), (*SEQ, "hid")))
+    return build(Mesh(mesh.devices.reshape(4, 4, 2, mesh.shape["hid"] // 2, 2), (*SEQ, *HID)))

time: 165 us -> 156 us (0.945)
  blocking collectives: 100 us -> 78.1 us
  Pallas kernels: 13.5 us -> 17.7 us
  waiting for transfers between devices: 5.92 us -> 9.97 us
  starting transfers between devices: 24.4 us -> 27 us
  other arithmetic: 3.98 us -> 5.71 us
    all_to_all x1, blocking collectives: 57.1 us -> 35.3 us  [local(): part = lax.all_to_all(part, 'zl', 0, 0, tiled=True)]
    pallas_call x4 -> x5, Pallas kernels: 13.5 us -> 17.7 us  [call(): pl.pallas_call(kernel, out_shape=[jax.ShapeDtypeStruct(s, t) for s, t in...]
    ppermute x0 -> x1, waiting for transfers between devices: none -> 4.05 us  [local(): give = lax.ppermute(give, 'zh', [(0, 1), (1, 0)])]
    ppermute x0 -> x1, starting transfers between devices: none -> 2.78 us  [local(): give = lax.ppermute(give, 'zh', [(0, 1), (1, 0)])]
  transfers between devices with their start and end apart: 4 -> 5, of which waited for: 2 -> 3; matrix products, arithmetic and copies ran while one was open for 2% -> 2% of each run, Pallas kernels for 2% -> 5%
where the time goes in v5:
time: 156 us; the launch traced here: 154 us
  blocking collectives  78.1 us (50%)
  starting transfers between devices  27 us (17%)
  Pallas kernels  17.7 us (11%)
  between operations  13.5 us (9%)
  waiting for transfers between devices  9.97 us (6%)
  other arithmetic  5.71 us (4%)
    all_gather x1, blocking collectives, local(): main = lax.all_gather(main, HID)  39.6 us
    all_to_all x1, blocking collectives, local(): part = lax.all_to_all(part, 'zl', 0, 0, tiled=True)  35.3 us
    pallas_call x5, Pallas kernels, call(): pl.pallas_call(kernel, out_shape=[jax.ShapeDtypeStruct(s, t) for s, t in...  17.7 us
    all_to_all x1, starting transfers between devices, local(): side = lax.all_to_all(side, HID, 0, 0, tiled=True)  13.1 us
    all_to_all x1, starting transfers between devices, local(): states = lax.all_to_all(states, ('y', 'x'), 0, 0, tiled=True)  9.22 us
    ppermute x1, waiting for transfers between devices, local(): give = lax.ppermute(give, 'zh', [(0, 1), (1, 0)])  4.05 us
    ppermute x1, waiting for transfers between devices, local(): prior = lax.ppermute(row, SEQ, [(n, n + 1) for n in range(blocks - 1)])  3.31 us
    all_gather x1, blocking collectives, local(): pair = lax.all_gather(state, 'c')  3.22 us
  transfers between devices with their start and end apart: 5, of which 3 were waited for; matrix products, arithmetic and copies ran while one was open for 2% of the time, Pallas kernels for 5%

profile of v5, /device:TPU:6, one launch (start us, length us, event | category | flops | bytes accessed | tf_op | source)
XLA Modules:
  0.0 153.5 jit_solution(7091324295331346251)
XLA Ops:
  6.5 0.0 all-gather.4.cloned.1.call-start
  6.5 2.6 %shard_map.136 = (f32[128,256]{1,0:T(8,128)}, bf16[128,256]{1,0:T(8,128)(2,1)}, bf16[72,256]{1,0:T(8,128)(2,1)}, f32[8,256]{1,0:T(8,128)}) custom-call(bf16[128,256]{1,0:T(8,128)(2,1)} %r_ref.1, bf16[128,256]{1,0:T(8,128)(2,1)} %k_ref.1, bf16[128,256]{1,0:T(8,128)(2,1)} %v_ref.1, f32[128,256]{1,0:T(8,128)} %logit_ref.1, f32[4,64]{1,0:T(4,128)} %boost_ref.1, ...), custom_call_target="tpu_custom_call" | custom-call | tf_op jit(solution)/shard_map/pallas_call | solution.py:266
  9.1 3.2 %all-gather = bf16[144,256]{1,0:T(8,128)(2,1)} all-gather(bf16[72,256]{1,0:T(8,128)(2,1)} %get-tuple-element.17), channel_id=2, replica_groups=mesh['y'=4,'x'=4,'c'=2,'zl'=8,'zh'=2] {'c'}, dimensions={0}, use_global_device_ids=true | all-gather | bytes 110592 | tf_op jit(solution)/shard_map/all_gather | solution.py:291
  12.3 0.6 pad_add_fusion.at_ref
  13.0 2.0 %shard_map.137 = (bf16[16,72,256]{2,1,0:T(8,128)(2,1)}, f32[8,256]{1,0:T(8,128)}, bf16[896,128]{1,0:T(8,128)(2,1)}) custom-call(s32[2]{0:T(128)} %pad_add_fusion.at_ref, bf16[2,72,256]{2,1,0:T(8,128)(2,1)} %bitcast.14, f32[8,256]{1,0:T(8,128)} %get-tuple-element.18.row_ref, bf16[448,128]{1,0:T(8,128)(2,1)} %bitcast.16, bf16[448,128]{1,0:T(8,128)(2,1)} %bitcast.17), custom_call_target="tpu_custom_call" | custom-call | tf_op jit(solution)/shard_map/pallas_call | solution.py:266
  15.0 0.0 all-gather.4.cloned.1.call-update
  15.0 9.2 %all-to-all-start = ((bf16[16,72,256]{2,1,0:T(8,128)(2,1)}), bf16[16,72,256]{2,1,0:T(8,128)(2,1)S(1)}, u32[]{:S(2)}, u32[]{:S(2)}) async-start(bf16[16,72,256]{2,1,0:T(8,128)(2,1)} %get-tuple-element.19), calls=%async_computation | async-start | bytes 1179648 | tf_op jit(solution)/shard_map/all_to_all | solution.py:299
  24.2 2.0 %collective-permute-start = (f32[8,256]{1,0:T(8,128)}, f32[8,256]{1,0:T(8,128)S(1)}, u32[]{:S(2)}, u32[]{:S(2)}) collective-permute-start(f32[8,256]{1,0:T(8,128)} %get-tuple-element.20), channel_id=1, source_target_pairs={{0,16},{16,32},{32,48},{48,64},{64,80},{80,96},{96,112},{112,128},... | collective-permute-start | bytes 24584 | tf_op jit(solution)/shard_map/ppermute | solution.py:300
  26.2 1.3 pad_maximum_fusion.ln_ref
  27.5 1.3 pad_maximum_fusion.1.gn_ref
  28.8 3.3 %collective-permute-done.prior_ref = f32[8,256]{1,0:T(8,128)S(1)} collective-permute-done((f32[8,256]{1,0:T(8,128)}, f32[8,256]{1,0:T(8,128)S(1)}, u32[]{:S(2)}, u32[]{:S(2)}) %collective-permute-start) | collective-permute-done | bytes 8224 | tf_op jit(solution)/shard_map/ppermute | solution.py:300
  32.1 0.0 copy-start.3
  32.1 2.6 %all-to-all-done.all_ref = bf16[16,72,256]{2,1,0:T(8,128)(2,1)S(1)} async-done(((bf16[16,72,256]{2,1,0:T(8,128)(2,1)}), bf16[16,72,256]{2,1,0:T(8,128)(2,1)S(1)}, u32[]{:S(2)}, u32[]{:S(2)}) %all-to-all-start) | async-done | bytes 589856 | tf_op jit(solution)/shard_map/all_to_all | solution.py:299
  34.7 0.0 copy-done.3
  34.7 0.8 copy-done
  35.5 2.5 %shard_map.138 = (f32[128,256]{1,0:T(8,128)}, bf16[120,256]{1,0:T(8,128)(2,1)}, bf16[16,2,8,256]{3,2,1,0:T(8,128)(2,1)}) custom-call(s32[2]{0:T(128)} %pad_add_fusion.at_ref, bf16[16,72,256]{2,1,0:T(8,128)(2,1)} %copy-done, bf16[2,72,256]{2,1,0:T(8,128)(2,1)} %bitcast.15, f32[8,256]{1,0:T(8,128)} %copy-done.3, f32[128,256]{1,0:T(8,128)} %get-tuple-element.21.own_ref, ...), custom_call_target="tpu_custom_call" | custom-call | tf_op jit(solution)/shard_map/pallas_call | solution.py:266
  38.0 13.1 %all-to-all-start.1 = ((bf16[16,2,8,256]{3,2,1,0:T(8,128)(2,1)}), bf16[16,2,8,256]{3,2,1,0:T(8,128)(2,1)S(1)}, u32[]{:S(2)}, u32[]{:S(2)}) async-start(bf16[16,2,8,256]{3,2,1,0:T(8,128)(2,1)} %get-tuple-element.25), calls=%async_computation.1 | async-start | bytes 262144 | tf_op jit(solution)/shard_map/all_to_all | solution.py:308
  51.1 0.6 pad_add_fusion.1.at_ref
  51.7 39.6 %all-gather.1 = bf16[1920,256]{1,0:T(8,128)(2,1)} all-gather(bf16[120,256]{1,0:T(8,128)(2,1)} %get-tuple-element.24), channel_id=3, replica_groups=mesh['y'=4,'x'=4,'c'=2,'zl'=8,'zh'=2] {'zl','zh'}, dimensions={0}, use_global_device_ids=true | all-gather | bytes 1044480 | tf_op jit(solution)/shard_map/all_gather | solution.py:309
  91.3 0.0 all-to-all-done.1.side_ref
  91.3 0.0 all-gather.4.cloned.1.call-done.w_hbm
  91.4 0.6 copy-done.1
  92.0 6.0 %shard_map.139 = (bf16[8,128,256]{2,1,0:T(8,128)(2,1)}, bf16[128,448]{1,0:T(8,128)(2,1)}) custom-call(s32[2]{0:T(128)} %pad_add_fusion.1.at_ref, bf16[16,120,256]{2,1,0:T(8,128)(2,1)} %bitcast.13, bf16[16,2,8,256]{3,2,1,0:T(8,128)(2,1)} %copy-done.1, bf16[28672,128]{1,0:T(8,128)(2,1)} %all-gather.4.cloned.1.call-done.w_hbm), custom_call_target="tpu_custom_call" | custom-call | tf_op jit(solution)/shard_map/pallas_call | solution.py:266
  98.0 0.0 copy-start.2
  98.0 2.8 %collective-permute-start.1 = (bf16[8,128,256]{2,1,0:T(8,128)(2,1)}, bf16[8,128,256]{2,1,0:T(8,128)(2,1)S(1)}, u32[]{:S(2)}, u32[]{:S(2)}) collective-permute-start(bf16[8,128,256]{2,1,0:T(8,128)(2,1)} %get-tuple-element.28), channel_id=1, source_target_pairs={{0,1},{1,0},{2,3},{3,2},{4,5},{5,4},{6,7},{7,6},{8,9},{9,8},{10,11... | collective-permute-start | bytes 1572872 | tf_op jit(solution)/shard_map/ppermute | solution.py:320
  100.8 4.6 %shard_map.140 = bf16[8,128,256]{2,1,0:T(8,128)(2,1)} custom-call(s32[2]{0:T(128)} %pad_add_fusion.1.at_ref, bf16[128,448]{1,0:T(8,128)(2,1)} %get-tuple-element.27.hidden_ref, bf16[28672,128]{1,0:T(8,128)(2,1)} %all-gather.4.cloned.1.call-done.w_hbm), custom_call_target="tpu_custom_call" | custom-call | tf_op jit(solution)/shard_map/pallas_call | solution.py:266
  105.4 4.1 %collective-permute-done.1 = bf16[8,128,256]{2,1,0:T(8,128)(2,1)S(1)} collective-permute-done((bf16[8,128,256]{2,1,0:T(8,128)(2,1)}, bf16[8,128,256]{2,1,0:T(8,128)(2,1)S(1)}, u32[]{:S(2)}, u32[]{:S(2)}) %collective-permute-start.1) | collective-permute-done | bytes 524320 | tf_op jit(solution)/shard_map/ppermute | solution.py:320
  109.5 1.2 add_convert_fusion
  110.6 35.3 %all_to_all.15 = bf16[8,128,256]{2,1,0:T(8,128)(2,1)S(1)} all-to-all(bf16[8,128,256]{2,1,0:T(8,128)(2,1)S(1)} %add_convert_fusion), channel_id=1, replica_groups=mesh['y'=4,'x'=4,'c'=2,'zl'=8,'zh'=2] {'zl'}, dimensions={0} | all-to-all | bytes 1048576 | tf_op jit(solution)/shard_map/all_to_all | solution.py:329
  146.0 0.1 convert_reduce_fusion
  146.0 0.0 copy-done.2
  146.0 0.6 add_convert_fusion.1
  (2 shorter events, 0.0 us)
Async XLA Ops:
  6.5 84.8 %all-gather.4.cloned.1.call-start = ((), (), s32[]{:S(2)}) async-start(), calls=%async_computation.3 | async-start | bytes 7569408 | tf_op jit(solution)/shard_map/all_gather | solution.py:298
  15.0 19.7 %all-to-all-start = ((bf16[16,72,256]{2,1,0:T(8,128)(2,1)}), bf16[16,72,256]{2,1,0:T(8,128)(2,1)S(1)}, u32[]{:S(2)}, u32[]{:S(2)}) async-start(bf16[16,72,256]{2,1,0:T(8,128)(2,1)} %get-tuple-element.19), calls=%async_computation | async-start | bytes 1179648 | tf_op jit(solution)/shard_map/all_to_all | solution.py:299
  24.2 7.9 %collective-permute-start = (f32[8,256]{1,0:T(8,128)}, f32[8,256]{1,0:T(8,128)S(1)}, u32[]{:S(2)}, u32[]{:S(2)}) collective-permute-start(f32[8,256]{1,0:T(8,128)} %get-tuple-element.20), channel_id=1, source_target_pairs={{0,16},{16,32},{32,48},{48,64},{64,80},{80,96},{96,112},{112,128},... | collective-permute-start | bytes 24584 | tf_op jit(solution)/shard_map/ppermute | solution.py:300
  32.1 2.6 %copy-start.3 = (f32[8,256]{1,0:T(8,128)}, f32[8,256]{1,0:T(8,128)S(1)}, u32[]{:S(2)}) copy-start(f32[8,256]{1,0:T(8,128)S(1)} %collective-permute-done.prior_ref) | copy-start | bytes 24580
  34.7 0.8 copy-start
  38.0 53.3 %all-to-all-start.1 = ((bf16[16,2,8,256]{3,2,1,0:T(8,128)(2,1)}), bf16[16,2,8,256]{3,2,1,0:T(8,128)(2,1)S(1)}, u32[]{:S(2)}, u32[]{:S(2)}) async-start(bf16[16,2,8,256]{3,2,1,0:T(8,128)(2,1)} %get-tuple-element.25), calls=%async_computation.1 | async-start | bytes 262144 | tf_op jit(solution)/shard_map/all_to_all | solution.py:308
  91.3 0.7 copy-start.1
  98.0 48.0 %copy-start.2 = (f32[128,256]{1,0:T(8,128)S(1)}, f32[128,256]{1,0:T(8,128)}, u32[]{:S(2)}) copy-start(f32[128,256]{1,0:T(8,128)} %get-tuple-element.23) | copy-start | bytes 393220
  98.0 11.4 %collective-permute-start.1 = (bf16[8,128,256]{2,1,0:T(8,128)(2,1)}, bf16[8,128,256]{2,1,0:T(8,128)(2,1)S(1)}, u32[]{:S(2)}, u32[]{:S(2)}) collective-permute-start(bf16[8,128,256]{2,1,0:T(8,128)(2,1)} %get-tuple-element.28), channel_id=1, source_target_pairs={{0,1},{1,0},{2,3},{3,2},{4,5},{5,4},{6,7},{7,6},{8,9},{9,8},{10,11... | collective-permute-start | bytes 1572872 | tf_op jit(solution)/shard_map/ppermute | solution.py:320
Sparse Core Ops, SparseCore 0:
  15.1 69.9 all-gather.3

commit v6 on v5

--- a/solution.py
+++ b/solution.py
@@ -37,9 +37,22 @@
     return ref[rows - 16 : rows, :].astype(F32)[15:16]
 
 
+def lines(*rows):
+    width = rows[0].shape[1]
+    line = iota((8, width), 0)
+    tile = jnp.zeros((8, width), F32)
+    for n, row in enumerate(rows):
+        tile = jnp.where(line == n, row.astype(F32), tile)
+    return tile.astype(BF16)
+
+
 def wkv_kernel(
-    r_ref, k_ref, v_ref, logit_ref, boost_ref, skip_ref, gate_ref, own_ref, rec_ref, pay_ref, row_ref
+    r_ref, k_ref, v_ref, logit_ref, boost_ref, skip_ref, gate_ref, wk_ref, wv_ref,
+    own_ref, rec_ref, pay_ref, w_ref,
 ):
+    units = wk_ref.shape[0]
+    w_ref[0:units] = wk_ref[...]
+    w_ref[units:] = wv_ref[...]
     rows, width = r_ref.shape
     logw = -jnp.exp(logit_ref[...])
     lower = (iota((rows, rows), 0) >= iota((rows, rows), 1)).astype(BF16)
@@ -82,15 +95,8 @@
         own_ref[:, at] = out + jnp.where(left, sums[0], sums[1]) * v[:, at].astype(F32)
         state = dot(v[:, at], k_end[:, at], TN)
         pay_ref[0:64, at] = jnp.where(left[0:64], state[0:64], state[64:128]).astype(BF16)
-    hi, lo = hi_lo(total)
-    line = iota((8, width), 0)
-    pay_ref[64:72, :] = jnp.where(
-        line == 0, hi.astype(F32), jnp.where(line == 1, lo.astype(F32), 0.0)
-    ).astype(BF16)
-    tail = jnp.where(line == 0, last_row(own_ref), 0.0)
-    tail = jnp.where(line == 1, last_row(rec_ref), tail)
-    tail = jnp.where(line == 2, last_row(skip_ref), tail)
-    row_ref[...] = jnp.where(line == 3, last_row(gate_ref), tail)
+    last = hi_lo(last_row(own_ref))
+    pay_ref[64:72, :] = lines(*hi_lo(total), *last, last_row(rec_ref), last_row(skip_ref), last_row(gate_ref))
 
 
 def apart(state, at):
@@ -100,32 +106,25 @@
     return jnp.concatenate(both, axis=0).astype(BF16)
 
 
-def pair_kernel(at_ref, pair_ref, row_ref, wk_ref, wv_ref, out_ref, send_ref, w_ref):
-    units = wk_ref.shape[0]
-    w_ref[0:units] = wk_ref[...]
-    w_ref[units:] = wv_ref[...]
+def pair_kernel(pair_ref, out_ref):
     a, b = pair_ref[0].astype(F32), pair_ref[1].astype(F32)
     last = b[64:65] + b[65:66]
     state = (a[0:64] * jnp.exp(last) + b[0:64]).astype(BF16)
-    hi, lo = hi_lo(a[64:65] + a[65:66] + last)
-    line = iota((8, a.shape[1]), 0)
-    tail = jnp.where(line == 0, hi.astype(F32), jnp.where(line == 1, lo.astype(F32), 0.0)).astype(BF16)
+    recall = jnp.broadcast_to(b[68:69], (8, b.shape[1])).astype(BF16)
+    own = [
+        dot(recall[:, at], apart(a[0:64], at), NT)[0:1]
+        for at in (slice(128 * p, 128 * p + 128) for p in range(b.shape[1] // 128))
+    ]
+    own = b[66:67] + b[67:68] + jnp.concatenate(own, axis=1)
+    start = a[64:65] + a[65:66]
+    tail = lines(*hi_lo(start + last), *hi_lo(own), b[68:69] * jnp.exp(start), b[69:70], b[70:71])
     for n in range(out_ref.shape[0]):
         out_ref[n, 0:64] = state
         out_ref[n, 64:72] = tail
-    second = at_ref[1] > 0
-    row = row_ref[...]
-    for p in range(a.shape[1] // 128):
-        at = slice(128 * p, 128 * p + 128)
-        recall = row[1:2, at]
-        more = dot(jnp.broadcast_to(recall, (8, 128)).astype(BF16), apart(a[0:64], at), NT)
-        fade = recall * (jnp.exp(a[64:65, at] + a[65:66, at]) - 1.0)
-        more = jnp.where(line[:, at] == 0, more, jnp.where(line[:, at] == 1, fade, 0.0))
-        send_ref[:, at] = row[:, at] + jnp.where(second, more, 0.0)
 
 
 def middle_kernel(
-    at_ref, all_ref, pair_ref, prior_ref, own_ref, rec_ref, skip_ref, gate_ref, gn_ref, ln_ref,
+    chip_ref, core_ref, all_ref, pair_ref, own_ref, rec_ref, skip_ref, gate_ref, gn_ref, ln_ref,
     mid_ref, main_ref, side_ref,
 ):
     rows, width = own_ref.shape
@@ -138,7 +137,7 @@
 
         return step
 
-    chip, core = at_ref[0], at_ref[1]
+    chip, core = chip_ref[0], core_ref[0]
     split = jnp.maximum(chip + core - 1, 0)
     old = lax.fori_loop(0, split, join(all_ref), jnp.zeros((64, width), F32))
     state = lax.fori_loop(split, chip, join(all_ref), old)
@@ -159,6 +158,9 @@
         return skip + normed * (gate / (1.0 + jnp.exp(-gate)))
 
     line = iota((8, 128), 0)
+    prior = all_ref[jnp.maximum(chip - 1, 0)].astype(F32)[64:72]
+    prior = jnp.where(core > 0, pair_ref[0].astype(F32)[64:72], prior)
+    prior = [prior[2:3] + prior[3:4], prior[4:5], prior[5:6], prior[6:7]]
     for p in range(width // 128):
         at = slice(128 * p, 128 * p + 128)
         middle = finish(
@@ -166,7 +168,7 @@
         )
         mid_ref[:, at] = middle
         main_ref[:, at] = middle[0:main].astype(BF16)
-        own, recall, skip, gate = (jnp.broadcast_to(prior_ref[n : n + 1, at], (8, 128)) for n in range(4))
+        own, recall, skip, gate = (jnp.broadcast_to(row[:, at], (8, 128)) for row in prior)
         tail = jnp.where(line == 0, finish(own, recall.astype(BF16), skip, gate, old, at), 0.0)
         for n in range(3):
             hi, lo = hi_lo(ln_ref[n : n + 1, at])
@@ -178,7 +180,7 @@
             side_ref[g, 1, :, at] = tail
 
 
-def ffn_kernel(at_ref, main_ref, side_ref, w_hbm, give_ref, hidden_ref, w_ref, sems):
+def ffn_kernel(seq_ref, zh_ref, main_ref, side_ref, w_hbm, give_ref, hidden_ref, w_ref, sems):
     _, rows, width = give_ref.shape
     groups, main = main_ref.shape[0:2]
     full = groups * width
@@ -215,7 +217,7 @@
 
     mu, scale = stats(load, rows)
     pmu, pscale = stats(lambda g: side_ref[g, 1].astype(F32)[0:1], 1)
-    live = at_ref[0] > 0
+    live = seq_ref[0] > 0
     head = iota((rows, width), 0) == 0
     acc = jnp.zeros((rows, units), F32)
     for g in range(groups):
@@ -232,17 +234,17 @@
     hidden = jnp.square(jnp.maximum(acc, 0.0)).astype(BF16)
     hidden_ref[...] = hidden
     for g in range(groups // 2):
-        give_ref[g] = dot(hidden, weights(2 * g + 1 - at_ref[1], units), NN).astype(BF16)
-
-
-def keep_kernel(at_ref, hidden_ref, w_hbm, keep_ref, w_ref, sems):
+        give_ref[g] = dot(hidden, weights(2 * g + 1 - zh_ref[0], units), NN).astype(BF16)
+
+
+def keep_kernel(zh_ref, hidden_ref, w_hbm, keep_ref, w_ref, sems):
     groups, rows, width = keep_ref.shape
     units = hidden_ref.shape[1]
     depth = w_hbm.shape[1]
     each = width // depth
 
     def copy(g, b):
-        start = (((2 * g + at_ref[1]) * each + b) * 2 + 1) * units
+        start = (((2 * g + zh_ref[0]) * each + b) * 2 + 1) * units
         return pltpu.make_async_copy(
             w_hbm.at[pl.ds(pl.multiple_of(start, 64), units)], w_ref.at[g * each + b], sems.at[g * each + b]
         )
@@ -278,50 +280,49 @@
         rows, width = skip.shape
         groups = lax.axis_size(HID)
         blocks = lax.axis_size(SEQ)
-        at_seq = lax.axis_index(SEQ)
-
-        core = lax.axis_index("c")
+        at_seq = lax.axis_index(SEQ).reshape(1)
+
         chips = blocks // lax.axis_size("c")
-        at = jnp.stack([lax.axis_index(("y", "x")), core])
-        own, recall, state, row = call(
+        chip = lax.axis_index(("y", "x")).reshape(1)
+        core = lax.axis_index("c").reshape(1)
+        zh = lax.axis_index("zh").reshape(1)
+        own, recall, state, weights = call(
             wkv_kernel,
-            [((rows, width), F32), ((rows, width), BF16), ((72, width), BF16), ((8, width), F32)],
-            recept, keys, values, logit, boost, skip, gating,
-        )
+            [
+                ((rows, width), F32),
+                ((rows, width), BF16),
+                ((72, width), BF16),
+                ((2 * wk.shape[1], wk.shape[0]), BF16),
+            ],
+            recept, keys, values, logit, boost, skip, gating, wk.T, wv.T,
+        )
+        weights = lax.all_gather(weights, SEQ, tiled=True)
         pair = lax.all_gather(state, "c")
-        states, row, weights = call(
-            pair_kernel,
-            [((chips, 72, width), BF16), ((8, width), F32), ((2 * wk.shape[1], wk.shape[0]), BF16)],
-            at, pair, row, wk.T, wv.T,
-            in_specs=[SMEM()] + [VMEM()] * 4,
-        )
-        weights = lax.all_gather(weights, SEQ, tiled=True)
+        (states,) = call(pair_kernel, [((chips, 72, width), BF16)], pair)
         states = lax.all_to_all(states, ("y", "x"), 0, 0, tiled=True)
-        prior = lax.ppermute(row, SEQ, [(n, n + 1) for n in range(blocks - 1)])
         middle, main, side = call(
             middle_kernel,
             [((rows, width), F32), ((rows - 8, width), BF16), ((groups, 2, 8, width), BF16)],
-            at, states, pair, prior, own, recall, skip, gating,
+            chip, core, states, pair, own, recall, skip, gating,
             jnp.stack([gn_gain, gn_bias]), jnp.stack([ln_gain, ln_bias, blend]),
-            in_specs=[SMEM()] + [VMEM()] * 9,
+            in_specs=[SMEM(), SMEM()] + [VMEM()] * 8,
         )
         side = lax.all_to_all(side, HID, 0, 0, tiled=True)
         main = lax.all_gather(main, HID)
-        at = jnp.stack([at_seq, lax.axis_index("zh")])
         any_space = pl.BlockSpec(memory_space=pl.ANY)
         units, depth = wk.shape[1], wk.shape[0]
         give, hidden = call(
             ffn_kernel,
             [((groups // 2, rows, width), BF16), ((rows, units), BF16)],
-            at, main, side, weights,
-            in_specs=[SMEM(), VMEM(), VMEM(), any_space],
+            at_seq, zh, main, side, weights,
+            in_specs=[SMEM(), SMEM(), VMEM(), VMEM(), any_space],
             scratch_shapes=[pltpu.VMEM(weights.shape, BF16), pltpu.SemaphoreType.DMA((min(8, groups),))],
         )
         give = lax.ppermute(give, "zh", [(0, 1), (1, 0)])
         (keep,) = call(
             keep_kernel,
             [((groups // 2, rows, width), BF16)],
-            at, hidden, weights,
+            zh, hidden, weights,
             in_specs=[SMEM(), VMEM(), any_space],
             scratch_shapes=[pltpu.VMEM((blocks // 2, units, depth), BF16), pltpu.SemaphoreType.DMA((blocks // 2,))],
         )

time: 156 us -> 155 us (level)
  waiting for transfers between devices: 9.97 us -> 12 us
  starting transfers between devices: 27 us -> 25 us
    all_to_all x1, waiting for transfers between devices: 2.57 us -> 7.9 us  [local(): states = lax.all_to_all(states, ('y', 'x'), 0, 0, tiled=True)]
    ppermute x1 -> x0, waiting for transfers between devices: 3.31 us -> none  [local(): prior = lax.ppermute(row, SEQ, [(n, n + 1) for n in range(blocks - 1)])]
    ppermute x1 -> x0, starting transfers between devices: 1.96 us -> none  [local(): prior = lax.ppermute(row, SEQ, [(n, n + 1) for n in range(blocks - 1)])]
  transfers between devices with their start and end apart: 5 -> 4, of which waited for: 3 -> 2; matrix products, arithmetic and copies ran while one was open for 2% -> 2% of each run, Pallas kernels for 5% -> 6%
where the time goes in v6:
time: 155 us; the launch traced here: 153 us
  blocking collectives  78.8 us (51%)
  starting transfers between devices  25 us (16%)
  Pallas kernels  17.6 us (11%)
  between operations  13.5 us (9%)
  waiting for transfers between devices  12 us (8%)
  other arithmetic  4.44 us (3%)
    all_gather x1, blocking collectives, local(): main = lax.all_gather(main, HID)  40.2 us
    all_to_all x1, blocking collectives, local(): part = lax.all_to_all(part, 'zl', 0, 0, tiled=True)  35.3 us
    pallas_call x5, Pallas kernels, call(): pl.pallas_call(kernel, out_shape=[jax.ShapeDtypeStruct(s, t) for s, t in...  17.6 us
    all_to_all x1, starting transfers between devices, local(): side = lax.all_to_all(side, HID, 0, 0, tiled=True)  13.1 us
    all_to_all x1, starting transfers between devices, local(): states = lax.all_to_all(states, ('y', 'x'), 0, 0, tiled=True)  9.21 us
    all_to_all x1, waiting for transfers between devices, local(): states = lax.all_to_all(states, ('y', 'x'), 0, 0, tiled=True)  7.9 us
    ppermute x1, waiting for transfers between devices, local(): give = lax.ppermute(give, 'zh', [(0, 1), (1, 0)])  4.1 us
    all_gather x1, blocking collectives, local(): pair = lax.all_gather(state, 'c')  3.25 us
  transfers between devices with their start and end apart: 4, of which 2 were waited for; matrix products, arithmetic and copies ran while one was open for 2% of the time, Pallas kernels for 6%

profile of v6, /device:TPU:6, one launch (start us, length us, event | category | flops | bytes accessed | tf_op | source)
XLA Modules:
  0.0 152.8 jit_solution(5240109655889045281)
XLA Ops:
  6.5 0.0 all-gather.4.cloned.1.call-start
  6.5 2.7 %shard_map.136 = (f32[128,256]{1,0:T(8,128)}, bf16[128,256]{1,0:T(8,128)(2,1)}, bf16[72,256]{1,0:T(8,128)(2,1)}, bf16[896,128]{1,0:T(8,128)(2,1)}) custom-call(bf16[128,256]{1,0:T(8,128)(2,1)} %r_ref.1, bf16[128,256]{1,0:T(8,128)(2,1)} %k_ref.1, bf16[128,256]{1,0:T(8,128)(2,1)} %v_ref.1, f32[128,256]{1,0:T(8,128)} %logit_ref.1, f32[4,64]{1,0:T(4,128)} %boost_ref.1, ...), custom_call_target="tpu_custom_call" | custom-call | tf_op jit(solution)/shard_map/pallas_call | solution.py:268
  9.3 0.0 all-gather.4.cloned.1.call-update
  9.3 3.3 %all-gather = bf16[144,256]{1,0:T(8,128)(2,1)} all-gather(bf16[72,256]{1,0:T(8,128)(2,1)} %get-tuple-element.14), channel_id=2, replica_groups=mesh['y'=4,'x'=4,'c'=2,'zl'=8,'zh'=2] {'c'}, dimensions={0}, use_global_device_ids=true | all-gather | bytes 110592 | tf_op jit(solution)/shard_map/all_gather | solution.py:300
  12.5 1.9 %shard_map.137 = bf16[16,72,256]{2,1,0:T(8,128)(2,1)} custom-call(bf16[2,72,256]{2,1,0:T(8,128)(2,1)} %bitcast.14), custom_call_target="tpu_custom_call" | custom-call | tf_op jit(solution)/shard_map/pallas_call | solution.py:268
  14.4 9.2 %all-to-all-start = ((bf16[16,72,256]{2,1,0:T(8,128)(2,1)}), bf16[16,72,256]{2,1,0:T(8,128)(2,1)S(1)}, u32[]{:S(2)}, u32[]{:S(2)}) async-start(bf16[16,72,256]{2,1,0:T(8,128)(2,1)} %shard_map.137), calls=%async_computation | async-start | bytes 1179648 | tf_op jit(solution)/shard_map/all_to_all | solution.py:302
  23.6 1.2 pad_maximum_fusion.1.gn_ref
  24.9 1.3 pad_maximum_fusion.ln_ref
  26.2 7.9 %all-to-all-done.all_ref = bf16[16,72,256]{2,1,0:T(8,128)(2,1)S(1)} async-done(((bf16[16,72,256]{2,1,0:T(8,128)(2,1)}), bf16[16,72,256]{2,1,0:T(8,128)(2,1)S(1)}, u32[]{:S(2)}, u32[]{:S(2)}) %all-to-all-start) | async-done | bytes 589856 | tf_op jit(solution)/shard_map/all_to_all | solution.py:302
  34.1 0.0 copy-start
  34.1 0.8 copy-done
  34.9 2.4 %shard_map.138 = (f32[128,256]{1,0:T(8,128)}, bf16[120,256]{1,0:T(8,128)(2,1)}, bf16[16,2,8,256]{3,2,1,0:T(8,128)(2,1)}) custom-call(s32[1]{0:T(128)} %bitcast.chip_ref, s32[1]{0:T(128)} %bitcast.1.core_ref, bf16[16,72,256]{2,1,0:T(8,128)(2,1)} %copy-done, bf16[2,72,256]{2,1,0:T(8,128)(2,1)} %bitcast.15, f32[128,256]{1,0:T(8,128)} %get-tuple-element.15.own_ref, ...), custom_call_target="tpu_custom_call" | custom-call | tf_op jit(solution)/shard_map/pallas_call | solution.py:268
  37.3 13.1 %all-to-all-start.1 = ((bf16[16,2,8,256]{3,2,1,0:T(8,128)(2,1)}), bf16[16,2,8,256]{3,2,1,0:T(8,128)(2,1)S(1)}, u32[]{:S(2)}, u32[]{:S(2)}) async-start(bf16[16,2,8,256]{3,2,1,0:T(8,128)(2,1)} %get-tuple-element.19), calls=%async_computation.1 | async-start | bytes 262144 | tf_op jit(solution)/shard_map/all_to_all | solution.py:310
  50.4 40.2 %all-gather.1 = bf16[1920,256]{1,0:T(8,128)(2,1)} all-gather(bf16[120,256]{1,0:T(8,128)(2,1)} %get-tuple-element.18), channel_id=3, replica_groups=mesh['y'=4,'x'=4,'c'=2,'zl'=8,'zh'=2] {'zl','zh'}, dimensions={0}, use_global_device_ids=true | all-gather | bytes 1044480 | tf_op jit(solution)/shard_map/all_gather | solution.py:311
  90.7 0.0 all-to-all-done.1.side_ref
  90.7 0.0 copy-start.1
  90.7 0.0 all-gather.4.cloned.1.call-done.w_hbm
  90.7 0.6 copy-done.1
  91.3 6.0 %shard_map.139 = (bf16[8,128,256]{2,1,0:T(8,128)(2,1)}, bf16[128,448]{1,0:T(8,128)(2,1)}) custom-call(s32[1]{0:T(128)} %bitcast.11.seq_ref, s32[1]{0:T(128)} %bitcast.10.zh_ref, bf16[16,120,256]{2,1,0:T(8,128)(2,1)} %bitcast.13, bf16[16,2,8,256]{3,2,1,0:T(8,128)(2,1)} %copy-done.1, bf16[28672,128]{1,0:T(8,128)(2,1)} %all-gather.4.cloned.1.call-done.w_hbm), custom_call_target="tpu_custom_call" | custom-call | tf_op jit(solution)/shard_map/pallas_call | solution.py:268
  97.3 0.0 copy-start.2
  97.4 2.8 %collective-permute-start = (bf16[8,128,256]{2,1,0:T(8,128)(2,1)}, bf16[8,128,256]{2,1,0:T(8,128)(2,1)S(1)}, u32[]{:S(2)}, u32[]{:S(2)}) collective-permute-start(bf16[8,128,256]{2,1,0:T(8,128)(2,1)} %get-tuple-element.22), channel_id=1, source_target_pairs={{0,1},{1,0},{2,3},{3,2},{4,5},{5,4},{6,7},{7,6},{8,9},{9,8},{10,11... | collective-permute-start | bytes 1572872 | tf_op jit(solution)/shard_map/ppermute | solution.py:321
  100.1 4.6 %shard_map.140 = bf16[8,128,256]{2,1,0:T(8,128)(2,1)} custom-call(s32[1]{0:T(128)} %bitcast.10.zh_ref, bf16[128,448]{1,0:T(8,128)(2,1)} %get-tuple-element.21.hidden_ref, bf16[28672,128]{1,0:T(8,128)(2,1)} %all-gather.4.cloned.1.call-done.w_hbm), custom_call_target="tpu_custom_call" | custom-call | tf_op jit(solution)/shard_map/pallas_call | solution.py:268
  104.7 4.1 %collective-permute-done = bf16[8,128,256]{2,1,0:T(8,128)(2,1)S(1)} collective-permute-done((bf16[8,128,256]{2,1,0:T(8,128)(2,1)}, bf16[8,128,256]{2,1,0:T(8,128)(2,1)S(1)}, u32[]{:S(2)}, u32[]{:S(2)}) %collective-permute-start) | collective-permute-done | bytes 524320 | tf_op jit(solution)/shard_map/ppermute | solution.py:321
  108.8 1.2 add_convert_fusion
  109.9 35.3 %all_to_all.15 = bf16[8,128,256]{2,1,0:T(8,128)(2,1)S(1)} all-to-all(bf16[8,128,256]{2,1,0:T(8,128)(2,1)S(1)} %add_convert_fusion), channel_id=1, replica_groups=mesh['y'=4,'x'=4,'c'=2,'zl'=8,'zh'=2] {'zl'}, dimensions={0} | all-to-all | bytes 1048576 | tf_op jit(solution)/shard_map/all_to_all | solution.py:330
  145.2 0.1 convert_reduce_fusion
  145.3 0.0 copy-done.2
  145.3 0.6 add_convert_fusion.1
Async XLA Ops:
  6.5 84.1 %all-gather.4.cloned.1.call-start = ((), (), s32[]{:S(2)}) async-start(), calls=%async_computation.3 | async-start | bytes 7569408 | tf_op jit(solution)/shard_map/all_gather | solution.py:299
  14.4 19.7 %all-to-all-start = ((bf16[16,72,256]{2,1,0:T(8,128)(2,1)}), bf16[16,72,256]{2,1,0:T(8,128)(2,1)S(1)}, u32[]{:S(2)}, u32[]{:S(2)}) async-start(bf16[16,72,256]{2,1,0:T(8,128)(2,1)} %shard_map.137), calls=%async_computation | async-start | bytes 1179648 | tf_op jit(solution)/shard_map/all_to_all | solution.py:302
  34.1 0.8 copy-start
  37.3 53.3 %all-to-all-start.1 = ((bf16[16,2,8,256]{3,2,1,0:T(8,128)(2,1)}), bf16[16,2,8,256]{3,2,1,0:T(8,128)(2,1)S(1)}, u32[]{:S(2)}, u32[]{:S(2)}) async-start(bf16[16,2,8,256]{3,2,1,0:T(8,128)(2,1)} %get-tuple-element.19), calls=%async_computation.1 | async-start | bytes 262144 | tf_op jit(solution)/shard_map/all_to_all | solution.py:310
  90.7 0.7 copy-start.1
  97.3 48.0 %copy-start.2 = (f32[128,256]{1,0:T(8,128)S(1)}, f32[128,256]{1,0:T(8,128)}, u32[]{:S(2)}) copy-start(f32[128,256]{1,0:T(8,128)} %get-tuple-element.17) | copy-start | bytes 393220
  97.4 11.4 %collective-permute-start = (bf16[8,128,256]{2,1,0:T(8,128)(2,1)}, bf16[8,128,256]{2,1,0:T(8,128)(2,1)S(1)}, u32[]{:S(2)}, u32[]{:S(2)}) collective-permute-start(bf16[8,128,256]{2,1,0:T(8,128)(2,1)} %get-tuple-element.22), channel_id=1, source_target_pairs={{0,1},{1,0},{2,3},{3,2},{4,5},{5,4},{6,7},{7,6},{8,9},{9,8},{10,11... | collective-permute-start | bytes 1572872 | tf_op jit(solution)/shard_map/ppermute | solution.py:321
Sparse Core Ops, SparseCore 0:
  10.5 69.9 all-gather.3

commit v7 on v6

--- a/solution.py
+++ b/solution.py
@@ -125,10 +125,9 @@
 
 def middle_kernel(
     chip_ref, core_ref, all_ref, pair_ref, own_ref, rec_ref, skip_ref, gate_ref, gn_ref, ln_ref,
-    mid_ref, main_ref, side_ref,
+    mid_ref, send_ref,
 ):
     rows, width = own_ref.shape
-    main = main_ref.shape[0]
 
     def join(ref):
         def step(i, state):
@@ -167,22 +166,21 @@
             own_ref[:, at], rec_ref[:, at], skip_ref[:, at].astype(F32), gate_ref[:, at].astype(F32), state, at
         )
         mid_ref[:, at] = middle
-        main_ref[:, at] = middle[0:main].astype(BF16)
         own, recall, skip, gate = (jnp.broadcast_to(row[:, at], (8, 128)) for row in prior)
         tail = jnp.where(line == 0, finish(own, recall.astype(BF16), skip, gate, old, at), 0.0)
         for n in range(3):
             hi, lo = hi_lo(ln_ref[n : n + 1, at])
             tail = jnp.where(line == 2 * n + 1, hi.astype(F32), tail)
             tail = jnp.where(line == 2 * n + 2, lo.astype(F32), tail)
-        edge, tail = middle[main:].astype(BF16), tail.astype(BF16)
-        for g in range(side_ref.shape[0]):
-            side_ref[g, 0, :, at] = edge
-            side_ref[g, 1, :, at] = tail
-
-
-def ffn_kernel(seq_ref, zh_ref, main_ref, side_ref, w_hbm, give_ref, hidden_ref, w_ref, sems):
-    _, rows, width = give_ref.shape
-    groups, main = main_ref.shape[0:2]
+        middle, tail = middle.astype(BF16), tail.astype(BF16)
+        for g in range(send_ref.shape[0]):
+            send_ref[g, 0:rows, at] = middle
+            send_ref[g, rows:, at] = tail
+
+
+def ffn_kernel(seq_ref, zh_ref, even_ref, odd_ref, w_hbm, give_ref, hidden_ref, w_ref, sems):
+    half, rows, width = give_ref.shape
+    groups = 2 * half
     full = groups * width
     depth = w_hbm.shape[1]
     tall = w_hbm.shape[0] // (full // depth)
@@ -203,33 +201,34 @@
     for q in range(chunks):
         copy(q).start()
 
-    def load(g):
-        return jnp.concatenate([main_ref[g].astype(F32), side_ref[g, 0].astype(F32)], axis=0)
-
-    def stats(get, n):
+    parts = [(ref, j, 2 * j + place) for j in range(half) for ref, place in ((even_ref, zh_ref[0]), (odd_ref, 1 - zh_ref[0]))]
+
+    def stats(first_row, last_row, n):
         first, second = jnp.zeros((n, width), F32), jnp.zeros((n, width), F32)
-        for g in range(groups):
-            x = get(g)
+        for ref, j, _ in parts:
+            x = ref[j, first_row:last_row].astype(F32)[0:n]
             first, second = first + x, second + x * x
         mu = jnp.sum(first, axis=1, keepdims=True) / full
         var = jnp.sum(second, axis=1, keepdims=True) / full - mu * mu
         return mu, lax.rsqrt(var + EPS_LAYER)
 
-    mu, scale = stats(load, rows)
-    pmu, pscale = stats(lambda g: side_ref[g, 1].astype(F32)[0:1], 1)
+    mu, scale = stats(0, rows, rows)
+    pmu, pscale = stats(rows, rows + 8, 1)
     live = seq_ref[0] > 0
     head = iota((rows, width), 0) == 0
     acc = jnp.zeros((rows, units), F32)
-    for g in range(groups):
-        side = side_ref[g, 1].astype(F32)
+    waited = 0
+    for ref, j, g in parts:
+        side = ref[j, rows : rows + 8].astype(F32)
         gain, bias, blend = (side[n : n + 1] + side[n + 1 : n + 2] for n in (1, 3, 5))
-        xn = ((load(g) - mu) * scale * gain + bias).astype(BF16).astype(F32)
+        xn = ((ref[j, 0:rows].astype(F32) - mu) * scale * gain + bias).astype(BF16).astype(F32)
         pn = ((side[0:1] - pmu) * pscale * gain + bias).astype(BF16).astype(F32)
         pn = jnp.where(live, pn, 0.0)
         prev = jnp.where(head, pn, pltpu.roll(xn, 1, 0))
         xk = (xn + (prev - xn) * blend).astype(BF16)
-        if g * width % step == 0:
-            copy(g * width // step).wait()
+        while waited * step < 2 * (j + 1) * width:
+            copy(waited).wait()
+            waited += 1
         acc = acc + dot(xk, weights(g, 0), NT)
     hidden = jnp.square(jnp.maximum(acc, 0.0)).astype(BF16)
     hidden_ref[...] = hidden
@@ -300,21 +299,21 @@
         pair = lax.all_gather(state, "c")
         (states,) = call(pair_kernel, [((chips, 72, width), BF16)], pair)
         states = lax.all_to_all(states, ("y", "x"), 0, 0, tiled=True)
-        middle, main, side = call(
+        middle, send = call(
             middle_kernel,
-            [((rows, width), F32), ((rows - 8, width), BF16), ((groups, 2, 8, width), BF16)],
+            [((rows, width), F32), ((groups // 2, rows + 8, width), BF16)],
             chip, core, states, pair, own, recall, skip, gating,
             jnp.stack([gn_gain, gn_bias]), jnp.stack([ln_gain, ln_bias, blend]),
             in_specs=[SMEM(), SMEM()] + [VMEM()] * 8,
         )
-        side = lax.all_to_all(side, HID, 0, 0, tiled=True)
-        main = lax.all_gather(main, HID)
+        mine = lax.all_to_all(send, "zl", 0, 0, tiled=True)
+        other = lax.ppermute(mine, "zh", [(0, 1), (1, 0)])
         any_space = pl.BlockSpec(memory_space=pl.ANY)
         units, depth = wk.shape[1], wk.shape[0]
         give, hidden = call(
             ffn_kernel,
             [((groups // 2, rows, width), BF16), ((rows, units), BF16)],
-            at_seq, zh, main, side, weights,
+            at_seq, zh, mine, other, weights,
             in_specs=[SMEM(), SMEM(), VMEM(), VMEM(), any_space],
             scratch_shapes=[pltpu.VMEM(weights.shape, BF16), pltpu.SemaphoreType.DMA((min(8, groups),))],
         )

time: 155 us -> 165 us (1.065)
  blocking collectives: 78.8 us -> 90.1 us
  starting transfers between devices: 25 us -> 15.2 us
  waiting for transfers between devices: 12 us -> 20.2 us
    all_to_all x0 -> x1, blocking collectives: none -> 46.9 us  [local(): mine = lax.all_to_all(send, 'zl', 0, 0, tiled=True)]
    all_gather x1 -> x0, blocking collectives: 40.2 us -> none  [local(): main = lax.all_gather(main, HID)]
    all_to_all x1 -> x0, starting transfers between devices: 13.1 us -> none  [local(): side = lax.all_to_all(side, HID, 0, 0, tiled=True)]
    ppermute x0 -> x1, waiting for transfers between devices: none -> 8.83 us  [local(): other = lax.ppermute(mine, 'zh', [(0, 1), (1, 0)])]
    all_to_all x1, blocking collectives: 35.3 us -> 40 us  [local(): part = lax.all_to_all(part, 'zl', 0, 0, tiled=True)]
    ppermute x0 -> x1, starting transfers between devices: none -> 2.57 us  [local(): other = lax.ppermute(mine, 'zh', [(0, 1), (1, 0)])]
  transfers between devices with their start and end apart: 4 -> 4, of which waited for: 2 -> 3; matrix products, arithmetic and copies ran while one was open for 2% -> 2% of each run, Pallas kernels for 6% -> 6%
where the time goes in v7:
time: 165 us; the launch traced here: 163 us
  blocking collectives  90.1 us (55%)
  waiting for transfers between devices  20.2 us (12%)
  Pallas kernels  17.8 us (11%)
  starting transfers between devices  15.2 us (9%)
  between operations  13.5 us (8%)
  other arithmetic  4.46 us (3%)
  local copies, waits for them, and re-layouts  1.67 us (1%)
    all_to_all x1, blocking collectives, local(): mine = lax.all_to_all(send, 'zl', 0, 0, tiled=True)  46.9 us
    all_to_all x1, blocking collectives, local(): part = lax.all_to_all(part, 'zl', 0, 0, tiled=True)  40 us
    pallas_call x5, Pallas kernels, call(): pl.pallas_call(kernel, out_shape=[jax.ShapeDtypeStruct(s, t) for s, t in...  17.8 us
    all_to_all x1, starting transfers between devices, local(): states = lax.all_to_all(states, ('y', 'x'), 0, 0, tiled=True)  9.21 us
    ppermute x1, waiting for transfers between devices, local(): other = lax.ppermute(mine, 'zh', [(0, 1), (1, 0)])  8.83 us
    all_to_all x1, waiting for transfers between devices, local(): states = lax.all_to_all(states, ('y', 'x'), 0, 0, tiled=True)  7.88 us
    ppermute x1, waiting for transfers between devices, local(): give = lax.ppermute(give, 'zh', [(0, 1), (1, 0)])  3.46 us
    ppermute x1, starting transfers between devices, local(): give = lax.ppermute(give, 'zh', [(0, 1), (1, 0)])  3.39 us
  transfers between devices with their start and end apart: 4, of which 3 were waited for; matrix products, arithmetic and copies ran while one was open for 2% of the time, Pallas kernels for 6%

profile of v7, /device:TPU:6, one launch (start us, length us, event | category | flops | bytes accessed | tf_op | source)
XLA Modules:
  0.0 162.9 jit_solution(1084224043260146652)
XLA Ops:
  6.5 0.0 all-gather.3.cloned.1.call-start
  6.5 2.7 %shard_map.136 = (f32[128,256]{1,0:T(8,128)}, bf16[128,256]{1,0:T(8,128)(2,1)}, bf16[72,256]{1,0:T(8,128)(2,1)}, bf16[896,128]{1,0:T(8,128)(2,1)}) custom-call(bf16[128,256]{1,0:T(8,128)(2,1)} %r_ref.1, bf16[128,256]{1,0:T(8,128)(2,1)} %k_ref.1, bf16[128,256]{1,0:T(8,128)(2,1)} %v_ref.1, f32[128,256]{1,0:T(8,128)} %logit_ref.1, f32[4,64]{1,0:T(4,128)} %boost_ref.1, ...), custom_call_target="tpu_custom_call" | custom-call | tf_op jit(solution)/shard_map/pallas_call | solution.py:267
  9.3 0.0 all-gather.3.cloned.1.call-update
  9.3 3.2 %all-gather = bf16[144,256]{1,0:T(8,128)(2,1)} all-gather(bf16[72,256]{1,0:T(8,128)(2,1)} %get-tuple-element.13), channel_id=2, replica_groups=mesh['y'=4,'x'=4,'c'=2,'zl'=8,'zh'=2] {'c'}, dimensions={0}, use_global_device_ids=true | all-gather | bytes 110592 | tf_op jit(solution)/shard_map/all_gather | solution.py:299
  12.5 1.9 %shard_map.137 = bf16[16,72,256]{2,1,0:T(8,128)(2,1)} custom-call(bf16[2,72,256]{2,1,0:T(8,128)(2,1)} %bitcast.12), custom_call_target="tpu_custom_call" | custom-call | tf_op jit(solution)/shard_map/pallas_call | solution.py:267
  14.4 9.2 %all-to-all-start = ((bf16[16,72,256]{2,1,0:T(8,128)(2,1)}), bf16[16,72,256]{2,1,0:T(8,128)(2,1)S(1)}, u32[]{:S(2)}, u32[]{:S(2)}) async-start(bf16[16,72,256]{2,1,0:T(8,128)(2,1)} %shard_map.137), calls=%async_computation | async-start | bytes 1179648 | tf_op jit(solution)/shard_map/all_to_all | solution.py:301
  23.6 1.3 pad_maximum_fusion.1.gn_ref
  24.9 1.3 pad_maximum_fusion.ln_ref
  26.2 7.9 %all-to-all-done.all_ref = bf16[16,72,256]{2,1,0:T(8,128)(2,1)S(1)} async-done(((bf16[16,72,256]{2,1,0:T(8,128)(2,1)}), bf16[16,72,256]{2,1,0:T(8,128)(2,1)S(1)}, u32[]{:S(2)}, u32[]{:S(2)}) %all-to-all-start) | async-done | bytes 589856 | tf_op jit(solution)/shard_map/all_to_all | solution.py:301
  34.1 0.0 copy-start
  34.1 0.8 copy-done
  34.9 2.6 %shard_map.138 = (f32[128,256]{1,0:T(8,128)}, bf16[8,136,256]{2,1,0:T(8,128)(2,1)}) custom-call(s32[1]{0:T(128)} %bitcast.chip_ref, s32[1]{0:T(128)} %bitcast.1.core_ref, bf16[16,72,256]{2,1,0:T(8,128)(2,1)} %copy-done, bf16[2,72,256]{2,1,0:T(8,128)(2,1)} %bitcast.13, f32[128,256]{1,0:T(8,128)} %get-tuple-element.14.own_ref, ...), custom_call_target="tpu_custom_call" | custom-call | tf_op jit(solution)/shard_map/pallas_call | solution.py:267
  37.5 46.9 %all_to_all.15.even_ref = bf16[8,136,256]{2,1,0:T(8,128)(2,1)S(1)} all-to-all(bf16[8,136,256]{2,1,0:T(8,128)(2,1)} %get-tuple-element.17), channel_id=1, replica_groups=mesh['y'=4,'x'=4,'c'=2,'zl'=8,'zh'=2] {'zl'}, dimensions={0} | all-to-all | bytes 1114112 | tf_op jit(solution)/shard_map/all_to_all | solution.py:309
  84.4 0.0 copy-start.1
  84.4 2.6 %collective-permute-start = (bf16[8,136,256]{2,1,0:T(8,128)(2,1)S(1)}, bf16[8,136,256]{2,1,0:T(8,128)(2,1)S(1)}, u32[]{:S(2)}, u32[]{:S(2)}) collective-permute-start(bf16[8,136,256]{2,1,0:T(8,128)(2,1)S(1)} %all_to_all.15.even_ref), channel_id=1, source_target_pairs={{0,1},{1,0},{2,3},{3,2},{4,5},{5,4},{6,7},{7,6},{8,9},{9,8},{10,11... | collective-permute-start | bytes 1671176 | tf_op jit(solution)/shard_map/ppermute | solution.py:310
  87.0 8.8 %collective-permute-done.odd_ref = bf16[8,136,256]{2,1,0:T(8,128)(2,1)S(1)} collective-permute-done((bf16[8,136,256]{2,1,0:T(8,128)(2,1)S(1)}, bf16[8,136,256]{2,1,0:T(8,128)(2,1)S(1)}, u32[]{:S(2)}, u32[]{:S(2)}) %collective-permute-start) | collective-permute-done | bytes 557088 | tf_op jit(solution)/shard_map/ppermute | solution.py:310
  95.8 0.0 copy-start.2
  95.8 0.0 all-gather.3.cloned.1.call-done.w_hbm
  95.8 0.0 copy-done.1
  95.8 0.8 copy-done.2
  96.7 6.1 %shard_map.139 = (bf16[8,128,256]{2,1,0:T(8,128)(2,1)}, bf16[128,448]{1,0:T(8,128)(2,1)}) custom-call(s32[1]{0:T(128)} %bitcast.11.seq_ref, s32[1]{0:T(128)} %bitcast.10.zh_ref, bf16[8,136,256]{2,1,0:T(8,128)(2,1)} %copy-done.1, bf16[8,136,256]{2,1,0:T(8,128)(2,1)} %copy-done.2, bf16[28672,128]{1,0:T(8,128)(2,1)} %all-gather.3.cloned.1.call-done.w_hbm), custom_call_target="tpu_custom_call" | custom-call | tf_op jit(solution)/shard_map/pallas_call | solution.py:267
  102.7 0.0 copy-start.3
  102.7 3.4 %collective-permute-start.1 = (bf16[8,128,256]{2,1,0:T(8,128)(2,1)}, bf16[8,128,256]{2,1,0:T(8,128)(2,1)S(1)}, u32[]{:S(2)}, u32[]{:S(2)}) collective-permute-start(bf16[8,128,256]{2,1,0:T(8,128)(2,1)} %get-tuple-element.20), channel_id=1, source_target_pairs={{0,1},{1,0},{2,3},{3,2},{4,5},{5,4},{6,7},{7,6},{8,9},{9,8},{10,11... | collective-permute-start | bytes 1572872 | tf_op jit(solution)/shard_map/ppermute | solution.py:320
  106.1 4.6 %shard_map.140 = bf16[8,128,256]{2,1,0:T(8,128)(2,1)} custom-call(s32[1]{0:T(128)} %bitcast.10.zh_ref, bf16[128,448]{1,0:T(8,128)(2,1)} %get-tuple-element.19.hidden_ref, bf16[28672,128]{1,0:T(8,128)(2,1)} %all-gather.3.cloned.1.call-done.w_hbm), custom_call_target="tpu_custom_call" | custom-call | tf_op jit(solution)/shard_map/pallas_call | solution.py:267
  110.7 3.5 %collective-permute-done.1 = bf16[8,128,256]{2,1,0:T(8,128)(2,1)S(1)} collective-permute-done((bf16[8,128,256]{2,1,0:T(8,128)(2,1)}, bf16[8,128,256]{2,1,0:T(8,128)(2,1)S(1)}, u32[]{:S(2)}, u32[]{:S(2)}) %collective-permute-start.1) | collective-permute-done | bytes 524320 | tf_op jit(solution)/shard_map/ppermute | solution.py:320
  114.2 1.2 add_convert_fusion
  115.3 40.0 %all_to_all.16 = bf16[8,128,256]{2,1,0:T(8,128)(2,1)S(1)} all-to-all(bf16[8,128,256]{2,1,0:T(8,128)(2,1)S(1)} %add_convert_fusion), channel_id=1, replica_groups=mesh['y'=4,'x'=4,'c'=2,'zl'=8,'zh'=2] {'zl'}, dimensions={0} | all-to-all | bytes 1048576 | tf_op jit(solution)/shard_map/all_to_all | solution.py:329
  155.3 0.1 convert_reduce_fusion
  155.4 0.0 copy-done.3
  155.4 0.6 add_convert_fusion.1
Async XLA Ops:
  6.5 89.3 %all-gather.3.cloned.1.call-start = ((), (), s32[]{:S(2)}) async-start(), calls=%async_computation.3 | async-start | bytes 7569408 | tf_op jit(solution)/shard_map/all_gather | solution.py:298
  14.4 19.7 %all-to-all-start = ((bf16[16,72,256]{2,1,0:T(8,128)(2,1)}), bf16[16,72,256]{2,1,0:T(8,128)(2,1)S(1)}, u32[]{:S(2)}, u32[]{:S(2)}) async-start(bf16[16,72,256]{2,1,0:T(8,128)(2,1)} %shard_map.137), calls=%async_computation | async-start | bytes 1179648 | tf_op jit(solution)/shard_map/all_to_all | solution.py:301
  34.1 0.8 copy-start
  84.4 11.4 %copy-start.1 = (bf16[8,136,256]{2,1,0:T(8,128)(2,1)}, bf16[8,136,256]{2,1,0:T(8,128)(2,1)S(1)}, u32[]{:S(2)}) copy-start(bf16[8,136,256]{2,1,0:T(8,128)(2,1)S(1)} %all_to_all.15.even_ref) | copy-start | bytes 1671172
  84.4 11.4 %collective-permute-start = (bf16[8,136,256]{2,1,0:T(8,128)(2,1)S(1)}, bf16[8,136,256]{2,1,0:T(8,128)(2,1)S(1)}, u32[]{:S(2)}, u32[]{:S(2)}) collective-permute-start(bf16[8,136,256]{2,1,0:T(8,128)(2,1)S(1)} %all_to_all.15.even_ref), channel_id=1, source_target_pairs={{0,1},{1,0},{2,3},{3,2},{4,5},{5,4},{6,7},{7,6},{8,9},{9,8},{10,11... | collective-permute-start | bytes 1671176 | tf_op jit(solution)/shard_map/ppermute | solution.py:310
  95.8 0.8 copy-start.2
  102.7 52.6 %copy-start.3 = (f32[128,256]{1,0:T(8,128)S(1)}, f32[128,256]{1,0:T(8,128)}, u32[]{:S(2)}) copy-start(f32[128,256]{1,0:T(8,128)} %get-tuple-element.16) | copy-start | bytes 393220
  102.7 11.4 %collective-permute-start.1 = (bf16[8,128,256]{2,1,0:T(8,128)(2,1)}, bf16[8,128,256]{2,1,0:T(8,128)(2,1)S(1)}, u32[]{:S(2)}, u32[]{:S(2)}) collective-permute-start(bf16[8,128,256]{2,1,0:T(8,128)(2,1)} %get-tuple-element.20), channel_id=1, source_target_pairs={{0,1},{1,0},{2,3},{3,2},{4,5},{5,4},{6,7},{7,6},{8,9},{9,8},{10,11... | collective-permute-start | bytes 1572872 | tf_op jit(solution)/shard_map/ppermute | solution.py:320
Sparse Core Ops, SparseCore 0:
  10.5 69.9 all-gather.2

commit v8 on v6

--- a/solution.py
+++ b/solution.py
@@ -263,11 +263,15 @@
 SMEM = functools.partial(pl.BlockSpec, memory_space=pltpu.SMEM)
 
 
+def near(x):
+    return pltpu.with_memory_space_constraint(x, pltpu.VMEM)
+
+
 def make(interpret):
     def call(kernel, outs, *args, in_specs=None, **more):
         return pl.pallas_call(
             kernel,
-            out_shape=[jax.ShapeDtypeStruct(s, t) for s, t in outs],
+            out_shape=[pltpu.HBM(s, t) if len(s) == 2 and s[0] > 512 else pltpu.VMEM(s, t) for s, t in outs],
             in_specs=in_specs or [VMEM() for _ in args],
             out_specs=[VMEM() for _ in outs],
             interpret=interpret,
@@ -298,12 +302,12 @@
         )
         weights = lax.all_gather(weights, SEQ, tiled=True)
         pair = lax.all_gather(state, "c")
-        (states,) = call(pair_kernel, [((chips, 72, width), BF16)], pair)
+        (states,) = call(pair_kernel, [((chips, 72, width), BF16)], near(pair))
         states = lax.all_to_all(states, ("y", "x"), 0, 0, tiled=True)
         middle, main, side = call(
             middle_kernel,
             [((rows, width), F32), ((rows - 8, width), BF16), ((groups, 2, 8, width), BF16)],
-            chip, core, states, pair, own, recall, skip, gating,
+            chip, core, near(states), near(pair), near(own), near(recall), skip, gating,
             jnp.stack([gn_gain, gn_bias]), jnp.stack([ln_gain, ln_bias, blend]),
             in_specs=[SMEM(), SMEM()] + [VMEM()] * 8,
         )
@@ -314,7 +318,7 @@
         give, hidden = call(
             ffn_kernel,
             [((groups // 2, rows, width), BF16), ((rows, units), BF16)],
-            at_seq, zh, main, side, weights,
+            at_seq, zh, main, near(side), weights,
             in_specs=[SMEM(), SMEM(), VMEM(), VMEM(), any_space],
             scratch_shapes=[pltpu.VMEM(weights.shape, BF16), pltpu.SemaphoreType.DMA((min(8, groups),))],
         )
@@ -322,7 +326,7 @@
         (keep,) = call(
             keep_kernel,
             [((groups // 2, rows, width), BF16)],
-            zh, hidden, weights,
+            zh, near(hidden), weights,
             in_specs=[SMEM(), VMEM(), any_space],
             scratch_shapes=[pltpu.VMEM((blocks // 2, units, depth), BF16), pltpu.SemaphoreType.DMA((blocks // 2,))],
         )

time: 155 us -> 150 us (0.968)
  the two profiles are of different devices: /device:TPU:6 before, /device:TPU:38 now
where the time goes in v8:
time: 150 us; the launch traced here: 149 us
  blocking collectives  79.5 us (53%)
  starting transfers between devices  26.5 us (18%)
  Pallas kernels  13.7 us (9%)
  between operations  13.4 us (9%)
  waiting for transfers between devices  12.5 us (8%)
  other arithmetic  3.46 us (2%)
    all_to_all x1, blocking collectives, local(): part = lax.all_to_all(part, 'zl', 0, 0, tiled=True)  40.1 us
    all_gather x1, blocking collectives, local(): main = lax.all_gather(main, HID)  37.6 us
    all_to_all x1, starting transfers between devices, local(): side = lax.all_to_all(side, HID, 0, 0, tiled=True)  15.2 us
    pallas_call x5, Pallas kernels, call(): pl.pallas_call(kernel, out_shape=[pltpu.HBM(s, t) if len(s) == 2 and s[0]...  13.7 us
    all_to_all x1, starting transfers between devices, local(): states = lax.all_to_all(states, ('y', 'x'), 0, 0, tiled=True)  7.42 us
    all_to_all x1, waiting for transfers between devices, local(): states = lax.all_to_all(states, ('y', 'x'), 0, 0, tiled=True)  7.34 us
    ppermute x1, waiting for transfers between devices, local(): give = lax.ppermute(give, 'zh', [(0, 1), (1, 0)])  5.17 us
    ppermute x1, starting transfers between devices, local(): give = lax.ppermute(give, 'zh', [(0, 1), (1, 0)])  3.82 us
  transfers between devices with their start and end apart: 4, of which 2 were waited for; matrix products, arithmetic and copies ran while one was open for 2% of the time, Pallas kernels for 4%

profile of v8, /device:TPU:38, one launch (start us, length us, event | category | flops | bytes accessed | tf_op | source)
XLA Modules:
  0.0 149.1 jit_solution(11378375271849791436)
XLA Ops:
  6.5 0.0 all-gather.4.cloned.1.call-start
  6.5 2.7 %shard_map.136 = (f32[128,256]{1,0:T(8,128)S(1)}, bf16[128,256]{1,0:T(8,128)(2,1)S(1)}, bf16[72,256]{1,0:T(8,128)(2,1)S(1)}, bf16[896,128]{1,0:T(8,128)(2,1)}) custom-call(bf16[128,256]{1,0:T(8,128)(2,1)} %r_ref.1, bf16[128,256]{1,0:T(8,128)(2,1)} %k_ref.1, bf16[128,256]{1,0:T(8,128)(2,1)} %v_ref.1, f32[128,256]{1,0:T(8,128)} %logit_ref.1, ...), custom_call_target="tpu_custom_call" | custom-call | tf_op jit(solution)/shard_map/pallas_call | solution.py:272
  9.2 0.0 all-gather.4.cloned.1.call-update
  9.2 1.9 %all-gather = bf16[144,256]{1,0:T(8,128)(2,1)S(1)} all-gather(bf16[72,256]{1,0:T(8,128)(2,1)S(1)} %get-tuple-element.14), channel_id=2, replica_groups=mesh['y'=4,'x'=4,'c'=2,'zl'=8,'zh'=2] {'c'}, dimensions={0}, use_global_device_ids=true | all-gather | bytes 110592 | tf_op jit(solution)/shard_map/all_gather | solution.py:304
  11.1 1.0 shard_map.137
  12.1 7.4 %all-to-all-start = ((bf16[16,72,256]{2,1,0:T(8,128)(2,1)}), bf16[16,72,256]{2,1,0:T(8,128)(2,1)S(1)}, u32[]{:S(2)}, u32[]{:S(2)}) async-start(bf16[16,72,256]{2,1,0:T(8,128)(2,1)} %shard_map.137), calls=%async_computation | async-start | bytes 1179648 | tf_op jit(solution)/shard_map/all_to_all | solution.py:306
  19.5 1.3 pad_maximum_fusion.1.gn_ref
  20.8 1.3 pad_maximum_fusion.ln_ref
  22.1 7.3 %all-to-all-done.all_ref = bf16[16,72,256]{2,1,0:T(8,128)(2,1)S(1)} async-done(((bf16[16,72,256]{2,1,0:T(8,128)(2,1)}), bf16[16,72,256]{2,1,0:T(8,128)(2,1)S(1)}, u32[]{:S(2)}, u32[]{:S(2)}) %all-to-all-start) | async-done | bytes 589856 | tf_op jit(solution)/shard_map/all_to_all | solution.py:306
  29.4 2.0 %shard_map.138 = (f32[128,256]{1,0:T(8,128)S(1)}, bf16[120,256]{1,0:T(8,128)(2,1)S(1)}, bf16[16,2,8,256]{3,2,1,0:T(8,128)(2,1)}) custom-call(s32[1]{0:T(128)} %bitcast.chip_ref, s32[1]{0:T(128)} %bitcast.1.core_ref, bf16[16,72,256]{2,1,0:T(8,128)(2,1)S(1)} %all-to-all-done.all_ref, bf16[2,72,256]{2,1,0:T(8,128)(2,1)S(1)} %bitcast.14, ...), custom_call_target="tpu_custom_call" | custom-call | tf_op jit(solution)/shard_map/pallas_call | solution.py:272
  31.4 15.2 %all-to-all-start.1 = ((bf16[16,2,8,256]{3,2,1,0:T(8,128)(2,1)}), bf16[16,2,8,256]{3,2,1,0:T(8,128)(2,1)S(1)}, u32[]{:S(2)}, u32[]{:S(2)}) async-start(bf16[16,2,8,256]{3,2,1,0:T(8,128)(2,1)} %get-tuple-element.19), calls=%async_computation.1 | async-start | bytes 262144 | tf_op jit(solution)/shard_map/all_to_all | solution.py:314
  46.7 37.6 %all-gather.1 = bf16[1920,256]{1,0:T(8,128)(2,1)} all-gather(bf16[120,256]{1,0:T(8,128)(2,1)S(1)} %get-tuple-element.18), channel_id=3, replica_groups=mesh['y'=4,'x'=4,'c'=2,'zl'=8,'zh'=2] {'zl','zh'}, dimensions={0}, use_global_device_ids=true | all-gather | bytes 1044480 | tf_op jit(solution)/shard_map/all_gather | solution.py:315
  84.2 0.0 all-to-all-done.1.side_ref
  84.2 0.0 all-gather.4.cloned.1.call-done.w_hbm
  84.2 5.2 %shard_map.139 = (bf16[8,128,256]{2,1,0:T(8,128)(2,1)S(1)}, bf16[128,448]{1,0:T(8,128)(2,1)S(1)}) custom-call(s32[1]{0:T(128)} %bitcast.11.seq_ref, s32[1]{0:T(128)} %bitcast.10.zh_ref, bf16[16,120,256]{2,1,0:T(8,128)(2,1)} %bitcast.15, bf16[16,2,8,256]{3,2,1,0:T(8,128)(2,1)S(1)} %all-to-all-done.1.side_ref, ...), custom_call_target="tpu_custom_call" | custom-call | tf_op jit(solution)/shard_map/pallas_call | solution.py:272
  89.4 3.8 %collective-permute-start = (bf16[8,128,256]{2,1,0:T(8,128)(2,1)S(1)}, bf16[8,128,256]{2,1,0:T(8,128)(2,1)S(1)}, u32[]{:S(2)}, u32[]{:S(2)}) collective-permute-start(bf16[8,128,256]{2,1,0:T(8,128)(2,1)S(1)} %get-tuple-element.22), channel_id=1, source_target_pairs={{0,1},{1,0},{2,3},{3,2},{4,5},{5,4},{6,7},{7,6},{8,9},{9,8},{10,11... | collective-permute-start | bytes 1572872 | tf_op jit(solution)/shard_map/ppermute | solution.py:325
  93.3 2.9 %shard_map.140 = bf16[8,128,256]{2,1,0:T(8,128)(2,1)S(1)} custom-call(s32[1]{0:T(128)} %bitcast.10.zh_ref, bf16[128,448]{1,0:T(8,128)(2,1)S(1)} %get-tuple-element.21.hidden_ref, bf16[28672,128]{1,0:T(8,128)(2,1)} %all-gather.4.cloned.1.call-done.w_hbm), custom_call_target="tpu_custom_call" | custom-call | tf_op jit(solution)/shard_map/pallas_call | solution.py:272
  96.1 5.2 %collective-permute-done = bf16[8,128,256]{2,1,0:T(8,128)(2,1)S(1)} collective-permute-done((bf16[8,128,256]{2,1,0:T(8,128)(2,1)S(1)}, bf16[8,128,256]{2,1,0:T(8,128)(2,1)S(1)}, u32[]{:S(2)}, u32[]{:S(2)}) %collective-permute-start) | collective-permute-done | bytes 524320 | tf_op jit(solution)/shard_map/ppermute | solution.py:325
  101.3 0.1 add_convert_fusion
  101.5 40.1 %all_to_all.15 = bf16[8,128,256]{2,1,0:T(8,128)(2,1)S(1)} all-to-all(bf16[8,128,256]{2,1,0:T(8,128)(2,1)S(1)} %add_convert_fusion), channel_id=1, replica_groups=mesh['y'=4,'x'=4,'c'=2,'zl'=8,'zh'=2] {'zl'}, dimensions={0} | all-to-all | bytes 1048576 | tf_op jit(solution)/shard_map/all_to_all | solution.py:334
  141.6 0.1 convert_reduce_fusion
  141.6 0.6 add_convert_fusion.1
Async XLA Ops:
  6.5 77.7 %all-gather.4.cloned.1.call-start = ((), (), s32[]{:S(2)}) async-start(), calls=%async_computation.3 | async-start | bytes 7569408 | tf_op jit(solution)/shard_map/all_gather | solution.py:303
  12.1 17.4 %all-to-all-start = ((bf16[16,72,256]{2,1,0:T(8,128)(2,1)}), bf16[16,72,256]{2,1,0:T(8,128)(2,1)S(1)}, u32[]{:S(2)}, u32[]{:S(2)}) async-start(bf16[16,72,256]{2,1,0:T(8,128)(2,1)} %shard_map.137), calls=%async_computation | async-start | bytes 1179648 | tf_op jit(solution)/shard_map/all_to_all | solution.py:306
  31.4 52.8 %all-to-all-start.1 = ((bf16[16,2,8,256]{3,2,1,0:T(8,128)(2,1)}), bf16[16,2,8,256]{3,2,1,0:T(8,128)(2,1)S(1)}, u32[]{:S(2)}, u32[]{:S(2)}) async-start(bf16[16,2,8,256]{3,2,1,0:T(8,128)(2,1)} %get-tuple-element.19), calls=%async_computation.1 | async-start | bytes 262144 | tf_op jit(solution)/shard_map/all_to_all | solution.py:314
  89.4 11.9 %collective-permute-start = (bf16[8,128,256]{2,1,0:T(8,128)(2,1)S(1)}, bf16[8,128,256]{2,1,0:T(8,128)(2,1)S(1)}, u32[]{:S(2)}, u32[]{:S(2)}) collective-permute-start(bf16[8,128,256]{2,1,0:T(8,128)(2,1)S(1)} %get-tuple-element.22), channel_id=1, source_target_pairs={{0,1},{1,0},{2,3},{3,2},{4,5},{5,4},{6,7},{7,6},{8,9},{9,8},{10,11... | collective-permute-start | bytes 1572872 | tf_op jit(solution)/shard_map/ppermute | solution.py:325
Sparse Core Ops, SparseCore 0:
  10.5 69.6 all-gather.3

commit v9 on v8

--- a/solution.py
+++ b/solution.py
@@ -47,12 +47,8 @@
 
 
 def wkv_kernel(
-    r_ref, k_ref, v_ref, logit_ref, boost_ref, skip_ref, gate_ref, wk_ref, wv_ref,
-    own_ref, rec_ref, pay_ref, w_ref,
+    r_ref, k_ref, v_ref, logit_ref, boost_ref, skip_ref, gate_ref, own_ref, rec_ref, pay_ref
 ):
-    units = wk_ref.shape[0]
-    w_ref[0:units] = wk_ref[...]
-    w_ref[units:] = wv_ref[...]
     rows, width = r_ref.shape
     logw = -jnp.exp(logit_ref[...])
     lower = (iota((rows, rows), 0) >= iota((rows, rows), 1)).astype(BF16)
@@ -106,6 +102,12 @@
     return jnp.concatenate(both, axis=0).astype(BF16)
 
 
+def pack_kernel(wk_ref, wv_ref, w_ref):
+    units = wk_ref.shape[0]
+    w_ref[0:units] = wk_ref[...]
+    w_ref[units:] = wv_ref[...]
+
+
 def pair_kernel(pair_ref, out_ref):
     a, b = pair_ref[0].astype(F32), pair_ref[1].astype(F32)
     last = b[64:65] + b[65:66]
@@ -290,15 +292,11 @@
         chip = lax.axis_index(("y", "x")).reshape(1)
         core = lax.axis_index("c").reshape(1)
         zh = lax.axis_index("zh").reshape(1)
-        own, recall, state, weights = call(
+        (weights,) = call(pack_kernel, [((2 * wk.shape[1], wk.shape[0]), BF16)], wk.T, wv.T)
+        own, recall, state = call(
             wkv_kernel,
-            [
-                ((rows, width), F32),
-                ((rows, width), BF16),
-                ((72, width), BF16),
-                ((2 * wk.shape[1], wk.shape[0]), BF16),
-            ],
-            recept, keys, values, logit, boost, skip, gating, wk.T, wv.T,
+            [((rows, width), F32), ((rows, width), BF16), ((72, width), BF16)],
+            recept, keys, values, logit, boost, skip, gating,
         )
         weights = lax.all_gather(weights, SEQ, tiled=True)
         pair = lax.all_gather(state, "c")
@@ -318,7 +316,7 @@
         give, hidden = call(
             ffn_kernel,
             [((groups // 2, rows, width), BF16), ((rows, units), BF16)],
-            at_seq, zh, main, near(side), weights,
+            at_seq, zh, near(main), near(side), weights,
             in_specs=[SMEM(), SMEM(), VMEM(), VMEM(), any_space],
             scratch_shapes=[pltpu.VMEM(weights.shape, BF16), pltpu.SemaphoreType.DMA((min(8, groups),))],
         )

time: 150 us -> 150 us (level)
    all_gather x1, blocking collectives: 37.6 us -> 35.5 us  [local(): main = lax.all_gather(main, HID)]
    all_to_all x1, blocking collectives: 40.1 us -> 41.6 us  [local(): part = lax.all_to_all(part, 'zl', 0, 0, tiled=True)]
    pallas_call x5 -> x6, Pallas kernels: 13.7 us -> 13.4 us  [call(): pl.pallas_call(kernel, out_shape=[pltpu.HBM(s, t) if len(s) == 2 and s[0]...]
  transfers between devices with their start and end apart: 4 -> 4, of which waited for: 2 -> 2; matrix products, arithmetic and copies ran while one was open for 2% -> 2% of each run, Pallas kernels for 4% -> 5%
where the time goes in v9:
time: 150 us; the launch traced here: 149 us
  blocking collectives  79 us (53%)
  starting transfers between devices  26.4 us (18%)
  waiting for transfers between devices  13.7 us (9%)
  Pallas kernels  13.4 us (9%)
  between operations  13.4 us (9%)
  other arithmetic  3.41 us (2%)
    all_to_all x1, blocking collectives, local(): part = lax.all_to_all(part, 'zl', 0, 0, tiled=True)  41.6 us
    all_gather x1, blocking collectives, local(): main = lax.all_gather(main, HID)  35.5 us
    all_to_all x1, starting transfers between devices, local(): side = lax.all_to_all(side, HID, 0, 0, tiled=True)  15.2 us
    pallas_call x6, Pallas kernels, call(): pl.pallas_call(kernel, out_shape=[pltpu.HBM(s, t) if len(s) == 2 and s[0]...  13.4 us
    all_to_all x1, starting transfers between devices, local(): states = lax.all_to_all(states, ('y', 'x'), 0, 0, tiled=True)  7.42 us
    all_to_all x1, waiting for transfers between devices, local(): states = lax.all_to_all(states, ('y', 'x'), 0, 0, tiled=True)  7.38 us
    ppermute x1, waiting for transfers between devices, local(): give = lax.ppermute(give, 'zh', [(0, 1), (1, 0)])  6.28 us
    ppermute x1, starting transfers between devices, local(): give = lax.ppermute(give, 'zh', [(0, 1), (1, 0)])  3.81 us
  transfers between devices with their start and end apart: 4, of which 2 were waited for; matrix products, arithmetic and copies ran while one was open for 2% of the time, Pallas kernels for 5%

profile of v9, /device:TPU:38, one launch (start us, length us, event | category | flops | bytes accessed | tf_op | source)
XLA Modules:
  0.0 149.4 jit_solution(10142800908215534899)
XLA Ops:
  6.5 0.0 all-gather.4.cloned.1.call-start
  6.5 1.7 %shard_map.139 = bf16[896,128]{1,0:T(8,128)(2,1)} custom-call(bf16[448,128]{1,0:T(8,128)(2,1)} %bitcast.16, bf16[448,128]{1,0:T(8,128)(2,1)} %bitcast.17), custom_call_target="tpu_custom_call" | custom-call | tf_op jit(solution)/shard_map/pallas_call | solution.py:274
  8.2 0.0 all-gather.4.cloned.1.call-update
  8.2 1.9 %shard_map.136 = (f32[128,256]{1,0:T(8,128)S(1)}, bf16[128,256]{1,0:T(8,128)(2,1)S(1)}, bf16[72,256]{1,0:T(8,128)(2,1)S(1)}) custom-call(bf16[128,256]{1,0:T(8,128)(2,1)} %r_ref.1, bf16[128,256]{1,0:T(8,128)(2,1)} %k_ref.1, bf16[128,256]{1,0:T(8,128)(2,1)} %v_ref.1, f32[128,256]{1,0:T(8,128)} %logit_ref.1, f32[4,64]{1,0:T(4,128)} %boost_ref.1, ...), custom_call_target="tpu_custom_call" | custom-call | tf_op jit(solution)/shard_map/pallas_call | solution.py:274
  10.2 1.9 %all-gather = bf16[144,256]{1,0:T(8,128)(2,1)S(1)} all-gather(bf16[72,256]{1,0:T(8,128)(2,1)S(1)} %get-tuple-element.13), channel_id=2, replica_groups=mesh['y'=4,'x'=4,'c'=2,'zl'=8,'zh'=2] {'c'}, dimensions={0}, use_global_device_ids=true | all-gather | bytes 110592 | tf_op jit(solution)/shard_map/all_gather | solution.py:302
  12.0 1.0 shard_map.137
  13.0 7.4 %all-to-all-start = ((bf16[16,72,256]{2,1,0:T(8,128)(2,1)}), bf16[16,72,256]{2,1,0:T(8,128)(2,1)S(1)}, u32[]{:S(2)}, u32[]{:S(2)}) async-start(bf16[16,72,256]{2,1,0:T(8,128)(2,1)} %shard_map.137), calls=%async_computation | async-start | bytes 1179648 | tf_op jit(solution)/shard_map/all_to_all | solution.py:304
  20.4 1.2 pad_maximum_fusion.1.gn_ref
  21.7 1.3 pad_maximum_fusion.ln_ref
  23.0 7.4 %all-to-all-done.all_ref = bf16[16,72,256]{2,1,0:T(8,128)(2,1)S(1)} async-done(((bf16[16,72,256]{2,1,0:T(8,128)(2,1)}), bf16[16,72,256]{2,1,0:T(8,128)(2,1)S(1)}, u32[]{:S(2)}, u32[]{:S(2)}) %all-to-all-start) | async-done | bytes 589856 | tf_op jit(solution)/shard_map/all_to_all | solution.py:304
  30.4 2.0 %shard_map.138 = (f32[128,256]{1,0:T(8,128)S(1)}, bf16[120,256]{1,0:T(8,128)(2,1)S(1)}, bf16[16,2,8,256]{3,2,1,0:T(8,128)(2,1)}) custom-call(s32[1]{0:T(128)} %bitcast.chip_ref, s32[1]{0:T(128)} %bitcast.1.core_ref, bf16[16,72,256]{2,1,0:T(8,128)(2,1)S(1)} %all-to-all-done.all_ref, bf16[2,72,256]{2,1,0:T(8,128)(2,1)S(1)} %bitcast.15, ...), custom_call_target="tpu_custom_call" | custom-call | tf_op jit(solution)/shard_map/pallas_call | solution.py:274
  32.4 15.2 %all-to-all-start.1 = ((bf16[16,2,8,256]{3,2,1,0:T(8,128)(2,1)}), bf16[16,2,8,256]{3,2,1,0:T(8,128)(2,1)S(1)}, u32[]{:S(2)}, u32[]{:S(2)}) async-start(bf16[16,2,8,256]{3,2,1,0:T(8,128)(2,1)} %get-tuple-element.18), calls=%async_computation.1 | async-start | bytes 262144 | tf_op jit(solution)/shard_map/all_to_all | solution.py:312
  47.6 35.5 %all-gather.1 = bf16[1920,256]{1,0:T(8,128)(2,1)S(1)} all-gather(bf16[120,256]{1,0:T(8,128)(2,1)S(1)} %get-tuple-element.17), channel_id=3, replica_groups=mesh['y'=4,'x'=4,'c'=2,'zl'=8,'zh'=2] {'zl','zh'}, dimensions={0}, use_global_device_ids=true | all-gather | bytes 1044480 | tf_op jit(solution)/shard_map/all_gather | solution.py:313
  83.1 0.0 all-to-all-done.1.side_ref
  83.1 0.0 all-gather.4.cloned.1.call-done.w_hbm
  83.1 4.0 %shard_map.140 = (bf16[8,128,256]{2,1,0:T(8,128)(2,1)S(1)}, bf16[128,448]{1,0:T(8,128)(2,1)S(1)}) custom-call(s32[1]{0:T(128)} %bitcast.9.seq_ref, s32[1]{0:T(128)} %bitcast.8.zh_ref, bf16[16,120,256]{2,1,0:T(8,128)(2,1)S(1)} %bitcast.13, bf16[16,2,8,256]{3,2,1,0:T(8,128)(2,1)S(1)} %all-to-all-done.1.side_ref, ...), custom_call_target="tpu_custom_call" | custom-call | tf_op jit(solution)/shard_map/pallas_call | solution.py:274
  87.1 3.8 %collective-permute-start = (bf16[8,128,256]{2,1,0:T(8,128)(2,1)S(1)}, bf16[8,128,256]{2,1,0:T(8,128)(2,1)S(1)}, u32[]{:S(2)}, u32[]{:S(2)}) collective-permute-start(bf16[8,128,256]{2,1,0:T(8,128)(2,1)S(1)} %get-tuple-element.20), channel_id=1, source_target_pairs={{0,1},{1,0},{2,3},{3,2},{4,5},{5,4},{6,7},{7,6},{8,9},{9,8},{10,11... | collective-permute-start | bytes 1572872 | tf_op jit(solution)/shard_map/ppermute | solution.py:323
  90.9 2.9 %shard_map.141 = bf16[8,128,256]{2,1,0:T(8,128)(2,1)S(1)} custom-call(s32[1]{0:T(128)} %bitcast.8.zh_ref, bf16[128,448]{1,0:T(8,128)(2,1)S(1)} %get-tuple-element.19.hidden_ref, bf16[28672,128]{1,0:T(8,128)(2,1)} %all-gather.4.cloned.1.call-done.w_hbm), custom_call_target="tpu_custom_call" | custom-call | tf_op jit(solution)/shard_map/pallas_call | solution.py:274
  93.8 6.3 %collective-permute-done = bf16[8,128,256]{2,1,0:T(8,128)(2,1)S(1)} collective-permute-done((bf16[8,128,256]{2,1,0:T(8,128)(2,1)S(1)}, bf16[8,128,256]{2,1,0:T(8,128)(2,1)S(1)}, u32[]{:S(2)}, u32[]{:S(2)}) %collective-permute-start) | collective-permute-done | bytes 524320 | tf_op jit(solution)/shard_map/ppermute | solution.py:323
  100.1 0.1 add_convert_fusion
  100.2 41.6 %all_to_all.15 = bf16[8,128,256]{2,1,0:T(8,128)(2,1)S(1)} all-to-all(bf16[8,128,256]{2,1,0:T(8,128)(2,1)S(1)} %add_convert_fusion), channel_id=1, replica_groups=mesh['y'=4,'x'=4,'c'=2,'zl'=8,'zh'=2] {'zl'}, dimensions={0} | all-to-all | bytes 1048576 | tf_op jit(solution)/shard_map/all_to_all | solution.py:332
  141.8 0.1 convert_reduce_fusion
  141.9 0.6 add_convert_fusion.1
Async XLA Ops:
  6.5 76.6 %all-gather.4.cloned.1.call-start = ((), (), s32[]{:S(2)}) async-start(), calls=%async_computation.3 | async-start | bytes 7569408 | tf_op jit(solution)/shard_map/all_gather | solution.py:301
  13.0 17.4 %all-to-all-start = ((bf16[16,72,256]{2,1,0:T(8,128)(2,1)}), bf16[16,72,256]{2,1,0:T(8,128)(2,1)S(1)}, u32[]{:S(2)}, u32[]{:S(2)}) async-start(bf16[16,72,256]{2,1,0:T(8,128)(2,1)} %shard_map.137), calls=%async_computation | async-start | bytes 1179648 | tf_op jit(solution)/shard_map/all_to_all | solution.py:304
  32.4 50.7 %all-to-all-start.1 = ((bf16[16,2,8,256]{3,2,1,0:T(8,128)(2,1)}), bf16[16,2,8,256]{3,2,1,0:T(8,128)(2,1)S(1)}, u32[]{:S(2)}, u32[]{:S(2)}) async-start(bf16[16,2,8,256]{3,2,1,0:T(8,128)(2,1)} %get-tuple-element.18), calls=%async_computation.1 | async-start | bytes 262144 | tf_op jit(solution)/shard_map/all_to_all | solution.py:312
  87.1 13.0 %collective-permute-start = (bf16[8,128,256]{2,1,0:T(8,128)(2,1)S(1)}, bf16[8,128,256]{2,1,0:T(8,128)(2,1)S(1)}, u32[]{:S(2)}, u32[]{:S(2)}) collective-permute-start(bf16[8,128,256]{2,1,0:T(8,128)(2,1)S(1)} %get-tuple-element.20), channel_id=1, source_target_pairs={{0,1},{1,0},{2,3},{3,2},{4,5},{5,4},{6,7},{7,6},{8,9},{9,8},{10,11... | collective-permute-start | bytes 1572872 | tf_op jit(solution)/shard_map/ppermute | solution.py:323
Sparse Core Ops, SparseCore 0:
  10.5 69.6 all-gather.3
